TPU v7x, 32 devices: a whole 2x2x4 slice. The times are simulated.
32 devices in a mesh: gx: 8 (over y, x, core), gy: 4 (over z).
Axes of the slice: x: 2, y: 2, z: 4, core: 2. Of those that a mesh axis runs over, the one named last changes fastest.
Arguments:
- eastward: float32 [64, 512, 128], P('gx', 'gy'), may hold values from -6 to 6
- northward: float32 [64, 512, 128], P('gx', 'gy'), may hold values from -6 to 6
- vertical: float32 [64, 512, 128], P('gx', 'gy'), may hold values from -6 to 6
- pressure: float32 [64, 512, 128], P('gx', 'gy'), may hold values from -6 to 6
- theta: float32 [64, 512, 128], P('gx', 'gy'), may hold values from -6 to 6
- humidity: float32 [64, 512, 128], P('gx', 'gy'), may hold values from 0.95 to 1.07
- sound_speed: float32 [128], replicated, may hold values from 0.25 to 1
- radius_sq: float32 [64, 8, 64, 512], P(None, None, 'gx', 'gy'), may hold values from 0.25 to 4
- multiplicity: bfloat16 [64, 8, 64, 512], P(None, None, 'gx', 'gy'), may hold values from 0.5 to 2
- droplet_count: int32 [8, 64, 512], P(None, 'gx', 'gy'), may hold values from 0 to 64
Outputs:
- eastward_out: float32 [64, 512, 128], P('gx', 'gy')
- northward_out: float32 [64, 512, 128], P('gx', 'gy')
- vertical_out: float32 [64, 512, 128], P('gx', 'gy')
- pressure_out: float32 [64, 512, 128], P('gx', 'gy')
- theta_out: float32 [64, 512, 128], P('gx', 'gy')
- humidity_out: float32 [64, 512, 128], P('gx', 'gy')
- radius_out: float32 [64, 8, 64, 512], P(None, None, 'gx', 'gy')
- saturation_profile: float32 [128], replicated
All inputs are finite; a program needn't handle non-finite values.
Results may differ from a plain program's by a relative error of at most 0.0003.
Values sent between devices are 32-bit elements; how exact they have to be, the bound alone decides.
No kernel may reach another device: no remote copies, remote signals or barrier semaphores. Data moves between devices by JAX's collectives and lax.ppermute only.
A program may use at most 64 MiB of HBM per device.

v0:
```python
import jax
import jax.numpy as jnp
from jax import lax
from jax.sharding import PartitionSpec as P

SUB = 3


TIME_STEP = 1.0
BUOYANCY = 0.5
VAPOUR_SLOPE = 0.01
GROWTH_RATE = 25.0
RADIUS_FLOOR = 0.0625
MASS_FACTOR = 0.0004
LATENT_HEAT = 200.0


def padded_2(value, sides, width):
    for axis, dim in sides:
        count, length = (lax.axis_size(axis), value.shape[dim])
        up = [(i, (i + 1) % count) for i in range(count)]
        down = [(j, i) for i, j in up]
        last = lax.slice_in_dim(value, length - width, length, axis=dim)
        initial = lax.slice_in_dim(value, 0, width, axis=dim)
        before = lax.ppermute(last, axis, up)
        after = lax.ppermute(initial, axis, down)
        value = jnp.concatenate([before, value, after], axis=dim)
    return value


def column_tables(sound_speed):
    levels = sound_speed.shape[0]
    rows = lax.broadcasted_iota(jnp.int32, (levels, levels), 0)
    cols = lax.broadcasted_iota(jnp.int32, (levels, levels), 1)
    inside = rows < levels - 1
    gradient = jnp.where(inside & (cols == rows + 1), 1.0, 0.0) - jnp.where(
        inside & (cols == rows), 1.0, 0.0
    )
    gradient = gradient.astype(jnp.float32)
    scaled = gradient * sound_speed[None, :]
    product = jnp.dot(
        scaled, gradient.T, precision=lax.Precision.HIGHEST, preferred_element_type=jnp.float32
    )
    matrix = jnp.eye(levels, dtype=jnp.float32) + TIME_STEP * TIME_STEP * product
    factor = jnp.linalg.cholesky(matrix)
    identity = jnp.eye(levels, dtype=jnp.float32)
    halfway = lax.linalg.triangular_solve(factor, identity, left_side=True, lower=True)
    inverse = lax.linalg.triangular_solve(
        factor, halfway, left_side=True, lower=True, transpose_a=True
    )
    lifted = TIME_STEP * jnp.dot(
        gradient.T, inverse, precision=lax.Precision.HIGHEST, preferred_element_type=jnp.float32
    )
    return (inverse, lifted, gradient)


def column_update(pressure, vertical, heat, divergence, sound_speed, tables):
    inverse, lifted, gradient = tables
    levels = pressure.shape[-1]
    interior = (lax.broadcasted_iota(jnp.int32, (levels,), 0) < levels - 1).astype(jnp.float32)
    explicit = pressure - TIME_STEP * sound_speed * divergence
    forcing = (interior * (vertical + TIME_STEP * BUOYANCY * heat)).reshape(-1, levels)
    flat_explicit = explicit.reshape(-1, levels)
    solved = jnp.dot(
        forcing, inverse, precision=lax.Precision.HIGHEST, preferred_element_type=jnp.float32
    )
    solved = solved - jnp.dot(
        flat_explicit, lifted, precision=lax.Precision.HIGHEST, preferred_element_type=jnp.float32
    )
    stepped = jnp.dot(
        solved, gradient, precision=lax.Precision.HIGHEST, preferred_element_type=jnp.float32
    )
    new_pressure = flat_explicit + TIME_STEP * sound_speed * stepped
    return (new_pressure.reshape(explicit.shape), solved.reshape(explicit.shape))


def horizontal_velocity(eastward, northward, padded):
    grad_east = (padded[2:, 1:-1] - padded[:-2, 1:-1]) * 0.5
    grad_north = (padded[1:-1, 2:] - padded[1:-1, :-2]) * 0.5
    return (eastward - TIME_STEP * grad_east, northward - TIME_STEP * grad_north)


def horizontal_spread(east_padded, north_padded):
    return (
        east_padded[2:, 1:-1]
        - east_padded[:-2, 1:-1]
        + north_padded[1:-1, 2:]
        - north_padded[1:-1, :-2]
    ) * 0.5


def condense(theta, humidity, radius_sq, multiplicity, droplet_count):
    levels = theta.shape[2]
    layers = radius_sq.shape[1]
    lowest = levels // 4
    sat = humidity * jnp.exp(-VAPOUR_SLOPE * theta) - 1.0
    cloud = jnp.transpose(sat[:, :, lowest : lowest + layers], (2, 0, 1))
    grown = jnp.maximum(radius_sq + GROWTH_RATE * cloud[None], RADIUS_FLOOR)
    live = lax.broadcasted_iota(jnp.int32, radius_sq.shape, 0) < droplet_count[None]
    mass = multiplicity.astype(jnp.float32) * (
        grown * jnp.sqrt(grown) - radius_sq * jnp.sqrt(radius_sq)
    )
    change = MASS_FACTOR * jnp.sum(jnp.where(live, mass, 0.0), axis=0)
    added = jnp.pad(
        jnp.transpose(change, (1, 2, 0)), ((0, 0), (0, 0), (lowest, levels - lowest - layers))
    )
    humidity_out = humidity - added
    theta_out = theta + LATENT_HEAT * added
    radius_out = jnp.where(live, grown, 0.0)
    percent = 100.0 * (humidity_out * jnp.exp(-VAPOUR_SLOPE * theta_out) - 1.0)
    return (humidity_out, theta_out, radius_out, percent)


def level_means(percent, theta_out, columns):
    totals = lax.psum(
        (jnp.sum(percent, axis=(0, 1)), jnp.sum(theta_out, axis=(0, 1))), ("gx", "gy")
    )
    return (totals[0] / columns, totals[1] / columns)


def local(
    eastward,
    northward,
    vertical,
    pressure,
    theta,
    humidity,
    sound_speed,
    radius_sq,
    multiplicity,
    droplet_count,
):
    humidity_out, theta_out, radius_out, percent = condense(
        theta, humidity, radius_sq, multiplicity, droplet_count
    )
    columns = float(theta.shape[0] * theta.shape[1] * lax.axis_size("gx") * lax.axis_size("gy"))
    tables = column_tables(sound_speed)
    saturation_profile, theta_mean = level_means(percent, theta_out, columns)
    heat = theta_out - theta_mean
    margin = 2 * SUB
    eastward, northward, vertical, pressure, heating = (
        padded_2(eastward, (("gx", 0), ("gy", 1)), margin),
        padded_2(northward, (("gx", 0), ("gy", 1)), margin),
        padded_2(vertical, (("gx", 0), ("gy", 1)), margin),
        padded_2(pressure, (("gx", 0), ("gy", 1)), margin),
        padded_2(heat, (("gx", 0), ("gy", 1)), margin),
    )
    for substep in range(SUB):
        east_new, north_new = horizontal_velocity(
            eastward[1:-1, 1:-1], northward[1:-1, 1:-1], pressure
        )
        spread = horizontal_spread(east_new, north_new)
        heating = heating[2:-2, 2:-2]
        pressure, vertical = column_update(
            pressure[2:-2, 2:-2], vertical[2:-2, 2:-2], heating, spread, sound_speed, tables
        )
        eastward, northward = (east_new[1:-1, 1:-1], north_new[1:-1, 1:-1])
    return (
        eastward,
        northward,
        vertical,
        pressure,
        theta_out,
        humidity_out,
        radius_out,
        saturation_profile,
    )


def solution(mesh):
    return jax.shard_map(
        local,
        mesh=mesh,
        in_specs=(
            P("gx", "gy", None),
            P("gx", "gy", None),
            P("gx", "gy", None),
            P("gx", "gy", None),
            P("gx", "gy", None),
            P("gx", "gy", None),
            P(),
            P(None, None, "gx", "gy"),
            P(None, None, "gx", "gy"),
            P(None, "gx", "gy"),
        ),
        out_specs=(
            P("gx", "gy", None),
            P("gx", "gy", None),
            P("gx", "gy", None),
            P("gx", "gy", None),
            P("gx", "gy", None),
            P("gx", "gy", None),
            P(None, None, "gx", "gy"),
            P(),
        ),
        check_vma=False,
    )
```

profile of v0, /device:TPU:0, one launch (start us, length us, event | category | flops | bytes accessed | tf_op | source)
XLA Modules:
  0.0 179.3 jit_solution(16261416911662587209)
XLA Ops:
  0.7 2.1 %fusion.102 = (f32[6,128,128]{2,1,0:T(8,128)}, f32[6,128,128]{2,1,0:T(8,128)}) fusion(f32[8,128,128]{2,1,0:T(8,128)} %param.13), kind=kLoop, calls=%fused_computation.159 | loop fusion | bytes 1572864 | tf_op jit(solution)/shard_map/slice | solution.py:24
  3.3 2.9 %collective-permute-start.5 = (f32[6,128,128]{2,1,0:T(8,128)}, f32[6,128,128]{2,1,0:T(8,128)}, u32[]{:S(2)}, u32[]{:S(2)}) collective-permute-start(f32[6,128,128]{2,1,0:T(8,128)} %get-tuple-element.67), channel_id=1, source_target_pairs={{4,0},{8,4},{12,8},{16,12},{20,16},{24,20},{28,24},{0,28},{5,1},{9... | collective-permute-start | bytes 1179656 | tf_op jit(solution)/shard_map/ppermute | solution.py:26
  7.2 2.6 %collective-permute-start.1 = (f32[6,128,128]{2,1,0:T(8,128)}, f32[6,128,128]{2,1,0:T(8,128)}, u32[]{:S(2)}, u32[]{:S(2)}) collective-permute-start(f32[6,128,128]{2,1,0:T(8,128)} %get-tuple-element.63), channel_id=1, source_target_pairs={{4,0},{8,4},{12,8},{16,12},{20,16},{24,20},{28,24},{0,28},{5,1},{9... | collective-permute-start | bytes 1179656 | tf_op jit(solution)/shard_map/ppermute | solution.py:26
  11.5 4.9 %fusion.6 = (f32[64,8,8,128]{3,2,1,0:T(8,128)}, f32[8,8,128]{2,1,0:T(8,128)S(1)}) fusion(f32[64,8,8,128]{3,2,1,0:T(8,128)} %param.17, f32[8,8,128]{2,1,0:T(8,128)S(1)} %fusion.58, s32[8,8,128]{2,1,0:T(8,128)S(1)} %copy-done.26, bf16[64,8,8,128]{3,2,1,0:T(8,128)(2,1)} %param.18), kind=kLoop, calls=%fused_computation.13 | loop fusion | flops 5758976 | bytes 5341184 | tf_op jit(solution)/shard_map/jit(_where)/select_n | solution.py:109
  17.4 44.2 %all-reduce.1 = (f32[128]{0:T(128)S(1)}, f32[128]{0:T(128)S(1)}) all-reduce(f32[128]{0:T(128)S(1)} %get-tuple-element.33, f32[128]{0:T(128)S(1)} %get-tuple-element.32), channel_id=1, replica_groups=mesh['gx'=8,'gy'=4] {'gx','gy'}, use_global_device_ids=true, to_apply=%region_2.3 | all-reduce | flops 256 | bytes 2048 | tf_op jit(solution)/shard_map/psum | solution.py:115
  63.8 11.7 %cholesky.17 = f32[128,128]{1,0:T(8,128)S(1)} custom-call(f32[128,128]{1,0:T(8,128)S(1)} %fusion.42), custom_call_target="Cholesky" | custom-call | tf_op jit(solution)/shard_map/jit(cholesky)/cholesky | solution.py:45
  76.9 9.8 %custom-call.8 = f32[1,128,128]{1,2,0:T(8,128)S(1)} custom-call(f32[1,128,128]{2,1,0:T(8,128)S(1)} %fusion.36), custom_call_target="InvertDiagBlocksLowerTriangular" | custom-call | tf_op jit(solution)/shard_map/triangular_solve | solution.py:48
  94.3 2.7 %collective-permute-start.9 = (f32[6,128,128]{2,1,0:T(8,128)}, f32[6,128,128]{2,1,0:T(8,128)}, u32[]{:S(2)}, u32[]{:S(2)}) collective-permute-start(f32[6,128,128]{2,1,0:T(8,128)} %get-tuple-element.65), channel_id=1, source_target_pairs={{4,0},{8,4},{12,8},{16,12},{20,16},{24,20},{28,24},{0,28},{5,1},{9... | collective-permute-start | bytes 1179656 | tf_op jit(solution)/shard_map/ppermute | solution.py:26
  98.1 4.5 %collective-permute-done.17 = f32[6,128,128]{1,0,2:T(8,128)S(1)} collective-permute-done((f32[6,128,128]{1,0,2:T(8,128)S(1)}, f32[6,128,128]{1,0,2:T(8,128)S(1)}, u32[]{:S(2)}, u32[]{:S(2)}) %collective-permute-start.17) | collective-permute-done | bytes 393248 | tf_op jit(solution)/shard_map/ppermute | solution.py:26
  102.5 2.8 %collective-permute-start.13 = (f32[6,128,128]{2,0,1:T(8,128)}, f32[6,128,128]{2,0,1:T(8,128)}, u32[]{:S(2)}, u32[]{:S(2)}) collective-permute-start(f32[6,128,128]{2,0,1:T(8,128)} %get-tuple-element.60), channel_id=1, source_target_pairs={{4,0},{8,4},{12,8},{16,12},{20,16},{24,20},{28,24},{0,28},{5,1},{9... | collective-permute-start | bytes 1179656 | tf_op jit(solution)/shard_map/ppermute | solution.py:26
  105.3 3.0 %collective-permute-done.16 = f32[6,128,128]{1,0,2:T(8,128)S(1)} collective-permute-done((f32[6,128,128]{1,0,2:T(8,128)S(1)}, f32[6,128,128]{1,0,2:T(8,128)S(1)}, u32[]{:S(2)}, u32[]{:S(2)}) %collective-permute-start.16) | collective-permute-done | bytes 393248 | tf_op jit(solution)/shard_map/ppermute | solution.py:25
  108.6 1.6 collective-permute-start.7
  111.2 2.1 %fusion.94 = (f32[20,6,128]{1,0,2:T(8,128)}, f32[20,6,128]{1,0,2:T(8,128)}) fusion(f32[20,128,128]{1,0,2:T(8,128)S(1)} %pad_maximum_fusion.1), kind=kLoop, calls=%fused_computation.151 | loop fusion | bytes 245760 | tf_op jit(solution)/shard_map/slice | solution.py:23
  117.0 1.9 %copy.56 = f32[20,6,128]{2,0,1:T(8,128)S(1)} copy(f32[20,6,128]{1,0,2:T(8,128)} %get-tuple-element.43) | data formatting | bytes 122880 | tf_op jit(solution)/shard_map/slice | solution.py:24
  118.9 1.9 %copy.55 = f32[20,6,128]{2,0,1:T(8,128)S(1)} copy(f32[20,6,128]{1,0,2:T(8,128)} %get-tuple-element.42) | data formatting | bytes 122880 | tf_op jit(solution)/shard_map/slice | solution.py:23
  120.8 3.4 %collective-permute-start.3 = (f32[20,6,128]{2,1,0:T(8,128)S(1)}, f32[20,6,128]{2,1,0:T(8,128)S(1)}, u32[]{:S(2)}, u32[]{:S(2)}) collective-permute-start(f32[20,6,128]{2,1,0:T(8,128)S(1)} %get-tuple-element.47), channel_id=1, source_target_pairs={{1,0},{2,1},{3,2},{0,3},{5,4},{6,5},{7,6},{4,7},{9,8},{10,9},{11,1... | collective-permute-start | bytes 184328 | tf_op jit(solution)/shard_map/ppermute | solution.py:26
  124.2 1.8 constant_dynamic-update-slice_fusion.6
  127.0 2.0 %collective-permute-start.18 = (f32[20,6,128]{2,0,1:T(8,128)S(1)}, f32[20,6,128]{2,0,1:T(8,128)S(1)}, u32[]{:S(2)}, u32[]{:S(2)}) collective-permute-start(f32[20,6,128]{2,0,1:T(8,128)S(1)} %copy.55), channel_id=1, source_target_pairs={{0,1},{1,2},{2,3},{3,0},{4,5},{5,6},{6,7},{7,4},{8,9},{9,10},{10,1... | collective-permute-start | bytes 184328 | tf_op jit(solution)/shard_map/ppermute | solution.py:25
  131.6 1.5 copy.58
  133.1 1.8 copy.50
  134.9 2.1 %collective-permute-start.15 = (f32[20,6,128]{2,0,1:T(8,128)S(1)}, f32[20,6,128]{2,0,1:T(8,128)S(1)}, u32[]{:S(2)}, u32[]{:S(2)}) collective-permute-start(f32[20,6,128]{2,0,1:T(8,128)S(1)} %get-tuple-element.41), channel_id=1, source_target_pairs={{1,0},{2,1},{3,2},{0,3},{5,4},{6,5},{7,6},{4,7},{9,8},{10,9},{11,1... | collective-permute-start | bytes 184328 | tf_op jit(solution)/shard_map/ppermute | solution.py:26
  137.3 2.4 %collective-permute-done.15 = f32[20,6,128]{2,0,1:T(8,128)S(1)} collective-permute-done((f32[20,6,128]{2,0,1:T(8,128)S(1)}, f32[20,6,128]{2,0,1:T(8,128)S(1)}, u32[]{:S(2)}, u32[]{:S(2)}) %collective-permute-start.15) | collective-permute-done | bytes 61472 | tf_op jit(solution)/shard_map/ppermute | solution.py:26
  139.7 4.5 %collective-permute-done.14 = f32[20,6,128]{2,0,1:T(8,128)S(1)} collective-permute-done((f32[20,6,128]{2,0,1:T(8,128)S(1)}, f32[20,6,128]{2,0,1:T(8,128)S(1)}, u32[]{:S(2)}, u32[]{:S(2)}) %collective-permute-start.14) | collective-permute-done | bytes 61472 | tf_op jit(solution)/shard_map/ppermute | solution.py:25
  145.6 2.1 %collective-permute-start.10 = (f32[20,6,128]{2,1,0:T(8,128)S(1)}, f32[20,6,128]{2,1,0:T(8,128)S(1)}, u32[]{:S(2)}, u32[]{:S(2)}) collective-permute-start(f32[20,6,128]{2,1,0:T(8,128)S(1)} %get-tuple-element.48), channel_id=1, source_target_pairs={{0,1},{1,2},{2,3},{3,0},{4,5},{5,6},{6,7},{7,4},{8,9},{9,10},{10,1... | collective-permute-start | bytes 184328 | tf_op jit(solution)/shard_map/ppermute | solution.py:25
  149.1 2.8 %collective-permute-done.10 = f32[20,6,128]{2,1,0:T(8,128)S(1)} collective-permute-done((f32[20,6,128]{2,1,0:T(8,128)S(1)}, f32[20,6,128]{2,1,0:T(8,128)S(1)}, u32[]{:S(2)}, u32[]{:S(2)}) %collective-permute-start.10) | collective-permute-done | bytes 61472 | tf_op jit(solution)/shard_map/ppermute | solution.py:25
  157.0 2.1 %reshape.77 = f32[1584,128]{1,0:T(8,128)} reshape(f32[12,132,128]{2,1,0:T(8,128)} %fusion.23) | data formatting | bytes 1622016 | tf_op jit(solution)/shard_map/reshape | solution.py:63
  159.1 2.3 %fusion.21 = f32[12,132,128]{2,1,0:T(8,128)} fusion(f32[20,140,128]{2,1,0:T(8,128)} %copy-done.2, f32[16,136,128]{2,1,0:T(8,128)S(1)} %bitcast.50, f32[128]{0:T(128)S(1)} %fusion.81), kind=kLoop, calls=%fused_computation.50 | loop fusion | flops 608256 | bytes 2433536 | tf_op jit(solution)/shard_map/mul | solution.py:62
  161.3 2.2 %reshape.79 = f32[1584,128]{1,0:T(8,128)} reshape(f32[12,132,128]{2,1,0:T(8,128)} %fusion.21) | data formatting | bytes 1622016 | tf_op jit(solution)/shard_map/reshape | solution.py:62
  163.5 1.9 %fusion.104 = f32[1584,128]{1,0:T(8,128)S(1)} fusion(f32[1584,128]{1,0:T(8,128)} %reshape.79, f32[128,128]{1,0:T(8,128)S(1)} %fusion.37), kind=kOutput, calls=%fused_computation.161 | convolution fusion | flops 311427072 | bytes 1687552 | tf_op jit(solution)/shard_map/dot_general | solution.py:64
  167.2 1.8 fusion.1
  169.0 2.1 %reshape.81 = f32[12,132,128]{2,1,0:T(8,128)} reshape(f32[1584,128]{1,0:T(8,128)} %copy-done.5) | data formatting | bytes 1622016 | tf_op jit(solution)/shard_map/reshape | solution.py:74
  177.8 1.5 fusion.11
  (162 shorter events, 41.2 us)
Async XLA Ops:
  0.6 9.2 %copy-start.10 = (f32[8,128,128]{2,1,0:T(8,128)S(1)}, f32[8,128,128]{2,1,0:T(8,128)}, u32[]{:S(2)}) copy-start(f32[8,128,128]{2,1,0:T(8,128)} %param.11) | copy-start | bytes 1572868
  2.8 88.2 %collective-permute-start.4 = (f32[6,128,128]{2,1,0:T(8,128)}, f32[6,128,128]{2,1,0:T(8,128)}, u32[]{:S(2)}, u32[]{:S(2)}) collective-permute-start(f32[6,128,128]{2,1,0:T(8,128)} %get-tuple-element.68), channel_id=1, source_target_pairs={{0,4},{4,8},{8,12},{12,16},{16,20},{20,24},{24,28},{28,0},{1,5},{5... | collective-permute-start | bytes 1179656 | tf_op jit(solution)/shard_map/ppermute | solution.py:25
  3.3 7.5 %copy-start.21 = (f32[8,128,128]{2,1,0:T(8,128)S(1)}, f32[8,128,128]{2,1,0:T(8,128)}, u32[]{:S(2)}) copy-start(f32[8,128,128]{2,1,0:T(8,128)} %param.15) | copy-start | bytes 1572868
  3.3 91.0 %collective-permute-start.5 = (f32[6,128,128]{2,1,0:T(8,128)}, f32[6,128,128]{2,1,0:T(8,128)}, u32[]{:S(2)}, u32[]{:S(2)}) collective-permute-start(f32[6,128,128]{2,1,0:T(8,128)} %get-tuple-element.67), channel_id=1, source_target_pairs={{4,0},{8,4},{12,8},{16,12},{20,16},{24,20},{28,24},{0,28},{5,1},{9... | collective-permute-start | bytes 1179656 | tf_op jit(solution)/shard_map/ppermute | solution.py:26
  7.2 86.0 %collective-permute-start = (f32[6,128,128]{2,1,0:T(8,128)}, f32[6,128,128]{2,1,0:T(8,128)}, u32[]{:S(2)}, u32[]{:S(2)}) collective-permute-start(f32[6,128,128]{2,1,0:T(8,128)} %get-tuple-element.64), channel_id=1, source_target_pairs={{0,4},{4,8},{8,12},{12,16},{16,20},{20,24},{24,28},{28,0},{1,5},{5... | collective-permute-start | bytes 1179656 | tf_op jit(solution)/shard_map/ppermute | solution.py:25
  7.2 106.2 %collective-permute-start.1 = (f32[6,128,128]{2,1,0:T(8,128)}, f32[6,128,128]{2,1,0:T(8,128)}, u32[]{:S(2)}, u32[]{:S(2)}) collective-permute-start(f32[6,128,128]{2,1,0:T(8,128)} %get-tuple-element.63), channel_id=1, source_target_pairs={{4,0},{8,4},{12,8},{16,12},{20,16},{24,20},{28,24},{0,28},{5,1},{9... | collective-permute-start | bytes 1179656 | tf_op jit(solution)/shard_map/ppermute | solution.py:26
  10.8 97.8 %collective-permute-start.8 = (f32[6,128,128]{2,1,0:T(8,128)}, f32[6,128,128]{2,1,0:T(8,128)}, u32[]{:S(2)}, u32[]{:S(2)}) collective-permute-start(f32[6,128,128]{2,1,0:T(8,128)} %get-tuple-element.66), channel_id=1, source_target_pairs={{0,4},{4,8},{8,12},{12,16},{16,20},{20,24},{24,28},{28,0},{1,5},{5... | collective-permute-start | bytes 1179656 | tf_op jit(solution)/shard_map/ppermute | solution.py:25
  10.8 155.5 %copy-start.28 = (s32[128]{0:T(128)}, s32[128]{0:T(128)S(1)}, u32[]{:S(2)}) copy-start(s32[128]{0:T(128)S(1)} %iota_add_fusion) | copy-start | bytes 1540
  10.8 155.5 %copy-start.30 = (pred[128]{0:T(512)(128)(4,1)}, pred[128]{0:T(512)(128)(4,1)S(1)}, u32[]{:S(2)}) copy-start(pred[128]{0:T(512)(128)(4,1)S(1)} %iota_compare_fusion.6) | copy-start | bytes 388
  17.4 70.1 %copy-start = (f32[8,128,128]{1,0,2:T(8,128)}, f32[8,128,128]{1,0,2:T(8,128)S(1)}, u32[]{:S(2)}) copy-start(f32[8,128,128]{1,0,2:T(8,128)S(1)} %get-tuple-element.37) | copy-start | bytes 1572868
  63.4 25.2 %copy-start.23 = (f32[8,128,128]{2,1,0:T(8,128)S(1)}, f32[8,128,128]{2,1,0:T(8,128)}, u32[]{:S(2)}) copy-start(f32[8,128,128]{2,1,0:T(8,128)} %param.12) | copy-start | bytes 1572868
  87.5 77.9 %copy-start.19 = (f32[128,128]{1,0:T(8,128)}, f32[128,128]{1,0:T(8,128)S(1)}, u32[]{:S(2)}) copy-start(f32[128,128]{1,0:T(8,128)S(1)} %fusion.44) | copy-start | bytes 196612
  87.6 68.1 %copy-start.34 = (f32[128]{0:T(128)}, f32[128]{0:T(128)S(1)}, u32[]{:S(2)}) copy-start(f32[128]{0:T(128)S(1)} %broadcast_multiply_fusion.2) | copy-start | bytes 1540
  87.6 71.5 %copy-start.32 = (f32[128]{0:T(128)}, f32[128]{0:T(128)S(1)}, u32[]{:S(2)}) copy-start(f32[128]{0:T(128)S(1)} %fusion.81) | copy-start | bytes 1540
  91.2 11.3 %collective-permute-start.17 = (f32[6,128,128]{1,0,2:T(8,128)S(1)}, f32[6,128,128]{1,0,2:T(8,128)S(1)}, u32[]{:S(2)}, u32[]{:S(2)}) collective-permute-start(f32[6,128,128]{1,0,2:T(8,128)S(1)} %copy-done.25), channel_id=1, source_target_pairs={{4,0},{8,4},{12,8},{16,12},{20,16},{24,20},{28,24},{0,28},{5,1},{9... | collective-permute-start | bytes 1179656 | tf_op jit(solution)/shard_map/ppermute | solution.py:26
  93.1 15.2 %collective-permute-start.16 = (f32[6,128,128]{1,0,2:T(8,128)S(1)}, f32[6,128,128]{1,0,2:T(8,128)S(1)}, u32[]{:S(2)}, u32[]{:S(2)}) collective-permute-start(f32[6,128,128]{1,0,2:T(8,128)S(1)} %copy-done.24), channel_id=1, source_target_pairs={{0,4},{4,8},{8,12},{12,16},{16,20},{20,24},{24,28},{28,0},{1,5},{5... | collective-permute-start | bytes 1179656 | tf_op jit(solution)/shard_map/ppermute | solution.py:25
  94.3 26.5 %collective-permute-start.9 = (f32[6,128,128]{2,1,0:T(8,128)}, f32[6,128,128]{2,1,0:T(8,128)}, u32[]{:S(2)}, u32[]{:S(2)}) collective-permute-start(f32[6,128,128]{2,1,0:T(8,128)} %get-tuple-element.65), channel_id=1, source_target_pairs={{4,0},{8,4},{12,8},{16,12},{20,16},{24,20},{28,24},{0,28},{5,1},{9... | collective-permute-start | bytes 1179656 | tf_op jit(solution)/shard_map/ppermute | solution.py:26
  98.1 10.5 %copy-start.11 = (f32[20,128,128]{2,1,0:T(8,128)}, f32[20,128,128]{2,1,0:T(8,128)S(1)}, u32[]{:S(2)}) copy-start(f32[20,128,128]{2,1,0:T(8,128)S(1)} %constant_dynamic-update-slice_fusion.3) | copy-start | bytes 3932164
  102.5 24.4 %collective-permute-start.13 = (f32[6,128,128]{2,0,1:T(8,128)}, f32[6,128,128]{2,0,1:T(8,128)}, u32[]{:S(2)}, u32[]{:S(2)}) collective-permute-start(f32[6,128,128]{2,0,1:T(8,128)} %get-tuple-element.60), channel_id=1, source_target_pairs={{4,0},{8,4},{12,8},{16,12},{20,16},{24,20},{28,24},{0,28},{5,1},{9... | collective-permute-start | bytes 1179656 | tf_op jit(solution)/shard_map/ppermute | solution.py:26
  108.3 18.7 %collective-permute-start.12 = (f32[6,128,128]{2,0,1:T(8,128)}, f32[6,128,128]{2,0,1:T(8,128)}, u32[]{:S(2)}, u32[]{:S(2)}) collective-permute-start(f32[6,128,128]{2,0,1:T(8,128)} %get-tuple-element.59), channel_id=1, source_target_pairs={{0,4},{4,8},{8,12},{12,16},{16,20},{20,24},{24,28},{28,0},{1,5},{5... | collective-permute-start | bytes 1179656 | tf_op jit(solution)/shard_map/ppermute | solution.py:25
  108.6 37.0 %collective-permute-start.7 = (f32[20,6,128]{2,1,0:T(8,128)S(1)}, f32[20,6,128]{2,1,0:T(8,128)S(1)}, u32[]{:S(2)}, u32[]{:S(2)}) collective-permute-start(f32[20,6,128]{2,1,0:T(8,128)S(1)} %get-tuple-element.51), channel_id=1, source_target_pairs={{1,0},{2,1},{3,2},{0,3},{5,4},{6,5},{7,6},{4,7},{9,8},{10,9},{11,1... | collective-permute-start | bytes 184328 | tf_op jit(solution)/shard_map/ppermute | solution.py:26
  113.3 34.3 %collective-permute-start.6 = (f32[20,6,128]{2,1,0:T(8,128)S(1)}, f32[20,6,128]{2,1,0:T(8,128)S(1)}, u32[]{:S(2)}, u32[]{:S(2)}) collective-permute-start(f32[20,6,128]{2,1,0:T(8,128)S(1)} %get-tuple-element.50), channel_id=1, source_target_pairs={{0,1},{1,2},{2,3},{3,0},{4,5},{5,6},{6,7},{7,4},{8,9},{9,10},{10,1... | collective-permute-start | bytes 184328 | tf_op jit(solution)/shard_map/ppermute | solution.py:25
  120.8 27.0 %collective-permute-start.3 = (f32[20,6,128]{2,1,0:T(8,128)S(1)}, f32[20,6,128]{2,1,0:T(8,128)S(1)}, u32[]{:S(2)}, u32[]{:S(2)}) collective-permute-start(f32[20,6,128]{2,1,0:T(8,128)S(1)} %get-tuple-element.47), channel_id=1, source_target_pairs={{1,0},{2,1},{3,2},{0,3},{5,4},{6,5},{7,6},{4,7},{9,8},{10,9},{11,1... | collective-permute-start | bytes 184328 | tf_op jit(solution)/shard_map/ppermute | solution.py:26
  126.9 8.0 %collective-permute-start.19 = (f32[20,6,128]{2,0,1:T(8,128)S(1)}, f32[20,6,128]{2,0,1:T(8,128)S(1)}, u32[]{:S(2)}, u32[]{:S(2)}) collective-permute-start(f32[20,6,128]{2,0,1:T(8,128)S(1)} %copy.56), channel_id=1, source_target_pairs={{1,0},{2,1},{3,2},{0,3},{5,4},{6,5},{7,6},{4,7},{9,8},{10,9},{11,1... | collective-permute-start | bytes 184328 | tf_op jit(solution)/shard_map/ppermute | solution.py:26
  127.0 10.1 %collective-permute-start.18 = (f32[20,6,128]{2,0,1:T(8,128)S(1)}, f32[20,6,128]{2,0,1:T(8,128)S(1)}, u32[]{:S(2)}, u32[]{:S(2)}) collective-permute-start(f32[20,6,128]{2,0,1:T(8,128)S(1)} %copy.55), channel_id=1, source_target_pairs={{0,1},{1,2},{2,3},{3,0},{4,5},{5,6},{6,7},{7,4},{8,9},{9,10},{10,1... | collective-permute-start | bytes 184328 | tf_op jit(solution)/shard_map/ppermute | solution.py:25
  134.9 4.8 %collective-permute-start.15 = (f32[20,6,128]{2,0,1:T(8,128)S(1)}, f32[20,6,128]{2,0,1:T(8,128)S(1)}, u32[]{:S(2)}, u32[]{:S(2)}) collective-permute-start(f32[20,6,128]{2,0,1:T(8,128)S(1)} %get-tuple-element.41), channel_id=1, source_target_pairs={{1,0},{2,1},{3,2},{0,3},{5,4},{6,5},{7,6},{4,7},{9,8},{10,9},{11,1... | collective-permute-start | bytes 184328 | tf_op jit(solution)/shard_map/ppermute | solution.py:26
  137.1 7.1 %collective-permute-start.14 = (f32[20,6,128]{2,0,1:T(8,128)S(1)}, f32[20,6,128]{2,0,1:T(8,128)S(1)}, u32[]{:S(2)}, u32[]{:S(2)}) collective-permute-start(f32[20,6,128]{2,0,1:T(8,128)S(1)} %get-tuple-element.40), channel_id=1, source_target_pairs={{0,1},{1,2},{2,3},{3,0},{4,5},{5,6},{6,7},{7,4},{8,9},{9,10},{10,1... | collective-permute-start | bytes 184328 | tf_op jit(solution)/shard_map/ppermute | solution.py:25
  137.3 7.2 %copy-start.2 = (f32[20,140,128]{2,1,0:T(8,128)}, f32[20,140,128]{2,1,0:T(8,128)S(1)}, u32[]{:S(2)}) copy-start(f32[20,140,128]{2,1,0:T(8,128)S(1)} %pad_maximum_fusion.3) | copy-start | bytes 4300804
  139.7 8.1 %collective-permute-start.2 = (f32[20,6,128]{2,1,0:T(8,128)S(1)}, f32[20,6,128]{2,1,0:T(8,128)S(1)}, u32[]{:S(2)}, u32[]{:S(2)}) collective-permute-start(f32[20,6,128]{2,1,0:T(8,128)S(1)} %get-tuple-element.46), channel_id=1, source_target_pairs={{0,1},{1,2},{2,3},{3,0},{4,5},{5,6},{6,7},{7,4},{8,9},{9,10},{10,1... | collective-permute-start | bytes 184328 | tf_op jit(solution)/shard_map/ppermute | solution.py:25
  144.2 4.9 %collective-permute-start.11 = (f32[20,6,128]{2,1,0:T(8,128)S(1)}, f32[20,6,128]{2,1,0:T(8,128)S(1)}, u32[]{:S(2)}, u32[]{:S(2)}) collective-permute-start(f32[20,6,128]{2,1,0:T(8,128)S(1)} %get-tuple-element.49), channel_id=1, source_target_pairs={{1,0},{2,1},{3,2},{0,3},{5,4},{6,5},{7,6},{4,7},{9,8},{10,9},{11,1... | collective-permute-start | bytes 184328 | tf_op jit(solution)/shard_map/ppermute | solution.py:26
  145.6 6.3 %copy-start.14 = (f32[20,128,128]{2,1,0:T(8,128)S(1)}, f32[20,128,128]{2,1,0:T(8,128)}, u32[]{:S(2)}) copy-start(f32[20,128,128]{2,1,0:T(8,128)} %constant_dynamic-update-slice_fusion.6) | copy-start | bytes 3932164
  145.6 6.3 %collective-permute-start.10 = (f32[20,6,128]{2,1,0:T(8,128)S(1)}, f32[20,6,128]{2,1,0:T(8,128)S(1)}, u32[]{:S(2)}, u32[]{:S(2)}) collective-permute-start(f32[20,6,128]{2,1,0:T(8,128)S(1)} %get-tuple-element.48), channel_id=1, source_target_pairs={{0,1},{1,2},{2,3},{3,0},{4,5},{5,6},{6,7},{7,4},{8,9},{9,10},{10,1... | collective-permute-start | bytes 184328 | tf_op jit(solution)/shard_map/ppermute | solution.py:25
  (24 other events, 50.7 us)
where the time goes:
time: 180 us; the launch traced here: 179 us
  blocking collectives  44.2 us (25%)
  local copies, waits for them, and re-layouts  39.7 us (22%)
  other arithmetic  39.6 us (22%)
  starting transfers between devices  24.3 us (14%)
  waiting for transfers between devices  18.4 us (10%)
  matrix products  11.8 us (7%)
    psum x1, blocking collectives, level_means(): lax.psum((jnp.sum(percent, axis=(0, 1)), jnp.sum(theta_out, axis=(0, 1)))...  44.2 us
    ppermute x10, starting transfers between devices, padded_2(): after = lax.ppermute(initial, axis, down)  19.1 us
    another operation x3, other arithmetic, column_tables(): factor = jnp.linalg.cholesky(matrix)  12.4 us
    unnamed x84, local copies, waits for them, and re-layouts  11.7 us
    another operation x2, other arithmetic, column_tables(): lax.linalg.triangular_solve(factor, halfway, left_side=True, lower=True,...  10.5 us
    ppermute x10, waiting for transfers between devices, padded_2(): before = lax.ppermute(last, axis, up)  10.3 us
    ppermute x10, waiting for transfers between devices, padded_2(): after = lax.ppermute(initial, axis, down)  8.11 us
    concatenate x5, local copies, waits for them, and re-layouts, padded_2(): value = jnp.concatenate([before, value, after], axis=dim)  7.08 us
  transfers between devices with their start and end apart: 20, of which 6 were waited for; matrix products, arithmetic and copies ran while one was open for 32% of the time, Pallas kernels for 0%

commit v1 on v0

v1 whole, which is shorter than its diff:
```python
import functools

import jax
import jax.numpy as jnp
from jax import lax
from jax.experimental import pallas as pl
from jax.experimental.pallas import tpu as pltpu
from jax.sharding import PartitionSpec as P

SUB = 3
BUOYANCY = 0.5
VAPOUR_SLOPE = 0.01
GROWTH_RATE = 25.0
RADIUS_FLOOR = 0.0625
MASS_FACTOR = 0.0004
LATENT_HEAT = 200.0
TERMS = 6
CHUNK = 8
GRANT = 24 * 1024 * 1024

VMEM = pl.BlockSpec(memory_space=pltpu.VMEM)


def exact_dot(a, b):
    return jnp.dot(a, b, precision=lax.Precision.HIGHEST, preferred_element_type=jnp.float32)


def power15(x):
    return x * x * lax.rsqrt(x)


def condense_kernel(
    sound_ref,
    theta_ref,
    humidity_ref,
    radius_ref,
    mult_ref,
    count_ref,
    theta_out,
    humidity_out,
    radius_out,
    sums_out,
    inverse_out,
    cloud,
    total,
    series,
    power,
):
    step, steps = (pl.program_id(0), pl.num_programs(0))
    rows, cols, levels = theta_ref.shape
    layers = count_ref.shape[0]
    lowest = levels // 4

    @pl.when(step == 0)
    def _():
        for i in range(rows):
            sat = humidity_ref[i] * jnp.exp(-VAPOUR_SLOPE * theta_ref[i]) - 1.0
            cloud[:, i, :] = GROWTH_RATE * sat.T[lowest : lowest + layers]
        total[...] = jnp.zeros_like(total)
        r = lax.broadcasted_iota(jnp.int32, (levels, levels), 0)
        k = lax.broadcasted_iota(jnp.int32, (levels, levels), 1)
        sound = jnp.broadcast_to(sound_ref[...], (levels, levels))
        upper = jnp.where((k == r + 1) & (k < levels - 1), -sound, 0.0)
        above = pltpu.roll(sound, levels - 1, 1)
        diagonal = jnp.where(k == r, jnp.where(k < levels - 1, 1.0 + sound + above, 1.0), 0.0)
        eye = jnp.where(k == r, 1.0, 0.0)
        residual = eye - (diagonal + upper + upper.T) * (1.0 / 3.0)
        series[...] = (eye + residual) * (1.0 / 3.0)
        power[...] = exact_dot(residual, residual)

    @pl.when((step > 0) & (step < TERMS))
    def _():
        old = series[...]
        series[...] = old + exact_dot(old, power[...])
        power[...] = exact_dot(power[...], power[...])

    for s in range(CHUNK):
        live = step * CHUNK + s < count_ref[...]
        radius = radius_ref[s]
        grown = jnp.maximum(radius + cloud[...], RADIUS_FLOOR)
        radius_out[s] = jnp.where(live, grown, 0.0)
        mass = mult_ref[s].astype(jnp.float32) * (power15(grown) - power15(radius))
        total[...] += jnp.where(live, mass, 0.0)

    @pl.when(step == steps - 1)
    def _():
        inverse_out[...] = series[...]
        percent_sum = jnp.zeros((cols, levels), jnp.float32)
        theta_sum = jnp.zeros((cols, levels), jnp.float32)
        for i in range(rows):
            change = MASS_FACTOR * total[:, i, :]
            added = jnp.concatenate(
                [
                    jnp.zeros((lowest, cols), jnp.float32),
                    change,
                    jnp.zeros((levels - lowest - layers, cols), jnp.float32),
                ],
                axis=0,
            ).T
            humid = humidity_ref[i] - added
            warm = theta_ref[i] + LATENT_HEAT * added
            humidity_out[i] = humid
            theta_out[i] = warm
            percent_sum += 100.0 * (humid * jnp.exp(-VAPOUR_SLOPE * warm) - 1.0)
            theta_sum += warm
        sums_out[0:1] = jnp.sum(percent_sum, axis=0, keepdims=True)
        sums_out[1:2] = jnp.sum(theta_sum, axis=0, keepdims=True)


def condense(sound, theta, humidity, radius_sq, multiplicity, count):
    slots = radius_sq.shape[0]
    levels = theta.shape[2]
    whole = lambda a: pl.BlockSpec(a.shape, lambda s: (0,) * a.ndim)
    part = pl.BlockSpec((CHUNK,) + radius_sq.shape[1:], lambda s: (s, 0, 0, 0))
    f32 = lambda *shape: jax.ShapeDtypeStruct(shape, jnp.float32)
    outs = (f32(*theta.shape), f32(*theta.shape), f32(*radius_sq.shape), f32(2, levels), f32(levels, levels))
    return pl.pallas_call(
        condense_kernel,
        grid=(slots // CHUNK,),
        in_specs=[whole(sound), whole(theta), whole(humidity), part, part, whole(count)],
        out_specs=[whole(outs[0]), whole(outs[1]), part, whole(outs[3]), whole(outs[4])],
        out_shape=outs,
        scratch_shapes=[
            pltpu.VMEM(radius_sq.shape[1:], jnp.float32),
            pltpu.VMEM(radius_sq.shape[1:], jnp.float32),
            pltpu.VMEM((levels, levels), jnp.float32),
            pltpu.VMEM((levels, levels), jnp.float32),
        ],
        compiler_params=pltpu.CompilerParams(
            dimension_semantics=("arbitrary",), vmem_limit_bytes=GRANT
        ),
        cost_estimate=pl.CostEstimate(
            flops=4_000_000_000, bytes_accessed=8_000_000, transcendentals=1_000_000
        ),
        name="condense",
    )(sound, theta, humidity, radius_sq, multiplicity, count)


def column_step(q, held, sound, inside, inverse):
    levels = q.shape[-1]
    source = inside * (held + q - pltpu.roll(q, levels - 1, 1))
    solved = exact_dot(source, inverse)
    masked = solved * inside
    return (q - sound * (masked - pltpu.roll(masked, 1, 1)), solved)


def substep_kernel(first, last, axes, columns, *refs):
    refs = list(refs)
    take = lambda n: [refs.pop(0) for _ in range(n)]
    sound_ref, inverse_ref, heat_ref, p_ref, u_ref, v_ref, w_ref = take(7)
    d_ref = None if first else refs.pop(0)
    xa, xb, ya, yb = take(4)
    sums_ref = refs.pop(0) if last else None
    u_out, v_out, w_out, p_out = take(4)
    if last:
        profile_out = refs.pop(0)
    else:
        d_out, sxa, sxb, sya, syb = take(5)
    wide, low, high = take(3)
    rows, cols, levels = p_ref.shape
    pad = 8
    even_x = lax.rem(lax.axis_index(axes[0]), 2) == 0
    even_y = lax.rem(lax.axis_index(axes[1]), 2) == 0
    low[...] = jnp.where(even_x, xb[...], xa[...])
    high[...] = jnp.where(even_x, xa[...], xb[...])
    wide[:, pad : pad + cols, :] = p_ref[...]
    for n in range(2):
        wide[:, pad - 2 + n, :] = jnp.where(even_y, yb[n], ya[n])
        wide[:, pad + cols + n, :] = jnp.where(even_y, ya[n], yb[n])
    sound = sound_ref[...]
    level = lax.broadcasted_iota(jnp.int32, (1, levels), 1)
    inside = (level < levels - 1).astype(jnp.float32)
    inverse = inverse_ref[...]
    if last:
        total = sums_ref[...] * (1.0 / columns)
        profile_out[...] = total[0:1]
        mean = jnp.broadcast_to(total[1:2], (8, levels))
        drift_p, drift_w = (jnp.zeros_like(mean), jnp.zeros_like(mean))
        for _ in range(SUB):
            drift_p, drift_w = column_step(
                drift_p, drift_w - BUOYANCY * mean, sound, inside, inverse
            )
        drift_p, drift_w = (drift_p[0:1], drift_w[0:1])

    def row(i):
        if i < 0:
            return low[i + 2]
        if i >= rows:
            return high[i - rows]
        return p_ref[i]

    for i in range(rows):
        p = p_ref[i]
        east = lambda n: wide[i, pad + n : pad + n + cols, :]
        u_out[i] = u_ref[i] - 0.5 * (row(i + 1) - row(i - 1))
        v_out[i] = v_ref[i] - 0.5 * (east(1) - east(-1))
        bend = 0.25 * ((row(i + 2) + row(i - 2)) + (east(2) + east(-2))) - p
        if first:
            spread = jnp.zeros_like(p)
            if i + 1 < rows:
                spread += u_ref[i + 1]
            if i > 0:
                spread -= u_ref[i - 1]
            j = lax.broadcasted_iota(jnp.int32, (cols, levels), 0)
            v = v_ref[i]
            spread += jnp.where(j < cols - 1, pltpu.roll(v, cols - 1, 0), 0.0)
            spread -= jnp.where(j > 0, pltpu.roll(v, 1, 0), 0.0)
            d = 0.5 * spread - bend
        else:
            d = d_ref[i] - bend
        new_p, new_w = column_step(
            p - sound * d, w_ref[i] + BUOYANCY * heat_ref[i], sound, inside, inverse
        )
        if last:
            new_p += drift_p
            new_w += drift_w
        else:
            d_out[i] = d
        p_out[i] = new_p
        w_out[i] = new_w
    if not last:
        up, down = (p_out[rows - 2 : rows], p_out[0:2])
        sxa[...] = jnp.where(even_x, up, down)
        sxb[...] = jnp.where(even_x, down, up)
        for n in range(2):
            up, down = (p_out[:, cols - 2 + n, :], p_out[:, n, :])
            sya[n] = jnp.where(even_y, up, down)
            syb[n] = jnp.where(even_y, down, up)


def substep(index, columns, sound, inverse, heat, state, halo, sums=None):
    first, last = (index == 0, index == SUB - 1)
    p = state[0]
    rows, cols, levels = p.shape
    f32 = lambda *shape: jax.ShapeDtypeStruct(shape, jnp.float32)
    outs = [f32(*p.shape)] * 4
    if last:
        outs += [f32(1, levels)]
    else:
        outs += [f32(*p.shape)] + [f32(2, cols, levels)] * 2 + [f32(2, rows, levels)] * 2
    args = [sound, inverse, heat, *state, *halo] + ([sums] if last else [])
    return pl.pallas_call(
        functools.partial(substep_kernel, first, last, ("gx", "gy"), columns),
        in_specs=[VMEM] * len(args),
        out_specs=[VMEM] * len(outs),
        out_shape=outs,
        scratch_shapes=[
            pltpu.VMEM((rows, cols + 16, levels), jnp.float32),
            pltpu.VMEM((2, cols, levels), jnp.float32),
            pltpu.VMEM((2, cols, levels), jnp.float32),
        ],
        compiler_params=pltpu.CompilerParams(vmem_limit_bytes=GRANT),
        cost_estimate=pl.CostEstimate(
            flops=1_000_000_000, bytes_accessed=6_000_000, transcendentals=0
        ),
        name=f"substep{index}",
    )(*args)


def swaps(count):
    near = [(i, i ^ 1) for i in range(count)]
    far = [(i, (i + 1) % count if i % 2 else (i - 1) % count) for i in range(count)]
    return near, far


def exchange(sends):
    xa, xb, ya, yb = sends
    near_x, far_x = swaps(lax.axis_size("gx"))
    near_y, far_y = swaps(lax.axis_size("gy"))
    return (
        lax.ppermute(xa, "gx", near_x),
        lax.ppermute(xb, "gx", far_x),
        lax.ppermute(ya, "gy", near_y),
        lax.ppermute(yb, "gy", far_y),
    )


def total_sum(value):
    for axis in ("gx", "gy"):
        count = lax.axis_size(axis)
        distance = 1
        while distance < count:
            value = value + lax.ppermute(value, axis, [(i, i ^ distance) for i in range(count)])
            distance *= 2
    return value


def local(
    eastward,
    northward,
    vertical,
    pressure,
    theta,
    humidity,
    sound_speed,
    radius_sq,
    multiplicity,
    droplet_count,
):
    columns = float(theta.shape[0] * theta.shape[1] * lax.axis_size("gx") * lax.axis_size("gy"))
    sound = sound_speed[None]
    p, u, v = (pressure, eastward, northward)
    even_x = lax.axis_index("gx") % 2 == 0
    even_y = lax.axis_index("gy") % 2 == 0
    up_x = jnp.stack([p[-2] + 2.0 * u[-1], p[-1]])
    down_x = jnp.stack([p[0], p[1] - 2.0 * u[0]])
    up_y = jnp.stack([p[:, -2] + 2.0 * v[:, -1], p[:, -1]])
    down_y = jnp.stack([p[:, 0], p[:, 1] - 2.0 * v[:, 0]])
    halo = exchange(
        (
            jnp.where(even_x, up_x, down_x),
            jnp.where(even_x, down_x, up_x),
            jnp.where(even_y, up_y, down_y),
            jnp.where(even_y, down_y, up_y),
        )
    )
    theta_out, humidity_out, radius_out, sums, inverse = condense(
        sound, theta, humidity, radius_sq, multiplicity, droplet_count
    )
    sums = total_sum(sums)
    state = (p, u, v, vertical)
    for index in range(SUB):
        done = index == SUB - 1
        results = substep(
            index, columns, sound, inverse, theta_out, state, halo, sums if done else None
        )
        u, v, w, p = results[:4]
        if not done:
            state = (p, u, v, w, results[4])
            halo = exchange(results[5:])
    profile = results[4][0]
    return (u, v, w, p, theta_out, humidity_out, radius_out, profile)


def solution(mesh):
    grid = P("gx", "gy", None)
    drops = P(None, None, "gx", "gy")
    return jax.shard_map(
        local,
        mesh=mesh,
        in_specs=(grid,) * 6 + (P(), drops, drops, P(None, "gx", "gy")),
        out_specs=(grid,) * 6 + (drops, P()),
        check_vma=False,
    )
```

time: 180 us -> 56.6 us (0.31)
  blocking collectives: 44.2 us -> 0 us
  other arithmetic: 39.6 us -> 1.07 us
  local copies, waits for them, and re-layouts: 39.7 us -> 9 us
  matrix products: 11.8 us -> 0 us
  Pallas kernels: 0 us -> 10.6 us
  starting transfers between devices: 24.3 us -> 19.2 us
  waiting for transfers between devices: 18.4 us -> 15.3 us
    psum x1 -> x0, blocking collectives: 44.2 us -> none  [level_means(): lax.psum((jnp.sum(percent, axis=(0, 1)), jnp.sum(theta_out, axis=(0, 1)))...]
    another operation x5 -> x0, other arithmetic: 22.9 us -> none  [the longest x3 12.4 us: column_tables(): factor = jnp.linalg.cholesky(matrix)]
    slice x13 -> x2, local copies, waits for them, and re-layouts: 13.1 us -> 1.64 us  [local(): up_y = jnp.stack([p[:, -2] + 2.0 * v[:, -1], p[:, -1]])]
    dot_general x11 -> x0, matrix products: 11.4 us -> none  [the longest x3 4.35 us: column_update(): jnp.dot(solved, gradient, precision=lax.Precision.HIGHEST, preferred_elem...]
    pallas_call x0 -> x4, Pallas kernels: none -> 10.6 us  [the longest x1 5.35 us: condense(): pl.pallas_call(condense_kernel, grid=(slots // CHUNK,), in_specs=[whole(s...]
    reshape x4 -> x0, local copies, waits for them, and re-layouts: 7.61 us -> none  [the longest x1 2.2 us: column_update(): (interior * (vertical + TIME_STEP * BUOYANCY * heat)).reshape(-1, levels)]
    concatenate x5 -> x0, local copies, waits for them, and re-layouts: 7.08 us -> none  [padded_2(): value = jnp.concatenate([before, value, after], axis=dim)]
    sub x7 -> x1, other arithmetic: 5.46 us -> 0.01 us  [local(): down_y = jnp.stack([p[:, 0], p[:, 1] - 2.0 * v[:, 0]])]
  transfers between devices with their start and end apart: 20 -> 17, of which waited for: 6 -> 7; matrix products, arithmetic and copies ran while one was open for 32% -> 2% of each run, Pallas kernels for 0% -> 10%
where the time goes in v1:
time: 56.6 us; the launch traced here: 56 us
  starting transfers between devices  19.2 us (34%)
  waiting for transfers between devices  15.3 us (27%)
  Pallas kernels  10.6 us (19%)
  local copies, waits for them, and re-layouts  9 us (16%)
  other arithmetic  1.07 us (2%)
  between operations  0.79 us (1%)
    ppermute x5, waiting for transfers between devices, total_sum(): lax.ppermute(value, axis, [(i, i ^ distance) for i in range(count)])  9.94 us
    unnamed x22, local copies, waits for them, and re-layouts  7.36 us
    ppermute x5, starting transfers between devices, total_sum(): lax.ppermute(value, axis, [(i, i ^ distance) for i in range(count)])  6.75 us
    ppermute x3, starting transfers between devices, exchange(): lax.ppermute(yb, 'gy', far_y)  5.45 us
    pallas_call x1, Pallas kernels, condense(): pl.pallas_call(condense_kernel, grid=(slots // CHUNK,), in_specs=[whole(s...  5.35 us
    pallas_call x3, Pallas kernels, substep(): pl.pallas_call(functools.partial(substep_kernel, first, last, ('gx', 'gy'...  5.25 us
    ppermute x3, starting transfers between devices, exchange(): lax.ppermute(xb, 'gx', far_x)  4.36 us
    ppermute x3, waiting for transfers between devices, exchange(): lax.ppermute(yb, 'gy', far_y)  3.82 us
  transfers between devices with their start and end apart: 17, of which 7 were waited for; matrix products, arithmetic and copies ran while one was open for 2% of the time, Pallas kernels for 10%

profile of v1, /device:TPU:0, one launch (start us, length us, event | category | flops | bytes accessed | tf_op | source)
XLA Modules:
  0.0 56.0 jit_solution(12141082545558424458)
XLA Ops:
  0.6 0.8 %fusion.4 = (f32[8,1,128]{2,1,0:T(1,128)S(1)}, f32[8,1,128]{2,1,0:T(1,128)S(1)}) fusion(f32[8,128,128]{2,1,0:T(8,128)} %refs_5_.1), kind=kLoop, calls=%fused_computation.12 | loop fusion | bytes 16384 | tf_op jit(solution)/shard_map/slice | solution.py:307
  1.4 0.8 %fusion.5 = (f32[8,1,128]{2,1,0:T(1,128)S(1)}, f32[8,1,128]{2,1,0:T(1,128)S(1)}, f32[8,1,128]{2,1,0:T(1,128)S(1)}, f32[8,1,128]{2,1,0:T(1,128)S(1)}) fusion(f32[8,128,128]{2,1,0:T(8,128)} %refs_3_.1), kind=kLoop, calls=%fused_computation.13 | loop fusion | bytes 32768 | tf_op jit(solution)/shard_map/slice | solution.py:307
  2.3 5.1 %collective-permute-start.3 = (f32[2,8,128]{2,1,0:T(8,128)S(1)}, f32[2,8,128]{2,1,0:T(8,128)S(1)}, u32[]{:S(2)}, u32[]{:S(2)}) collective-permute-start(f32[2,8,128]{2,1,0:T(8,128)S(1)} %get-tuple-element.76), channel_id=1, source_target_pairs={{0,3},{1,2},{2,1},{3,0},{4,7},{5,6},{6,5},{7,4},{8,11},{9,10},{10,... | collective-permute-start | bytes 24584 | tf_op jit(solution)/shard_map/ppermute | solution.py:274
  7.5 1.0 %multiply_add_fusion = (f32[1,128,128]{2,1,0:T(8,128)S(1)}, f32[1,128,128]{2,1,0:T(8,128)S(1)}, f32[1,128,128]{2,1,0:T(8,128)S(1)}, f32[1,128,128]{2,1,0:T(8,128)S(1)}) fusion(f32[8,128,128]{2,1,0:T(8,128)} %refs_4_.1, f32[8,128,128]{2,1,0:T(8,128)} %refs_3_.1), kind=kLoop, calls=%fused_computation.5 | loop fusion | flops 65536 | bytes 655360 | tf_op jit(solution)/shard_map/add | solution.py:305
  8.5 1.7 %collective-permute-start.1 = (f32[2,128,128]{2,1,0:T(8,128)S(1)}, f32[2,128,128]{2,1,0:T(8,128)S(1)}, u32[]{:S(2)}, u32[]{:S(2)}) collective-permute-start(f32[2,128,128]{2,1,0:T(8,128)S(1)} %get-tuple-element.74), channel_id=1, source_target_pairs={{0,28},{4,8},{8,4},{12,16},{16,12},{20,24},{24,20},{28,0},{1,29},{... | collective-permute-start | bytes 393224 | tf_op jit(solution)/shard_map/ppermute | solution.py:272
  10.2 1.6 %copy-done.3 = f32[64,8,8,128]{3,2,1,0:T(8,128)S(1)} copy-done((f32[64,8,8,128]{3,2,1,0:T(8,128)S(1)}, f32[64,8,8,128]{3,2,1,0:T(8,128)}, u32[]{:S(2)}) %copy-start.3) | copy-done | bytes 2097176
  11.8 1.2 %copy-done.4 = bf16[64,8,8,128]{3,2,1,0:T(8,128)(2,1)S(1)} copy-done((bf16[64,8,8,128]{3,2,1,0:T(8,128)(2,1)S(1)}, bf16[64,8,8,128]{3,2,1,0:T(8,128)(2,1)}, u32[]{:S(2)}) %copy-start.4) | copy-done | bytes 1048600
  13.0 1.0 %copy-done.5 = f32[8,128,128]{2,1,0:T(8,128)S(1)} copy-done((f32[8,128,128]{2,1,0:T(8,128)S(1)}, f32[8,128,128]{2,1,0:T(8,128)}, u32[]{:S(2)}) %copy-start.5) | copy-done | bytes 524312
  14.1 1.0 %copy-done.6 = f32[8,128,128]{2,1,0:T(8,128)S(1)} copy-done((f32[8,128,128]{2,1,0:T(8,128)S(1)}, f32[8,128,128]{2,1,0:T(8,128)}, u32[]{:S(2)}) %copy-start.6) | copy-done | bytes 524312
  15.1 0.8 %copy-done.8 = s32[8,8,128]{2,1,0:T(8,128)S(1)} copy-done((s32[8,8,128]{2,1,0:T(8,128)S(1)}, s32[8,8,128]{2,1,0:T(8,128)}, u32[]{:S(2)}) %copy-start.8) | copy-done | bytes 32792
  15.9 0.7 %copy-done.9 = f32[128]{0:T(128)S(1)} copy-done((f32[128]{0:T(128)S(1)}, f32[128]{0:T(128)}, u32[]{:S(2)}) %copy-start.9) | copy-done | bytes 536
  16.5 5.3 %condense.1 = (f32[8,128,128]{2,1,0:T(8,128)}, f32[8,128,128]{2,1,0:T(8,128)}, f32[64,8,8,128]{3,2,1,0:T(8,128)}, f32[2,128]{1,0:T(2,128)S(1)}, f32[128,128]{1,0:T(8,128)S(1)}) custom-call(f32[1,128]{1,0:T(1,128)S(1)} %bitcast.16, f32[8,128,128]{2,1,0:T(8,128)S(1)} %copy-done.5, f32[8,128,128]{2,1,0:T(8,128)S(1)} %copy-done.6, ...), custom_call_target="tpu_custom_call" | custom-call | flops 4000000000 | bytes 8000000 | tf_op jit(solution)/shard_map/condense/pallas_call | solution.py:117
  21.9 1.0 %copy-done.10 = f32[8,128,128]{2,1,0:T(8,128)S(1)} copy-done((f32[8,128,128]{2,1,0:T(8,128)S(1)}, f32[8,128,128]{2,1,0:T(8,128)}, u32[]{:S(2)}) %copy-start.10) | copy-done | bytes 524312
  23.0 1.3 %substep0.1 = (f32[8,128,128]{2,1,0:T(8,128)S(1)}, f32[8,128,128]{2,1,0:T(8,128)S(1)}, f32[8,128,128]{2,1,0:T(8,128)S(1)}, f32[8,128,128]{2,1,0:T(8,128)S(1)}, f...) custom-call(f32[1,128]{1,0:T(1,128)S(1)} %bitcast.17, ...), custom_call_target="tpu_custom_call" | custom-call | flops 1000000000 | bytes 6000000 | tf_op jit(solution)/shard_map/substep0/pallas_call | solution.py:242
  24.2 0.6 %collective-permute-start.4 = (f32[2,128,128]{2,1,0:T(8,128)S(1)}, f32[2,128,128]{2,1,0:T(8,128)S(1)}, u32[]{:S(2)}, u32[]{:S(2)}) collective-permute-start(f32[2,128,128]{2,1,0:T(8,128)S(1)} %get-tuple-element.43), channel_id=1, source_target_pairs={{0,4},{4,0},{8,12},{12,8},{16,20},{20,16},{24,28},{28,24},{1,5},{5... | collective-permute-start | bytes 393224 | tf_op jit(solution)/shard_map/ppermute | solution.py:271
  24.8 1.0 %collective-permute-start.5 = (f32[2,128,128]{2,1,0:T(8,128)S(1)}, f32[2,128,128]{2,1,0:T(8,128)S(1)}, u32[]{:S(2)}, u32[]{:S(2)}) collective-permute-start(f32[2,128,128]{2,1,0:T(8,128)S(1)} %get-tuple-element.44), channel_id=1, source_target_pairs={{0,28},{4,8},{8,4},{12,16},{16,12},{20,24},{24,20},{28,0},{1,29},{... | collective-permute-start | bytes 393224 | tf_op jit(solution)/shard_map/ppermute | solution.py:272
  25.8 2.0 %collective-permute-start.6 = (f32[2,8,128]{2,1,0:T(8,128)S(1)}, f32[2,8,128]{2,1,0:T(8,128)S(1)}, u32[]{:S(2)}, u32[]{:S(2)}) collective-permute-start(f32[2,8,128]{2,1,0:T(8,128)S(1)} %get-tuple-element.45), channel_id=1, source_target_pairs={{0,1},{1,0},{2,3},{3,2},{4,5},{5,4},{6,7},{7,6},{8,9},{9,8},{10,11... | collective-permute-start | bytes 24584 | tf_op jit(solution)/shard_map/ppermute | solution.py:273
  27.9 1.5 %collective-permute-done.6.refs_10_ = f32[2,8,128]{2,1,0:T(8,128)S(1)} collective-permute-done((f32[2,8,128]{2,1,0:T(8,128)S(1)}, f32[2,8,128]{2,1,0:T(8,128)S(1)}, u32[]{:S(2)}, u32[]{:S(2)}) %collective-permute-start.6) | collective-permute-done | bytes 8224 | tf_op jit(solution)/shard_map/ppermute | solution.py:273
  29.5 3.8 %collective-permute-done.7.refs_11_ = f32[2,8,128]{2,1,0:T(8,128)S(1)} collective-permute-done((f32[2,8,128]{2,1,0:T(8,128)S(1)}, f32[2,8,128]{2,1,0:T(8,128)S(1)}, u32[]{:S(2)}, u32[]{:S(2)}) %collective-permute-start.7) | collective-permute-done | bytes 8224 | tf_op jit(solution)/shard_map/ppermute | solution.py:274
  33.3 1.2 %substep1.1 = (f32[8,128,128]{2,1,0:T(8,128)S(1)}, f32[8,128,128]{2,1,0:T(8,128)S(1)}, f32[8,128,128]{2,1,0:T(8,128)S(1)}, f32[8,128,128]{2,1,0:T(8,128)S(1)}, f...) custom-call(f32[1,128]{1,0:T(1,128)S(1)} %bitcast.18, ...), custom_call_target="tpu_custom_call" | custom-call | flops 1000000000 | bytes 6000000 | tf_op jit(solution)/shard_map/substep1/pallas_call | solution.py:242
  34.6 1.6 %collective-permute-start.9 = (f32[2,128,128]{2,1,0:T(8,128)S(1)}, f32[2,128,128]{2,1,0:T(8,128)S(1)}, u32[]{:S(2)}, u32[]{:S(2)}) collective-permute-start(f32[2,128,128]{2,1,0:T(8,128)S(1)} %get-tuple-element.53), channel_id=1, source_target_pairs={{0,28},{4,8},{8,4},{12,16},{16,12},{20,24},{24,20},{28,0},{1,29},{... | collective-permute-start | bytes 393224 | tf_op jit(solution)/shard_map/ppermute | solution.py:272
  36.2 0.2 collective-permute-start.11
  36.5 1.2 %collective-permute-done.12 = f32[2,128]{1,0:T(2,128)S(1)} collective-permute-done((f32[2,128]{1,0:T(2,128)S(1)}, f32[2,128]{1,0:T(2,128)S(1)}, u32[]{:S(2)}, u32[]{:S(2)}) %collective-permute-start.12) | collective-permute-done | bytes 1056 | tf_op jit(solution)/shard_map/ppermute | solution.py:283
  37.6 1.0 %collective-permute-start.13 = (f32[2,128]{1,0:T(2,128)S(1)}, f32[2,128]{1,0:T(2,128)S(1)}, u32[]{:S(2)}, u32[]{:S(2)}) collective-permute-start(f32[2,128]{1,0:T(2,128)S(1)} %add.44), channel_id=1, source_target_pairs={{0,8},{4,12},{8,0},{12,4},{16,24},{20,28},{24,16},{28,20},{1,9},{5... | collective-permute-start | bytes 3080 | tf_op jit(solution)/shard_map/ppermute | solution.py:283
  38.6 2.6 %collective-permute-done.13 = f32[2,128]{1,0:T(2,128)S(1)} collective-permute-done((f32[2,128]{1,0:T(2,128)S(1)}, f32[2,128]{1,0:T(2,128)S(1)}, u32[]{:S(2)}, u32[]{:S(2)}) %collective-permute-start.13) | collective-permute-done | bytes 1056 | tf_op jit(solution)/shard_map/ppermute | solution.py:283
  41.2 0.7 %collective-permute-start.14 = (f32[2,128]{1,0:T(2,128)S(1)}, f32[2,128]{1,0:T(2,128)S(1)}, u32[]{:S(2)}, u32[]{:S(2)}) collective-permute-start(f32[2,128]{1,0:T(2,128)S(1)} %add.45), channel_id=1, source_target_pairs={{0,16},{4,20},{8,24},{12,28},{16,0},{20,4},{24,8},{28,12},{1,17},{... | collective-permute-start | bytes 3080 | tf_op jit(solution)/shard_map/ppermute | solution.py:283
  41.9 2.8 %collective-permute-done.14 = f32[2,128]{1,0:T(2,128)S(1)} collective-permute-done((f32[2,128]{1,0:T(2,128)S(1)}, f32[2,128]{1,0:T(2,128)S(1)}, u32[]{:S(2)}, u32[]{:S(2)}) %collective-permute-start.14) | collective-permute-done | bytes 1056 | tf_op jit(solution)/shard_map/ppermute | solution.py:283
  44.8 1.8 %collective-permute-start.15 = (f32[2,128]{1,0:T(2,128)S(1)}, f32[2,128]{1,0:T(2,128)S(1)}, u32[]{:S(2)}, u32[]{:S(2)}) collective-permute-start(f32[2,128]{1,0:T(2,128)S(1)} %add.46), channel_id=1, source_target_pairs={{0,1},{1,0},{2,3},{3,2},{4,5},{5,4},{6,7},{7,6},{8,9},{9,8},{10,11... | collective-permute-start | bytes 3080 | tf_op jit(solution)/shard_map/ppermute | solution.py:283
  46.6 1.8 %collective-permute-done.15 = f32[2,128]{1,0:T(2,128)S(1)} collective-permute-done((f32[2,128]{1,0:T(2,128)S(1)}, f32[2,128]{1,0:T(2,128)S(1)}, u32[]{:S(2)}, u32[]{:S(2)}) %collective-permute-start.15) | collective-permute-done | bytes 1056 | tf_op jit(solution)/shard_map/ppermute | solution.py:283
  48.4 3.3 %collective-permute-start.16 = (f32[2,128]{1,0:T(2,128)S(1)}, f32[2,128]{1,0:T(2,128)S(1)}, u32[]{:S(2)}, u32[]{:S(2)}) collective-permute-start(f32[2,128]{1,0:T(2,128)S(1)} %add.47), channel_id=1, source_target_pairs={{0,2},{1,3},{2,0},{3,1},{4,6},{5,7},{6,4},{7,5},{8,10},{9,11},{10,... | collective-permute-start | bytes 3080 | tf_op jit(solution)/shard_map/ppermute | solution.py:283
  51.6 1.6 %collective-permute-done.16 = f32[2,128]{1,0:T(2,128)S(1)} collective-permute-done((f32[2,128]{1,0:T(2,128)S(1)}, f32[2,128]{1,0:T(2,128)S(1)}, u32[]{:S(2)}, u32[]{:S(2)}) %collective-permute-start.16) | collective-permute-done | bytes 1056 | tf_op jit(solution)/shard_map/ppermute | solution.py:283
  53.2 2.8 %substep2.1 = (f32[8,128,128]{2,1,0:T(8,128)}, f32[8,128,128]{2,1,0:T(8,128)}, f32[8,128,128]{2,1,0:T(8,128)}, f32[8,128,128]{2,1,0:T(8,128)}, f32[1,128]{1,0:T(1,128)}) custom-call(f32[1,128]{1,0:T(1,128)S(1)} %bitcast.19, f32[128,128]{1,0:T(8,128)S(1)} %get-tuple-element.36.refs_1_, f32[8,128,128]{2,1,0:T(8,128)S(1)} %copy-done.10, ...), custom_call_target="tpu_custom_call" | custom-call | flops 1000000000 | bytes 6000000 | tf_op jit(solution)/shard_map/substep2/pallas_call | solution.py:242
  (39 shorter events, 0.3 us)
Async XLA Ops:
  2.3 19.6 %collective-permute-start.3 = (f32[2,8,128]{2,1,0:T(8,128)S(1)}, f32[2,8,128]{2,1,0:T(8,128)S(1)}, u32[]{:S(2)}, u32[]{:S(2)}) collective-permute-start(f32[2,8,128]{2,1,0:T(8,128)S(1)} %get-tuple-element.76), channel_id=1, source_target_pairs={{0,3},{1,2},{2,1},{3,0},{4,7},{5,6},{6,5},{7,4},{8,11},{9,10},{10,... | collective-permute-start | bytes 24584 | tf_op jit(solution)/shard_map/ppermute | solution.py:274
  7.5 14.4 %collective-permute-start.2 = (f32[2,8,128]{2,1,0:T(8,128)S(1)}, f32[2,8,128]{2,1,0:T(8,128)S(1)}, u32[]{:S(2)}, u32[]{:S(2)}) collective-permute-start(f32[2,8,128]{2,1,0:T(8,128)S(1)} %get-tuple-element.77), channel_id=1, source_target_pairs={{0,1},{1,0},{2,3},{3,2},{4,5},{5,4},{6,7},{7,6},{8,9},{9,8},{10,11... | collective-permute-start | bytes 24584 | tf_op jit(solution)/shard_map/ppermute | solution.py:273
  8.5 13.4 %collective-permute-start.1 = (f32[2,128,128]{2,1,0:T(8,128)S(1)}, f32[2,128,128]{2,1,0:T(8,128)S(1)}, u32[]{:S(2)}, u32[]{:S(2)}) collective-permute-start(f32[2,128,128]{2,1,0:T(8,128)S(1)} %get-tuple-element.74), channel_id=1, source_target_pairs={{0,28},{4,8},{8,4},{12,16},{16,12},{20,24},{24,20},{28,0},{1,29},{... | collective-permute-start | bytes 393224 | tf_op jit(solution)/shard_map/ppermute | solution.py:272
  10.2 11.7 %collective-permute-start = (f32[2,128,128]{2,1,0:T(8,128)S(1)}, f32[2,128,128]{2,1,0:T(8,128)S(1)}, u32[]{:S(2)}, u32[]{:S(2)}) collective-permute-start(f32[2,128,128]{2,1,0:T(8,128)S(1)} %get-tuple-element.75), channel_id=1, source_target_pairs={{0,4},{4,0},{8,12},{12,8},{16,20},{20,16},{24,28},{28,24},{1,5},{5... | collective-permute-start | bytes 393224 | tf_op jit(solution)/shard_map/ppermute | solution.py:271
  10.2 1.6 %copy-start.3 = (f32[64,8,8,128]{3,2,1,0:T(8,128)S(1)}, f32[64,8,8,128]{3,2,1,0:T(8,128)}, u32[]{:S(2)}) copy-start(f32[64,8,8,128]{3,2,1,0:T(8,128)} %radius_ref.1) | copy-start | bytes 6291460
  11.8 1.2 %copy-start.4 = (bf16[64,8,8,128]{3,2,1,0:T(8,128)(2,1)S(1)}, bf16[64,8,8,128]{3,2,1,0:T(8,128)(2,1)}, u32[]{:S(2)}) copy-start(bf16[64,8,8,128]{3,2,1,0:T(8,128)(2,1)} %mult_ref.1) | copy-start | bytes 3145732
  13.0 1.0 %copy-start.5 = (f32[8,128,128]{2,1,0:T(8,128)S(1)}, f32[8,128,128]{2,1,0:T(8,128)}, u32[]{:S(2)}) copy-start(f32[8,128,128]{2,1,0:T(8,128)} %theta_ref.1) | copy-start | bytes 1572868
  14.0 1.0 %copy-start.6 = (f32[8,128,128]{2,1,0:T(8,128)S(1)}, f32[8,128,128]{2,1,0:T(8,128)}, u32[]{:S(2)}) copy-start(f32[8,128,128]{2,1,0:T(8,128)} %humidity_ref.1) | copy-start | bytes 1572868
  15.1 0.8 %copy-start.8 = (s32[8,8,128]{2,1,0:T(8,128)S(1)}, s32[8,8,128]{2,1,0:T(8,128)}, u32[]{:S(2)}) copy-start(s32[8,8,128]{2,1,0:T(8,128)} %count_ref.1) | copy-start | bytes 98308
  15.8 0.7 %copy-start.9 = (f32[128]{0:T(128)S(1)}, f32[128]{0:T(128)}, u32[]{:S(2)}) copy-start(f32[128]{0:T(128)} %param.16) | copy-start | bytes 1540
  16.5 5.4 %copy-start = (f32[8,128,128]{2,1,0:T(8,128)S(1)}, f32[8,128,128]{2,1,0:T(8,128)}, u32[]{:S(2)}) copy-start(f32[8,128,128]{2,1,0:T(8,128)} %refs_3_.1) | copy-start | bytes 1572868
  16.5 5.4 %copy-start.1 = (f32[8,128,128]{2,1,0:T(8,128)S(1)}, f32[8,128,128]{2,1,0:T(8,128)}, u32[]{:S(2)}) copy-start(f32[8,128,128]{2,1,0:T(8,128)} %refs_4_.1) | copy-start | bytes 1572868
  16.5 5.4 %copy-start.2 = (f32[8,128,128]{2,1,0:T(8,128)S(1)}, f32[8,128,128]{2,1,0:T(8,128)}, u32[]{:S(2)}) copy-start(f32[8,128,128]{2,1,0:T(8,128)} %refs_5_.1) | copy-start | bytes 1572868
  16.5 5.4 %copy-start.7 = (f32[8,128,128]{2,1,0:T(8,128)S(1)}, f32[8,128,128]{2,1,0:T(8,128)}, u32[]{:S(2)}) copy-start(f32[8,128,128]{2,1,0:T(8,128)} %refs_6_.1) | copy-start | bytes 1572868
  21.9 1.0 %copy-start.10 = (f32[8,128,128]{2,1,0:T(8,128)S(1)}, f32[8,128,128]{2,1,0:T(8,128)}, u32[]{:S(2)}) copy-start(f32[8,128,128]{2,1,0:T(8,128)} %get-tuple-element.32.refs_2_) | copy-start | bytes 1572868
  24.2 9.1 %collective-permute-start.4 = (f32[2,128,128]{2,1,0:T(8,128)S(1)}, f32[2,128,128]{2,1,0:T(8,128)S(1)}, u32[]{:S(2)}, u32[]{:S(2)}) collective-permute-start(f32[2,128,128]{2,1,0:T(8,128)S(1)} %get-tuple-element.43), channel_id=1, source_target_pairs={{0,4},{4,0},{8,12},{12,8},{16,20},{20,16},{24,28},{28,24},{1,5},{5... | collective-permute-start | bytes 393224 | tf_op jit(solution)/shard_map/ppermute | solution.py:271
  24.8 8.5 %collective-permute-start.5 = (f32[2,128,128]{2,1,0:T(8,128)S(1)}, f32[2,128,128]{2,1,0:T(8,128)S(1)}, u32[]{:S(2)}, u32[]{:S(2)}) collective-permute-start(f32[2,128,128]{2,1,0:T(8,128)S(1)} %get-tuple-element.44), channel_id=1, source_target_pairs={{0,28},{4,8},{8,4},{12,16},{16,12},{20,24},{24,20},{28,0},{1,29},{... | collective-permute-start | bytes 393224 | tf_op jit(solution)/shard_map/ppermute | solution.py:272
  25.8 3.7 %collective-permute-start.6 = (f32[2,8,128]{2,1,0:T(8,128)S(1)}, f32[2,8,128]{2,1,0:T(8,128)S(1)}, u32[]{:S(2)}, u32[]{:S(2)}) collective-permute-start(f32[2,8,128]{2,1,0:T(8,128)S(1)} %get-tuple-element.45), channel_id=1, source_target_pairs={{0,1},{1,0},{2,3},{3,2},{4,5},{5,4},{6,7},{7,6},{8,9},{9,8},{10,11... | collective-permute-start | bytes 24584 | tf_op jit(solution)/shard_map/ppermute | solution.py:273
  27.9 5.4 %collective-permute-start.7 = (f32[2,8,128]{2,1,0:T(8,128)S(1)}, f32[2,8,128]{2,1,0:T(8,128)S(1)}, u32[]{:S(2)}, u32[]{:S(2)}) collective-permute-start(f32[2,8,128]{2,1,0:T(8,128)S(1)} %get-tuple-element.46), channel_id=1, source_target_pairs={{0,3},{1,2},{2,1},{3,0},{4,7},{5,6},{6,5},{7,4},{8,11},{9,10},{10,... | collective-permute-start | bytes 24584 | tf_op jit(solution)/shard_map/ppermute | solution.py:274
  34.5 18.7 %collective-permute-start.8 = (f32[2,128,128]{2,1,0:T(8,128)S(1)}, f32[2,128,128]{2,1,0:T(8,128)S(1)}, u32[]{:S(2)}, u32[]{:S(2)}) collective-permute-start(f32[2,128,128]{2,1,0:T(8,128)S(1)} %get-tuple-element.52), channel_id=1, source_target_pairs={{0,4},{4,0},{8,12},{12,8},{16,20},{20,16},{24,28},{28,24},{1,5},{5... | collective-permute-start | bytes 393224 | tf_op jit(solution)/shard_map/ppermute | solution.py:271
  34.6 18.6 %collective-permute-start.9 = (f32[2,128,128]{2,1,0:T(8,128)S(1)}, f32[2,128,128]{2,1,0:T(8,128)S(1)}, u32[]{:S(2)}, u32[]{:S(2)}) collective-permute-start(f32[2,128,128]{2,1,0:T(8,128)S(1)} %get-tuple-element.53), channel_id=1, source_target_pairs={{0,28},{4,8},{8,4},{12,16},{16,12},{20,24},{24,20},{28,0},{1,29},{... | collective-permute-start | bytes 393224 | tf_op jit(solution)/shard_map/ppermute | solution.py:272
  36.2 16.9 %collective-permute-start.10 = (f32[2,8,128]{2,1,0:T(8,128)S(1)}, f32[2,8,128]{2,1,0:T(8,128)S(1)}, u32[]{:S(2)}, u32[]{:S(2)}) collective-permute-start(f32[2,8,128]{2,1,0:T(8,128)S(1)} %get-tuple-element.54), channel_id=1, source_target_pairs={{0,1},{1,0},{2,3},{3,2},{4,5},{5,4},{6,7},{7,6},{8,9},{9,8},{10,11... | collective-permute-start | bytes 24584 | tf_op jit(solution)/shard_map/ppermute | solution.py:273
  36.2 16.9 %collective-permute-start.11 = (f32[2,8,128]{2,1,0:T(8,128)S(1)}, f32[2,8,128]{2,1,0:T(8,128)S(1)}, u32[]{:S(2)}, u32[]{:S(2)}) collective-permute-start(f32[2,8,128]{2,1,0:T(8,128)S(1)} %get-tuple-element.55), channel_id=1, source_target_pairs={{0,3},{1,2},{2,1},{3,0},{4,7},{5,6},{6,5},{7,4},{8,11},{9,10},{10,... | collective-permute-start | bytes 24584 | tf_op jit(solution)/shard_map/ppermute | solution.py:274
  36.5 1.2 %collective-permute-start.12 = (f32[2,128]{1,0:T(2,128)S(1)}, f32[2,128]{1,0:T(2,128)S(1)}, u32[]{:S(2)}, u32[]{:S(2)}) collective-permute-start(f32[2,128]{1,0:T(2,128)S(1)} %get-tuple-element.56), channel_id=1, source_target_pairs={{0,4},{4,0},{8,12},{12,8},{16,20},{20,16},{24,28},{28,24},{1,5},{5... | collective-permute-start | bytes 3080 | tf_op jit(solution)/shard_map/ppermute | solution.py:283
  37.6 3.6 %collective-permute-start.13 = (f32[2,128]{1,0:T(2,128)S(1)}, f32[2,128]{1,0:T(2,128)S(1)}, u32[]{:S(2)}, u32[]{:S(2)}) collective-permute-start(f32[2,128]{1,0:T(2,128)S(1)} %add.44), channel_id=1, source_target_pairs={{0,8},{4,12},{8,0},{12,4},{16,24},{20,28},{24,16},{28,20},{1,9},{5... | collective-permute-start | bytes 3080 | tf_op jit(solution)/shard_map/ppermute | solution.py:283
  41.2 3.6 %collective-permute-start.14 = (f32[2,128]{1,0:T(2,128)S(1)}, f32[2,128]{1,0:T(2,128)S(1)}, u32[]{:S(2)}, u32[]{:S(2)}) collective-permute-start(f32[2,128]{1,0:T(2,128)S(1)} %add.45), channel_id=1, source_target_pairs={{0,16},{4,20},{8,24},{12,28},{16,0},{20,4},{24,8},{28,12},{1,17},{... | collective-permute-start | bytes 3080 | tf_op jit(solution)/shard_map/ppermute | solution.py:283
  44.8 3.6 %collective-permute-start.15 = (f32[2,128]{1,0:T(2,128)S(1)}, f32[2,128]{1,0:T(2,128)S(1)}, u32[]{:S(2)}, u32[]{:S(2)}) collective-permute-start(f32[2,128]{1,0:T(2,128)S(1)} %add.46), channel_id=1, source_target_pairs={{0,1},{1,0},{2,3},{3,2},{4,5},{5,4},{6,7},{7,6},{8,9},{9,8},{10,11... | collective-permute-start | bytes 3080 | tf_op jit(solution)/shard_map/ppermute | solution.py:283
  48.4 4.8 %collective-permute-start.16 = (f32[2,128]{1,0:T(2,128)S(1)}, f32[2,128]{1,0:T(2,128)S(1)}, u32[]{:S(2)}, u32[]{:S(2)}) collective-permute-start(f32[2,128]{1,0:T(2,128)S(1)} %add.47), channel_id=1, source_target_pairs={{0,2},{1,3},{2,0},{3,1},{4,6},{5,7},{6,4},{7,5},{8,10},{9,11},{10,... | collective-permute-start | bytes 3080 | tf_op jit(solution)/shard_map/ppermute | solution.py:283

commit v2 on v1

v2 whole, which is shorter than its diff:
```python
import functools

import jax
import jax.numpy as jnp
from jax import lax
from jax.experimental import pallas as pl
from jax.experimental.pallas import tpu as pltpu
from jax.sharding import PartitionSpec as P

SUB = 3
BUOYANCY = 0.5
VAPOUR_SLOPE = 0.01
GROWTH_RATE = 25.0
RADIUS_FLOOR = 0.0625
MASS_FACTOR = 0.0004
LATENT_HEAT = 200.0
TERMS = 6
CHUNK = 8
GRANT = 24 * 1024 * 1024
PAD = 8
SIDE = 20
EXTRA = 56

VMEM = pl.BlockSpec(memory_space=pltpu.VMEM)


def exact_dot(a, b):
    return jnp.dot(a, b, precision=lax.Precision.HIGHEST, preferred_element_type=jnp.float32)


def power15(x):
    return x * x * lax.rsqrt(x)


def column_step(q, held, sound, inside, inverse):
    levels = q.shape[-1]
    source = inside * (held + q - pltpu.roll(q, levels - 1, 1))
    solved = exact_dot(source, inverse)
    masked = solved * inside
    return (q - sound * (masked - pltpu.roll(masked, 1, 1)), solved)


def interior(levels):
    level = lax.broadcasted_iota(jnp.int32, (1, levels), 1)
    return (level < levels - 1).astype(jnp.float32)


def even(axis):
    return lax.rem(lax.axis_index(axis), 2) == 0


def clear_rim(wide, rows, cols):
    shape = wide.shape
    for r in (0, 1, rows + 2, rows + 3):
        wide[r] = jnp.zeros(shape[1:], jnp.float32)
    for r in range(2, rows + 2):
        wide[r, 0:PAD, :] = jnp.zeros((PAD, shape[2]), jnp.float32)
        wide[r, PAD + cols :, :] = jnp.zeros((PAD, shape[2]), jnp.float32)


def bend(wide, r, cols):
    east = lambda n: wide[r, PAD + n : PAD + n + cols, :]
    up = wide[r + 2, PAD : PAD + cols, :]
    down = wide[r - 2, PAD : PAD + cols, :]
    return 0.25 * ((up + down) + (east(2) + east(-2))) - east(0)


def inverse_series(step, sound_ref, series, power):
    levels = series.shape[0]

    @pl.when(step == 0)
    def _():
        r = lax.broadcasted_iota(jnp.int32, (levels, levels), 0)
        k = lax.broadcasted_iota(jnp.int32, (levels, levels), 1)
        sound = jnp.broadcast_to(sound_ref[...], (levels, levels))
        upper = jnp.where((k == r + 1) & (k < levels - 1), -sound, 0.0)
        above = pltpu.roll(sound, levels - 1, 1)
        diagonal = jnp.where(k == r, jnp.where(k < levels - 1, 1.0 + sound + above, 1.0), 0.0)
        eye = jnp.where(k == r, 1.0, 0.0)
        residual = eye - (diagonal + upper + upper.T) * (1.0 / 3.0)
        series[...] = (eye + residual) * (1.0 / 3.0)
        power[...] = exact_dot(residual, residual)

    @pl.when((step > 0) & (step < TERMS))
    def _():
        old = series[...]
        series[...] = old + exact_dot(old, power[...])
        power[...] = exact_dot(power[...], power[...])


def first_kernel(
    axes,
    sound_hbm,
    theta_hbm,
    humidity_hbm,
    radius_hbm,
    mult_hbm,
    count_hbm,
    p_hbm,
    u_hbm,
    v_hbm,
    w_hbm,
    theta_final,
    humidity_final,
    radius_final,
    sums_out,
    series,
    p1_out,
    p2_out,
    p3_out,
    w3_out,
    drift_out,
    xa_out,
    xb_out,
    ya_out,
    yb_out,
    edge_out,
    cloud,
    total,
    power,
    wide,
    w2_out,
    d2_out,
    sound_ref,
    theta_ref,
    humidity_ref,
    radius_all,
    mult_all,
    count_ref,
    p_ref,
    u_ref,
    v_ref,
    w_ref,
    theta_out,
    humidity_out,
    radius_out,
    sems,
    chunk_sems,
):
    steps = radius_all.shape[0] // CHUNK
    rows, cols, levels = theta_ref.shape
    layers = count_ref.shape[0]
    lowest = levels // 4
    pairs = (
        (theta_hbm, theta_ref),
        (humidity_hbm, humidity_ref),
        (sound_hbm, sound_ref),
        (count_hbm, count_ref),
        (p_hbm, p_ref),
        (u_hbm, u_ref),
        (v_hbm, v_ref),
        (w_hbm, w_ref),
        (theta_out, theta_final),
        (humidity_out, humidity_final),
    )
    moves = [pltpu.make_async_copy(x, y, sems.at[n]) for n, (x, y) in enumerate(pairs)]

    def chunk_move(x, y, kind, step):
        span = pl.ds(step * CHUNK, CHUNK)
        return pltpu.make_async_copy(x.at[span], y.at[span], chunk_sems.at[kind, step])

    for move in moves[:4]:
        move.start()
    for step in range(steps):
        chunk_move(radius_hbm, radius_all, 0, step).start()
        chunk_move(mult_hbm, mult_all, 1, step).start()
    for move in moves[4:8]:
        move.start()
    for move in moves[:4]:
        move.wait()
    for i in range(rows):
        sat = humidity_ref[i] * jnp.exp(-VAPOUR_SLOPE * theta_ref[i]) - 1.0
        cloud[:, i, :] = GROWTH_RATE * sat.T[lowest : lowest + layers]
    total[...] = jnp.zeros_like(total)

    @pl.loop(0, steps)
    def _(step):
        chunk_move(radius_hbm, radius_all, 0, step).wait()
        chunk_move(mult_hbm, mult_all, 1, step).wait()
        inverse_series(step, sound_ref, series, power)
        for n in range(CHUNK):
            s = step * CHUNK + n
            live = s < count_ref[...]
            radius = radius_all[s]
            grown = jnp.maximum(radius + cloud[...], RADIUS_FLOOR)
            radius_out[s] = jnp.where(live, grown, 0.0)
            mass = mult_all[s].astype(jnp.float32) * (power15(grown) - power15(radius))
            total[...] += jnp.where(live, mass, 0.0)
        chunk_move(radius_out, radius_final, 2, step).start()

    if True:
        percent_sum = jnp.zeros((cols, levels), jnp.float32)
        theta_sum = jnp.zeros((cols, levels), jnp.float32)
        for i in range(rows):
            change = MASS_FACTOR * total[:, i, :]
            added = jnp.concatenate(
                [
                    jnp.zeros((lowest, cols), jnp.float32),
                    change,
                    jnp.zeros((levels - lowest - layers, cols), jnp.float32),
                ],
                axis=0,
            ).T
            humid = humidity_ref[i] - added
            warm = theta_ref[i] + LATENT_HEAT * added
            humidity_out[i] = humid
            theta_out[i] = warm
            percent_sum += 100.0 * (humid * jnp.exp(-VAPOUR_SLOPE * warm) - 1.0)
            theta_sum += warm
        sums_out[0:1] = jnp.sum(percent_sum, axis=0, keepdims=True)
        sums_out[1:2] = jnp.sum(theta_sum, axis=0, keepdims=True)

        for move in moves[8:]:
            move.start()
        for move in moves[4:8]:
            move.wait()
        sound = sound_ref[...]
        inside = interior(levels)
        inverse = series[...]
        clear_rim(wide, rows, cols)
        for i in range(rows):
            wide[i + 2, PAD : PAD + cols, :] = p_ref[i]
        j = lax.broadcasted_iota(jnp.int32, (cols, levels), 0)
        for i in range(rows):
            spread = jnp.zeros((cols, levels), jnp.float32)
            if i + 1 < rows:
                spread += u_ref[i + 1]
            if i > 0:
                spread -= u_ref[i - 1]
            v = v_ref[i]
            spread += jnp.where(j < cols - 1, pltpu.roll(v, cols - 1, 0), 0.0)
            spread -= jnp.where(j > 0, pltpu.roll(v, 1, 0), 0.0)
            d = 0.5 * spread - bend(wide, i + 2, cols)
            p1, w1 = column_step(
                p_ref[i] - sound * d,
                w_ref[i] + BUOYANCY * theta_out[i],
                sound,
                inside,
                inverse,
            )
            d2_out[i] = d
            p1_out[i] = p1
            w2_out[i] = w1
        for i in range(rows):
            wide[i + 2, PAD : PAD + cols, :] = p1_out[i]
        for i in range(rows):
            d = d2_out[i] - bend(wide, i + 2, cols)
            p2, w2 = column_step(
                p1_out[i] - sound * d,
                w2_out[i] + BUOYANCY * theta_out[i],
                sound,
                inside,
                inverse,
            )
            d2_out[i] = d
            p2_out[i] = p2
            w2_out[i] = w2

        for i in range(rows):
            wide[i + 2, PAD : PAD + cols, :] = p2_out[i]
        for i in range(rows):
            d = d2_out[i] - bend(wide, i + 2, cols)
            p3_out[i], w3_out[i] = column_step(
                p2_out[i] - sound * d,
                w2_out[i] + BUOYANCY * theta_out[i],
                sound,
                inside,
                inverse,
            )
        r = lax.broadcasted_iota(jnp.int32, (levels, levels), 0)
        k = lax.broadcasted_iota(jnp.int32, (levels, levels), 1)
        push = jnp.where(k == r, -BUOYANCY, 0.0)
        drift_p, drift_w = (jnp.zeros_like(push), jnp.zeros_like(push))
        for _ in range(SUB):
            drift_p, drift_w = column_step(drift_p, drift_w + push, sound, inside, inverse)
        drift_out[:, 0:levels] = drift_p
        drift_out[:, levels:] = drift_w

        even_x, even_y = (even(axes[0]), even(axes[1]))
        for k, field in enumerate((p_ref, p1_out, p2_out)):
            for n in range(2):
                if k > 0:
                    up, down = (field[rows - 2 + n], field[n])
                    xa_out[2 * k + n] = jnp.where(even_x, up, down)
                    xb_out[2 * k + n] = jnp.where(even_x, down, up)
                up, down = (field[:, cols - 2 + n, :], field[:, n, :])
                ya_out[2 * k + n] = jnp.where(even_y, up, down)
                yb_out[2 * k + n] = jnp.where(even_y, down, up)
        up, down = (p_ref[rows - 2] + 2.0 * u_ref[rows - 1], p_ref[1] - 2.0 * u_ref[0])
        xa_out[0] = jnp.where(even_x, up, p_ref[0])
        xa_out[1] = jnp.where(even_x, p_ref[rows - 1], down)
        xb_out[0] = jnp.where(even_x, p_ref[0], up)
        xb_out[1] = jnp.where(even_x, down, p_ref[rows - 1])
        up, down = (v_ref[:, cols - 1, :], v_ref[:, 0, :])
        ya_out[6] = jnp.where(even_y, up, down)
        yb_out[6] = jnp.where(even_y, down, up)
        for m, i in enumerate((0, rows - 1)):
            up, down = (u_ref[i, cols - 2 : cols, :], u_ref[i, 0:2, :])
            ya_out[7, 2 * m : 2 * m + 2, :] = jnp.where(even_y, up, down)
            yb_out[7, 2 * m : 2 * m + 2, :] = jnp.where(even_y, down, up)
        far_up, far_down = ([], [])
        for side, c in ((far_up, cols - 4), (far_down, 2)):
            for n in range(2):
                line = lambda ref, i: ref[i, c + n : c + n + 1, :]
                side += [line(p_ref, 0), line(p_ref, 1) - 2.0 * line(u_ref, 0)]
            for n in range(2):
                line = lambda ref, i: ref[i, c + n : c + n + 1, :]
                side += [
                    line(p_ref, rows - 2) + 2.0 * line(u_ref, rows - 1),
                    line(p_ref, rows - 1),
                ]
        up, down = (jnp.concatenate(far_up, axis=0), jnp.concatenate(far_down, axis=0))
        ya_out[8, 0:8, :] = jnp.where(even_y, up, down)
        yb_out[8, 0:8, :] = jnp.where(even_y, down, up)
        for out in (ya_out, yb_out):
            out[7, 4:, :] = jnp.zeros((rows - 4, levels), jnp.float32)
            out[9] = jnp.zeros((rows, levels), jnp.float32)
            out[9, 0:2, :] = sums_out[...]
        for m, i in enumerate((0, rows - 2)):
            for n in range(2):
                edge_out[4 * m + n : 4 * m + n + 1, :] = v_ref[i + n, 0:1, :]
                edge_out[4 * m + 2 + n : 4 * m + 3 + n, :] = v_ref[i + n, cols - 1 : cols, :]
        for m, i in enumerate((1, rows - 2)):
            edge_out[8 + 4 * m : 10 + 4 * m, :] = p_ref[i, 0:2, :]
            edge_out[10 + 4 * m : 12 + 4 * m, :] = p_ref[i, cols - 2 : cols, :]
        for step in range(steps):
            chunk_move(radius_out, radius_final, 2, step).wait()
        for move in moves[8:]:
            move.wait()


def first(sound, theta, humidity, radius_sq, multiplicity, count, p, u, v, w):
    slots = radius_sq.shape[0]
    rows, cols, levels = theta.shape
    hbm = pl.BlockSpec(memory_space=pltpu.HBM)
    f32 = lambda *shape: jax.ShapeDtypeStruct(shape, jnp.float32)
    block = f32(*theta.shape)
    outs = (
        [block, block, f32(*radius_sq.shape), f32(2, levels), f32(levels, levels)]
        + [block] * 4
        + [f32(levels, 2 * levels)]
        + [f32(6, cols, levels)] * 2
        + [f32(10, rows, levels)] * 2
        + [f32(16, levels)]
    )
    local_block = pltpu.VMEM(theta.shape, jnp.float32)
    layer_block = pltpu.VMEM(radius_sq.shape[1:], jnp.float32)
    return pl.pallas_call(
        functools.partial(first_kernel, ("gx", "gy")),
        in_specs=[hbm] * 10,
        out_specs=[hbm] * 3 + [VMEM] * 12,
        out_shape=outs,
        scratch_shapes=[
            layer_block,
            layer_block,
            pltpu.VMEM((levels, levels), jnp.float32),
            pltpu.VMEM((rows + 4, cols + 2 * PAD, levels), jnp.float32),
            local_block,
            local_block,
            pltpu.VMEM(sound.shape, jnp.float32),
            local_block,
            local_block,
            pltpu.VMEM(radius_sq.shape, jnp.float32),
            pltpu.VMEM(multiplicity.shape, multiplicity.dtype),
            pltpu.VMEM(count.shape, count.dtype),
        ]
        + [local_block] * 6
        + [
            pltpu.VMEM(radius_sq.shape, jnp.float32),
            pltpu.SemaphoreType.DMA((10,)),
            pltpu.SemaphoreType.DMA((3, slots // CHUNK)),
        ],
        compiler_params=pltpu.CompilerParams(vmem_limit_bytes=GRANT),
        cost_estimate=pl.CostEstimate(
            flops=8_000_000_000, bytes_accessed=12_000_000, transcendentals=1_000_000
        ),
        name="condense_and_evolve",
    )(sound, theta, humidity, radius_sq, multiplicity, count, p, u, v, w)


def corner_kernel(axes, ya_ref, yb_ref, edge_ref, sums_ref, a_out, b_out, sums_out):
    even_x, even_y = (even(axes[0]), even(axes[1]))
    rows = ya_ref.shape[1]
    levels = ya_ref.shape[2]
    low = jnp.where(even_y, yb_ref[...], ya_ref[...])
    high = jnp.where(even_y, ya_ref[...], yb_ref[...])

    def put(at, up, down):
        size = up.shape[0]
        a_out[at : at + size, :] = jnp.where(even_x, up, down)
        b_out[at : at + size, :] = jnp.where(even_x, down, up)

    for m, side in enumerate((low, high)):
        at = SIDE * m
        for n in range(4):
            put(at + 2 * n, side[n, rows - 2 : rows], side[n, 0:2])
        put(at + 8, side[7, 2:4], side[7, 0:2])
        put(at + 10, side[6, rows - 2 : rows], side[6, 0:2])
        inner = (side[0] + 2.0 * side[6], side[1]) if m == 0 else (side[0], side[1] - 2.0 * side[6])
        for n in range(2):
            put(at + 12 + 2 * n, inner[n][rows - 4 : rows - 2], inner[n][2:4])
        put(at + 16, side[8, 4:8], side[8, 0:4])
    put(2 * SIDE, edge_ref[4:8, :], edge_ref[0:4, :])
    put(2 * SIDE + 4, edge_ref[12:16, :], edge_ref[8:12, :])
    both = sums_ref[...] + ya_ref[9, 0:2, :]
    put(2 * SIDE + 8, both, both)
    sums_out[...] = both
    rest = jnp.zeros((EXTRA - 2 * SIDE - 10, levels), jnp.float32)
    put(2 * SIDE + 10, rest, rest)


def corner(ya, yb, edge, sums):
    levels = ya.shape[2]
    out = jax.ShapeDtypeStruct((EXTRA, levels), jnp.float32)
    return pl.pallas_call(
        functools.partial(corner_kernel, ("gx", "gy")),
        in_specs=[VMEM] * 4,
        out_specs=[VMEM] * 3,
        out_shape=[out, out, jax.ShapeDtypeStruct(sums.shape, jnp.float32)],
        compiler_params=pltpu.CompilerParams(vmem_limit_bytes=GRANT),
        cost_estimate=pl.CostEstimate(flops=10_000_000, bytes_accessed=100_000, transcendentals=0),
        name="corner",
    )(ya, yb, edge, sums)


def cross(mu, field, rows, cols):
    for r in range(rows + 4):
        if r < 2 or rows <= r < rows + 2:
            mu[r] = 0.25 * field[r + 2]
        elif r < 4 or r >= rows + 2:
            mu[r] = 0.25 * field[r - 2]
        else:
            mu[r] = jnp.zeros(mu.shape[1:], jnp.float32)
    for c in range(2):
        for base in (PAD, PAD + cols):
            mu[:, base - 2 + c, :] += 0.25 * field[:, base + c, :]
            mu[:, base + c, :] += 0.25 * field[:, base - 2 + c, :]


def last_kernel(
    axes,
    columns,
    sound_ref,
    inverse_ref,
    p0_ref,
    u_ref,
    v_ref,
    p1_ref,
    p2_ref,
    p3_ref,
    w3_ref,
    xa,
    xb,
    ya,
    yb,
    ca,
    cb,
    drift_ref,
    sums_ref,
    u_out,
    v_out,
    w_out,
    p_out,
    profile_out,
    f0,
    f1,
    f2,
    mu,
    yp,
    yw,
    yd,
    urows,
    vcols,
):
    rows, cols, levels = p0_ref.shape
    ext = cols + 2 * PAD
    even_x, even_y = (even(axes[0]), even(axes[1]))
    sound = sound_ref[...]
    inside = interior(levels)
    inverse = inverse_ref[...]
    body = slice(PAD, PAD + cols)
    low_y = jnp.where(even_y, yb[...], ya[...])
    high_y = jnp.where(even_y, ya[...], yb[...])
    low_c = jnp.where(even_x, cb[...], ca[...])
    high_c = jnp.where(even_x, ca[...], cb[...])
    pick = lambda one, two, n: jnp.where(even_x, one[n], two[n])
    sides = ((low_y, PAD - 2), (high_y, PAD + cols))
    ends = ((low_c, 0, xb, xa), (high_c, rows + 2, xa, xb))

    for r in range(rows + 4):
        for f in (f0, f1, f2):
            f[r, 0:PAD, :] = jnp.zeros((PAD, levels), jnp.float32)
            f[r, PAD + cols :, :] = jnp.zeros((PAD, levels), jnp.float32)
    for k, (f, ref) in enumerate(((f0, p0_ref), (f1, p1_ref), (f2, p2_ref))):
        for i in range(rows):
            f[i + 2, body, :] = ref[i]
        for _, at, one, two in ends:
            for n in range(2):
                f[at + n, body, :] = pick(one, two, 2 * k + n)
        for side, at in sides:
            for n in range(2):
                f[2 : rows + 2, at + n, :] = side[2 * k + n]
        if k < 2:
            for corner_rows, at, _, _ in ends:
                for m, (_, c) in enumerate(sides):
                    for n in range(2):
                        start = SIDE * m + 4 * k + 2 * n
                        for e in range(2):
                            f[at + e, c + n : c + n + 1, :] = corner_rows[start + e : start + e + 1]
    virtual = []
    for m, (c_rows, at, one, two) in enumerate(ends):
        outer = at + m
        virtual.append(f0[outer, body, :])
        for n, c in enumerate((PAD, PAD + cols - 2)):
            start = 2 * SIDE + 4 + 2 * n
            f0[outer, c : c + 2, :] = c_rows[start : start + 2]
    urows[...] = jnp.zeros_like(urows)
    for m, (c_rows, at, one, two) in enumerate(ends):
        outer, inner = ((0, 1), (3, 2))[m]
        urows[inner, body, :] = u_ref[0 if m == 0 else rows - 1]
        for s, (side, c) in enumerate(sides):
            urows[outer, c : c + 2, :] = c_rows[SIDE * s + 8 : SIDE * s + 10]
            urows[inner, c : c + 2, :] = side[7, 2 * m : 2 * m + 2]
    for s, (side, c) in enumerate(sides):
        outer, inner = ((0, 1), (3, 2))[s]
        vcols[outer, 2 : rows + 2, :] = side[6]
        vcols[inner, 2 : rows + 2, :] = v_ref[:, 0 if s == 0 else cols - 1, :]
        for c_rows, at, _, _ in ends:
            vcols[outer, at : at + 2, :] = c_rows[SIDE * s + 10 : SIDE * s + 12]
            vcols[inner, at : at + 2, :] = c_rows[2 * SIDE + 2 * s : 2 * SIDE + 2 * s + 2]

    cross(mu, f0, rows, cols)
    mu[2, body, :] += 0.25 * (virtual[0] - f0[0, body, :])
    mu[rows + 1, body, :] += 0.25 * (virtual[1] - f0[rows + 3, body, :])
    mu[1] -= 0.5 * urows[1]
    mu[2] += 0.5 * urows[0]
    mu[rows + 1] -= 0.5 * urows[3]
    mu[rows + 2] += 0.5 * urows[2]
    mu[:, PAD - 1, :] -= 0.5 * vcols[1]
    mu[:, PAD, :] += 0.5 * vcols[0]
    mu[:, PAD + cols - 1, :] -= 0.5 * vcols[3]
    mu[:, PAD + cols, :] += 0.5 * vcols[2]
    for c_rows, at, row in ((low_c, 0, 2), (high_c, rows + 2, rows)):
        for s, c in enumerate((PAD - 4, PAD + cols + 2)):
            for n in range(2):
                start = SIDE * s + 16 + 2 * n
                for e in range(2):
                    mu[row + e, c + n : c + n + 1, :] = 0.25 * c_rows[start + e : start + e + 1]
    far = 0.25 * jnp.concatenate(
        [c_rows[SIDE * s + 12 : SIDE * s + 16] for c_rows in (low_c, high_c) for s in range(2)],
        axis=0,
    )
    far, _ = column_step(sound * far, jnp.zeros_like(far), sound, inside, inverse)
    far = 0.25 * far

    for r in range(rows + 4):
        if 4 <= r < rows:
            spans = (slice(0, 2 * PAD), slice(cols, ext))
            clear = jnp.zeros((cols - 2 * PAD, levels), jnp.float32)
            for y in (yp, yw, yd):
                y[r, 2 * PAD : cols, :] = clear
        else:
            spans = (slice(0, ext),)
        for span in spans:
            d = -mu[r, span, :]
            q = -sound * d
            yp[r, span, :], yw[r, span, :] = column_step(
                q, jnp.zeros_like(q), sound, inside, inverse
            )
            yd[r, span, :] = d
    cross(mu, f1, rows, cols)
    for r in range(rows + 4):
        y = yp[r]
        near = pltpu.roll(y, 2, 0) + pltpu.roll(y, ext - 2, 0)
        if r >= 2:
            near += yp[r - 2]
        if r < rows + 2:
            near += yp[r + 2]
        mu[r] += 0.25 * near - y
        f0[r] += f1[r] + y
    for m, at in enumerate((0, rows + 2)):
        for s, c in enumerate((PAD, PAD + cols - 2)):
            for n in range(2):
                start = 8 * m + 4 * s + 2 * n
                for e in range(2):
                    mu[at + e, c + n : c + n + 1, :] += far[start + e : start + e + 1]
    for r in range(rows + 4):
        d = yd[r] - mu[r]
        p, w = column_step(yp[r] - sound * d, yw[r], sound, inside, inverse)
        yd[r] = d
        yp[r] = p
        yw[r] = w
        f0[r] += f2[r] + p
    cross(mu, f2, rows, cols)
    total = sums_ref[...] * (1.0 / columns)
    profile_out[...] = total[0:1]
    mean = jnp.broadcast_to(total[1:2], (8, levels))
    drift = exact_dot(mean, drift_ref[...])
    drift_p, drift_w = (drift[0:1, 0:levels], drift[0:1, levels:])
    for i in range(rows):
        r = i + 2
        d = yd[r, body, :] - mu[r, body, :] - bend(yp, r, cols)
        p, w = column_step(
            yp[r, body, :] - sound * d, yw[r, body, :], sound, inside, inverse
        )
        p_out[i] = p3_ref[i] + p + drift_p
        w_out[i] = w3_ref[i] + w + drift_w
        u_out[i] = u_ref[i] - 0.5 * (f0[r + 1, body, :] - f0[r - 1, body, :])
        east = lambda n: f0[r, PAD + n : PAD + n + cols, :]
        v_out[i] = v_ref[i] - 0.5 * (east(1) - east(-1))


def last(columns, *args):
    rows, cols, levels = args[2].shape
    f32 = lambda *shape: jax.ShapeDtypeStruct(shape, jnp.float32)
    block = f32(rows, cols, levels)
    wide = pltpu.VMEM((rows + 4, cols + 2 * PAD, levels), jnp.float32)
    return pl.pallas_call(
        functools.partial(last_kernel, ("gx", "gy"), columns),
        in_specs=[VMEM] * len(args),
        out_specs=[VMEM] * 5,
        out_shape=[block] * 4 + [f32(1, levels)],
        scratch_shapes=[wide] * 7
        + [
            pltpu.VMEM((4, cols + 2 * PAD, levels), jnp.float32),
            pltpu.VMEM((4, rows + 4, levels), jnp.float32),
        ],
        compiler_params=pltpu.CompilerParams(vmem_limit_bytes=GRANT),
        cost_estimate=pl.CostEstimate(
            flops=3_000_000_000, bytes_accessed=6_000_000, transcendentals=0
        ),
        name="response",
    )(*args)


def swaps(count):
    near = [(i, i ^ 1) for i in range(count)]
    far = [(i, (i + 1) % count if i % 2 else (i - 1) % count) for i in range(count)]
    return near, far


def exchange(a, b, axis):
    near, far = swaps(lax.axis_size(axis))
    return lax.ppermute(a, axis, near), lax.ppermute(b, axis, far)


def total_sum(value):
    for axis in ("gx", "gy"):
        count = lax.axis_size(axis)
        distance = 2
        while distance < count:
            value = value + lax.ppermute(value, axis, [(i, i ^ distance) for i in range(count)])
            distance *= 2
    return value


def local(
    eastward,
    northward,
    vertical,
    pressure,
    theta,
    humidity,
    sound_speed,
    radius_sq,
    multiplicity,
    droplet_count,
):
    columns = float(theta.shape[0] * theta.shape[1] * lax.axis_size("gx") * lax.axis_size("gy"))
    sound = sound_speed[None]
    (
        theta_out,
        humidity_out,
        radius_out,
        sums,
        inverse,
        p1,
        p2,
        p3,
        w3,
        drift,
        xa,
        xb,
        ya,
        yb,
        edge,
    ) = first(
        *(
            pltpu.with_memory_space_constraint(x, pltpu.HBM)
            for x in (
                sound,
                theta,
                humidity,
                radius_sq,
                multiplicity,
                droplet_count,
                pressure,
                eastward,
                northward,
                vertical,
            )
        )
    )
    xa, xb = exchange(xa, xb, "gx")
    ya, yb = exchange(ya, yb, "gy")
    ca, cb, sums = corner(ya, yb, edge, sums)
    ca, cb = exchange(ca, cb, "gx")
    at = 2 * SIDE + 8
    sums = total_sum(sums + ca[at : at + 2])
    u, v, w, p, profile = last(
        columns,
        sound,
        inverse,
        pressure,
        eastward,
        northward,
        p1,
        p2,
        p3,
        w3,
        xa,
        xb,
        ya,
        yb,
        ca,
        cb,
        drift,
        sums,
    )
    return (u, v, w, p, theta_out, humidity_out, radius_out, profile[0])


def solution(mesh):
    grid = P("gx", "gy", None)
    drops = P(None, None, "gx", "gy")
    return jax.shard_map(
        local,
        mesh=mesh,
        in_specs=(grid,) * 6 + (P(), drops, drops, P(None, "gx", "gy")),
        out_specs=(grid,) * 6 + (drops, P()),
        check_vma=False,
    )
```

time: 56.6 us -> 38.5 us (0.68)
  local copies, waits for them, and re-layouts: 9 us -> 0.02 us
  starting transfers between devices: 19.2 us -> 11.1 us
  Pallas kernels: 10.6 us -> 13.2 us
  waiting for transfers between devices: 15.3 us -> 13.3 us
  other arithmetic: 1.07 us -> 0.01 us
    unnamed x22 -> x8, local copies, waits for them, and re-layouts: 7.36 us -> 0.02 us
    ppermute x5 -> x3, starting transfers between devices: 6.75 us -> 2.24 us  [total_sum(): lax.ppermute(value, axis, [(i, i ^ distance) for i in range(count)])]
    ppermute x12 -> x6, starting transfers between devices: 12.5 us -> 8.86 us  [exchange(): return (lax.ppermute(a, axis, near), lax.ppermute(b, axis, far))]
    pallas_call x4 -> x3, Pallas kernels: 10.6 us -> 13.2 us  [the longest x1 8.42 us: first(): pl.pallas_call(functools.partial(first_kernel, ('gx', 'gy')), in_specs=[h...]
    slice x2 -> x0, local copies, waits for them, and re-layouts: 1.64 us -> none  [local(): up_y = jnp.stack([p[:, -2] + 2.0 * v[:, -1], p[:, -1]])]
    ppermute x12 -> x6, waiting for transfers between devices: 5.39 us -> 3.88 us  [exchange(): return (lax.ppermute(a, axis, near), lax.ppermute(b, axis, far))]
    add x1, other arithmetic: 1.02 us -> 0.01 us  [local(): sums = total_sum(sums + ca[at:at + 2])]
    ppermute x5 -> x3, waiting for transfers between devices: 9.94 us -> 9.38 us  [total_sum(): lax.ppermute(value, axis, [(i, i ^ distance) for i in range(count)])]
  transfers between devices with their start and end apart: 17 -> 9, of which waited for: 7 -> 5; matrix products, arithmetic and copies ran while one was open for 2% -> 0% of each run, Pallas kernels for 10% -> 0%
where the time goes in v2:
time: 38.5 us; the launch traced here: 38.3 us
  waiting for transfers between devices  13.3 us (35%)
  Pallas kernels  13.2 us (34%)
  starting transfers between devices  11.1 us (29%)
  between operations  0.74 us (2%)
    ppermute x3, waiting for transfers between devices, total_sum(): lax.ppermute(value, axis, [(i, i ^ distance) for i in range(count)])  9.38 us
    ppermute x6, starting transfers between devices, exchange(): return (lax.ppermute(a, axis, near), lax.ppermute(b, axis, far))  8.86 us
    pallas_call x1, Pallas kernels, first(): pl.pallas_call(functools.partial(first_kernel, ('gx', 'gy')), in_specs=[h...  8.42 us
    pallas_call x1, Pallas kernels, last(): pl.pallas_call(functools.partial(last_kernel, ('gx', 'gy'), columns), in_...  4.74 us
    ppermute x6, waiting for transfers between devices, exchange(): return (lax.ppermute(a, axis, near), lax.ppermute(b, axis, far))  3.88 us
    ppermute x3, starting transfers between devices, total_sum(): lax.ppermute(value, axis, [(i, i ^ distance) for i in range(count)])  2.24 us
  transfers between devices with their start and end apart: 9, of which 5 were waited for; matrix products, arithmetic and copies ran while one was open for 0% of the time, Pallas kernels for 0%

profile of v2, /device:TPU:0, one launch (start us, length us, event | category | flops | bytes accessed | tf_op | source)
XLA Modules:
  0.0 38.3 jit_solution(16845497774938930516)
XLA Ops:
  0.6 0.0 copy-start
  0.6 0.0 copy-start.1
  0.7 0.0 copy-start.2
  0.7 0.0 copy-start.3
  0.7 8.4 %condense_and_evolve.1 = (f32[8,128,128]{2,1,0:T(8,128)}, f32[8,128,128]{2,1,0:T(8,128)}, f32[64,8,8,128]{3,2,1,0:T(8,128)}, f32[2,128]{1,0:T(2,128)S(1)}, f32[1...) custom-call(f32[1,128]{1,0:T(1,128)} %bitcast.2, ...), custom_call_target="tpu_custom_call" | custom-call | flops 8000000000 | bytes 12000000 | tf_op jit(solution)/shard_map/condense_and_evolve/pallas_call | solution.py:348
  9.1 0.6 %collective-permute-start = (f32[6,128,128]{2,1,0:T(8,128)S(1)}, f32[6,128,128]{2,1,0:T(8,128)S(1)}, u32[]{:S(2)}, u32[]{:S(2)}) collective-permute-start(f32[6,128,128]{2,1,0:T(8,128)S(1)} %get-tuple-element.36), channel_id=1, source_target_pairs={{0,4},{4,0},{8,12},{12,8},{16,20},{20,16},{24,28},{28,24},{1,5},{5... | collective-permute-start | bytes 1179656 | tf_op jit(solution)/shard_map/ppermute | solution.py:644
  9.7 3.5 %collective-permute-start.1 = (f32[6,128,128]{2,1,0:T(8,128)S(1)}, f32[6,128,128]{2,1,0:T(8,128)S(1)}, u32[]{:S(2)}, u32[]{:S(2)}) collective-permute-start(f32[6,128,128]{2,1,0:T(8,128)S(1)} %get-tuple-element.37), channel_id=1, source_target_pairs={{0,28},{4,8},{8,4},{12,16},{16,12},{20,24},{24,20},{28,0},{1,29},{... | collective-permute-start | bytes 1179656 | tf_op jit(solution)/shard_map/ppermute | solution.py:644
  13.2 1.6 %collective-permute-start.2 = (f32[10,8,128]{2,1,0:T(8,128)S(1)}, f32[10,8,128]{2,1,0:T(8,128)S(1)}, u32[]{:S(2)}, u32[]{:S(2)}) collective-permute-start(f32[10,8,128]{2,1,0:T(8,128)S(1)} %get-tuple-element.38), channel_id=1, source_target_pairs={{0,1},{1,0},{2,3},{3,2},{4,5},{5,4},{6,7},{7,6},{8,9},{9,8},{10,11... | collective-permute-start | bytes 122888 | tf_op jit(solution)/shard_map/ppermute | solution.py:644
  14.8 2.5 %collective-permute-start.3 = (f32[10,8,128]{2,1,0:T(8,128)S(1)}, f32[10,8,128]{2,1,0:T(8,128)S(1)}, u32[]{:S(2)}, u32[]{:S(2)}) collective-permute-start(f32[10,8,128]{2,1,0:T(8,128)S(1)} %get-tuple-element.39), channel_id=1, source_target_pairs={{0,3},{1,2},{2,1},{3,0},{4,7},{5,6},{6,5},{7,4},{8,11},{9,10},{10,... | collective-permute-start | bytes 122888 | tf_op jit(solution)/shard_map/ppermute | solution.py:644
  17.3 0.0 collective-permute-done.2.ya_ref.ya
  17.3 3.3 %collective-permute-done.3.yb_ref.yb = f32[10,8,128]{2,1,0:T(8,128)S(1)} collective-permute-done((f32[10,8,128]{2,1,0:T(8,128)S(1)}, f32[10,8,128]{2,1,0:T(8,128)S(1)}, u32[]{:S(2)}, u32[]{:S(2)}) %collective-permute-start.3) | collective-permute-done | bytes 40992 | tf_op jit(solution)/shard_map/ppermute | solution.py:644
  20.6 0.1 collective-permute-start.4
  20.7 0.6 %collective-permute-start.5 = (f32[56,128]{1,0:T(8,128)S(1)}, f32[56,128]{1,0:T(8,128)S(1)}, u32[]{:S(2)}, u32[]{:S(2)}) collective-permute-start(f32[56,128]{1,0:T(8,128)S(1)} %get-tuple-element.43), channel_id=1, source_target_pairs={{0,28},{4,8},{8,4},{12,16},{16,12},{20,24},{24,20},{28,0},{1,29},{... | collective-permute-start | bytes 86024 | tf_op jit(solution)/shard_map/ppermute | solution.py:644
  21.3 0.5 %collective-permute-done.4.ca = f32[56,128]{1,0:T(8,128)S(1)} collective-permute-done((f32[56,128]{1,0:T(8,128)S(1)}, f32[56,128]{1,0:T(8,128)S(1)}, u32[]{:S(2)}, u32[]{:S(2)}) %collective-permute-start.4) | collective-permute-done | bytes 28704 | tf_op jit(solution)/shard_map/ppermute | solution.py:644
  21.9 0.9 %collective-permute-start.6 = (f32[2,128]{1,0:T(2,128)S(1)}, f32[2,128]{1,0:T(2,128)S(1)}, u32[]{:S(2)}, u32[]{:S(2)}) collective-permute-start(f32[2,128]{1,0:T(2,128)S(1)} %slice_add_fusion), channel_id=1, source_target_pairs={{0,8},{4,12},{8,0},{12,4},{16,24},{20,28},{24,16},{28,20},{1,9},{5... | collective-permute-start | bytes 3080 | tf_op jit(solution)/shard_map/ppermute | solution.py:652
  22.8 2.6 %collective-permute-done.6 = f32[2,128]{1,0:T(2,128)S(1)} collective-permute-done((f32[2,128]{1,0:T(2,128)S(1)}, f32[2,128]{1,0:T(2,128)S(1)}, u32[]{:S(2)}, u32[]{:S(2)}) %collective-permute-start.6) | collective-permute-done | bytes 1056 | tf_op jit(solution)/shard_map/ppermute | solution.py:652
  25.5 0.5 %collective-permute-start.7 = (f32[2,128]{1,0:T(2,128)S(1)}, f32[2,128]{1,0:T(2,128)S(1)}, u32[]{:S(2)}, u32[]{:S(2)}) collective-permute-start(f32[2,128]{1,0:T(2,128)S(1)} %add.13), channel_id=1, source_target_pairs={{0,16},{4,20},{8,24},{12,28},{16,0},{20,4},{24,8},{28,12},{1,17},{... | collective-permute-start | bytes 3080 | tf_op jit(solution)/shard_map/ppermute | solution.py:652
  26.0 3.1 %collective-permute-done.7 = f32[2,128]{1,0:T(2,128)S(1)} collective-permute-done((f32[2,128]{1,0:T(2,128)S(1)}, f32[2,128]{1,0:T(2,128)S(1)}, u32[]{:S(2)}, u32[]{:S(2)}) %collective-permute-start.7) | collective-permute-done | bytes 1056 | tf_op jit(solution)/shard_map/ppermute | solution.py:652
  29.0 0.8 %collective-permute-start.8 = (f32[2,128]{1,0:T(2,128)S(1)}, f32[2,128]{1,0:T(2,128)S(1)}, u32[]{:S(2)}, u32[]{:S(2)}) collective-permute-start(f32[2,128]{1,0:T(2,128)S(1)} %add.14), channel_id=1, source_target_pairs={{0,2},{1,3},{2,0},{3,1},{4,6},{5,7},{6,4},{7,5},{8,10},{9,11},{10,... | collective-permute-start | bytes 3080 | tf_op jit(solution)/shard_map/ppermute | solution.py:652
  29.8 3.7 %collective-permute-done.8 = f32[2,128]{1,0:T(2,128)S(1)} collective-permute-done((f32[2,128]{1,0:T(2,128)S(1)}, f32[2,128]{1,0:T(2,128)S(1)}, u32[]{:S(2)}, u32[]{:S(2)}) %collective-permute-start.8) | collective-permute-done | bytes 1056 | tf_op jit(solution)/shard_map/ppermute | solution.py:652
  33.5 0.0 collective-permute-done.5.cb
  33.5 0.0 collective-permute-done.xa
  33.5 0.0 collective-permute-done.1.xb
  33.5 0.0 copy-done
  33.5 0.0 copy-done.1
  33.6 0.0 copy-done.2
  33.6 0.0 copy-done.3
  33.6 4.7 %response.1 = (f32[8,128,128]{2,1,0:T(8,128)}, f32[8,128,128]{2,1,0:T(8,128)}, f32[8,128,128]{2,1,0:T(8,128)}, f32[8,128,128]{2,1,0:T(8,128)}, f32[1,128]{1,0:T(1,128)}) custom-call(f32[1,128]{1,0:T(1,128)S(1)} %bitcast.3, f32[128,128]{1,0:T(8,128)S(1)} %get-tuple-element.31.inverse_ref, f32[8,128,128]{2,1,0:T(8,128)S(1)} %copy-done, ...), custom_call_target="tpu_custom_call" | custom-call | flops 3000000000 | bytes 6000000 | tf_op jit(solution)/shard_map/response/pallas_call | solution.py:618
  (5 shorter events, 0.0 us)
Async XLA Ops:
  0.6 32.9 %copy-start = (f32[8,128,128]{2,1,0:T(8,128)S(1)}, f32[8,128,128]{2,1,0:T(8,128)}, u32[]{:S(2)}) copy-start(f32[8,128,128]{2,1,0:T(8,128)} %p0_ref.1) | copy-start | bytes 1572868
  0.6 32.9 %copy-start.1 = (f32[8,128,128]{2,1,0:T(8,128)S(1)}, f32[8,128,128]{2,1,0:T(8,128)}, u32[]{:S(2)}) copy-start(f32[8,128,128]{2,1,0:T(8,128)} %u_ref.1) | copy-start | bytes 1572868
  0.7 32.9 %copy-start.2 = (f32[8,128,128]{2,1,0:T(8,128)S(1)}, f32[8,128,128]{2,1,0:T(8,128)}, u32[]{:S(2)}) copy-start(f32[8,128,128]{2,1,0:T(8,128)} %v_ref.1) | copy-start | bytes 1572868
  0.7 32.9 %copy-start.3 = (f32[128]{0:T(128)S(1)}, f32[128]{0:T(128)}, u32[]{:S(2)}) copy-start(f32[128]{0:T(128)} %param.16) | copy-start | bytes 1540
  9.1 24.4 %collective-permute-start = (f32[6,128,128]{2,1,0:T(8,128)S(1)}, f32[6,128,128]{2,1,0:T(8,128)S(1)}, u32[]{:S(2)}, u32[]{:S(2)}) collective-permute-start(f32[6,128,128]{2,1,0:T(8,128)S(1)} %get-tuple-element.36), channel_id=1, source_target_pairs={{0,4},{4,0},{8,12},{12,8},{16,20},{20,16},{24,28},{28,24},{1,5},{5... | collective-permute-start | bytes 1179656 | tf_op jit(solution)/shard_map/ppermute | solution.py:644
  9.7 23.9 %collective-permute-start.1 = (f32[6,128,128]{2,1,0:T(8,128)S(1)}, f32[6,128,128]{2,1,0:T(8,128)S(1)}, u32[]{:S(2)}, u32[]{:S(2)}) collective-permute-start(f32[6,128,128]{2,1,0:T(8,128)S(1)} %get-tuple-element.37), channel_id=1, source_target_pairs={{0,28},{4,8},{8,4},{12,16},{16,12},{20,24},{24,20},{28,0},{1,29},{... | collective-permute-start | bytes 1179656 | tf_op jit(solution)/shard_map/ppermute | solution.py:644
  13.2 4.1 %collective-permute-start.2 = (f32[10,8,128]{2,1,0:T(8,128)S(1)}, f32[10,8,128]{2,1,0:T(8,128)S(1)}, u32[]{:S(2)}, u32[]{:S(2)}) collective-permute-start(f32[10,8,128]{2,1,0:T(8,128)S(1)} %get-tuple-element.38), channel_id=1, source_target_pairs={{0,1},{1,0},{2,3},{3,2},{4,5},{5,4},{6,7},{7,6},{8,9},{9,8},{10,11... | collective-permute-start | bytes 122888 | tf_op jit(solution)/shard_map/ppermute | solution.py:644
  14.8 5.8 %collective-permute-start.3 = (f32[10,8,128]{2,1,0:T(8,128)S(1)}, f32[10,8,128]{2,1,0:T(8,128)S(1)}, u32[]{:S(2)}, u32[]{:S(2)}) collective-permute-start(f32[10,8,128]{2,1,0:T(8,128)S(1)} %get-tuple-element.39), channel_id=1, source_target_pairs={{0,3},{1,2},{2,1},{3,0},{4,7},{5,6},{6,5},{7,4},{8,11},{9,10},{10,... | collective-permute-start | bytes 122888 | tf_op jit(solution)/shard_map/ppermute | solution.py:644
  20.6 1.3 %collective-permute-start.4 = (f32[56,128]{1,0:T(8,128)S(1)}, f32[56,128]{1,0:T(8,128)S(1)}, u32[]{:S(2)}, u32[]{:S(2)}) collective-permute-start(f32[56,128]{1,0:T(8,128)S(1)} %get-tuple-element.42), channel_id=1, source_target_pairs={{0,4},{4,0},{8,12},{12,8},{16,20},{20,16},{24,28},{28,24},{1,5},{5... | collective-permute-start | bytes 86024 | tf_op jit(solution)/shard_map/ppermute | solution.py:644
  20.7 12.8 %collective-permute-start.5 = (f32[56,128]{1,0:T(8,128)S(1)}, f32[56,128]{1,0:T(8,128)S(1)}, u32[]{:S(2)}, u32[]{:S(2)}) collective-permute-start(f32[56,128]{1,0:T(8,128)S(1)} %get-tuple-element.43), channel_id=1, source_target_pairs={{0,28},{4,8},{8,4},{12,16},{16,12},{20,24},{24,20},{28,0},{1,29},{... | collective-permute-start | bytes 86024 | tf_op jit(solution)/shard_map/ppermute | solution.py:644
  21.9 3.6 %collective-permute-start.6 = (f32[2,128]{1,0:T(2,128)S(1)}, f32[2,128]{1,0:T(2,128)S(1)}, u32[]{:S(2)}, u32[]{:S(2)}) collective-permute-start(f32[2,128]{1,0:T(2,128)S(1)} %slice_add_fusion), channel_id=1, source_target_pairs={{0,8},{4,12},{8,0},{12,4},{16,24},{20,28},{24,16},{28,20},{1,9},{5... | collective-permute-start | bytes 3080 | tf_op jit(solution)/shard_map/ppermute | solution.py:652
  25.5 3.6 %collective-permute-start.7 = (f32[2,128]{1,0:T(2,128)S(1)}, f32[2,128]{1,0:T(2,128)S(1)}, u32[]{:S(2)}, u32[]{:S(2)}) collective-permute-start(f32[2,128]{1,0:T(2,128)S(1)} %add.13), channel_id=1, source_target_pairs={{0,16},{4,20},{8,24},{12,28},{16,0},{20,4},{24,8},{28,12},{1,17},{... | collective-permute-start | bytes 3080 | tf_op jit(solution)/shard_map/ppermute | solution.py:652
  29.0 4.5 %collective-permute-start.8 = (f32[2,128]{1,0:T(2,128)S(1)}, f32[2,128]{1,0:T(2,128)S(1)}, u32[]{:S(2)}, u32[]{:S(2)}) collective-permute-start(f32[2,128]{1,0:T(2,128)S(1)} %add.14), channel_id=1, source_target_pairs={{0,2},{1,3},{2,0},{3,1},{4,6},{5,7},{6,4},{7,5},{8,10},{9,11},{10,... | collective-permute-start | bytes 3080 | tf_op jit(solution)/shard_map/ppermute | solution.py:652

commit v3 on v2

--- a/solution.py
+++ b/solution.py
@@ -32,10 +32,33 @@
     return x * x * lax.rsqrt(x)
 
 
-def column_step(q, held, sound, inside, inverse):
+def split(x):
+    high = x.astype(jnp.bfloat16)
+    return high, (x - high.astype(jnp.float32)).astype(jnp.bfloat16)
+
+
+def stack_weights(inverse, weights):
+    levels = inverse.shape[0]
+    high, low = split(inverse)
+    weights[0:levels, 0:levels] = high
+    weights[0:levels, levels:] = low
+    weights[levels:, 0:levels] = high
+    weights[levels:, levels:] = jnp.zeros_like(low)
+
+
+def split_dot(x, weights):
+    levels = x.shape[-1]
+    both = jnp.concatenate(split(x), axis=1)
+    out = jnp.dot(both, weights, preferred_element_type=jnp.float32)
+    return out[:, :levels] + out[:, levels:]
+
+
+def column_step(q, held, sound, inside, weights):
     levels = q.shape[-1]
-    source = inside * (held + q - pltpu.roll(q, levels - 1, 1))
-    solved = exact_dot(source, inverse)
+    source = q - pltpu.roll(q, levels - 1, 1)
+    if held is not None:
+        source = source + held
+    solved = split_dot(inside * source, weights)
     masked = solved * inside
     return (q - sound * (masked - pltpu.roll(masked, 1, 1)), solved)
 
@@ -104,12 +127,12 @@
     humidity_final,
     radius_final,
     sums_out,
-    series,
+    weights,
     p1_out,
     p2_out,
-    p3_out,
-    w3_out,
-    drift_out,
+    w2_out,
+    d2_out,
+    heat_out,
     xa_out,
     xb_out,
     ya_out,
@@ -118,9 +141,8 @@
     cloud,
     total,
     power,
+    series,
     wide,
-    w2_out,
-    d2_out,
     sound_ref,
     theta_ref,
     humidity_ref,
@@ -131,7 +153,6 @@
     u_ref,
     v_ref,
     w_ref,
-    theta_out,
     humidity_out,
     radius_out,
     sems,
@@ -150,7 +171,7 @@
         (u_hbm, u_ref),
         (v_hbm, v_ref),
         (w_hbm, w_ref),
-        (theta_out, theta_final),
+        (heat_out, theta_final),
         (humidity_out, humidity_final),
     )
     moves = [pltpu.make_async_copy(x, y, sems.at[n]) for n, (x, y) in enumerate(pairs)]
@@ -188,145 +209,125 @@
             total[...] += jnp.where(live, mass, 0.0)
         chunk_move(radius_out, radius_final, 2, step).start()
 
-    if True:
-        percent_sum = jnp.zeros((cols, levels), jnp.float32)
-        theta_sum = jnp.zeros((cols, levels), jnp.float32)
-        for i in range(rows):
-            change = MASS_FACTOR * total[:, i, :]
-            added = jnp.concatenate(
-                [
-                    jnp.zeros((lowest, cols), jnp.float32),
-                    change,
-                    jnp.zeros((levels - lowest - layers, cols), jnp.float32),
-                ],
-                axis=0,
-            ).T
-            humid = humidity_ref[i] - added
-            warm = theta_ref[i] + LATENT_HEAT * added
-            humidity_out[i] = humid
-            theta_out[i] = warm
-            percent_sum += 100.0 * (humid * jnp.exp(-VAPOUR_SLOPE * warm) - 1.0)
-            theta_sum += warm
-        sums_out[0:1] = jnp.sum(percent_sum, axis=0, keepdims=True)
-        sums_out[1:2] = jnp.sum(theta_sum, axis=0, keepdims=True)
-
-        for move in moves[8:]:
-            move.start()
-        for move in moves[4:8]:
-            move.wait()
-        sound = sound_ref[...]
-        inside = interior(levels)
-        inverse = series[...]
-        clear_rim(wide, rows, cols)
-        for i in range(rows):
-            wide[i + 2, PAD : PAD + cols, :] = p_ref[i]
-        j = lax.broadcasted_iota(jnp.int32, (cols, levels), 0)
-        for i in range(rows):
-            spread = jnp.zeros((cols, levels), jnp.float32)
-            if i + 1 < rows:
-                spread += u_ref[i + 1]
-            if i > 0:
-                spread -= u_ref[i - 1]
-            v = v_ref[i]
-            spread += jnp.where(j < cols - 1, pltpu.roll(v, cols - 1, 0), 0.0)
-            spread -= jnp.where(j > 0, pltpu.roll(v, 1, 0), 0.0)
-            d = 0.5 * spread - bend(wide, i + 2, cols)
-            p1, w1 = column_step(
-                p_ref[i] - sound * d,
-                w_ref[i] + BUOYANCY * theta_out[i],
-                sound,
-                inside,
-                inverse,
-            )
-            d2_out[i] = d
-            p1_out[i] = p1
-            w2_out[i] = w1
-        for i in range(rows):
-            wide[i + 2, PAD : PAD + cols, :] = p1_out[i]
-        for i in range(rows):
-            d = d2_out[i] - bend(wide, i + 2, cols)
-            p2, w2 = column_step(
-                p1_out[i] - sound * d,
-                w2_out[i] + BUOYANCY * theta_out[i],
-                sound,
-                inside,
-                inverse,
-            )
-            d2_out[i] = d
-            p2_out[i] = p2
-            w2_out[i] = w2
-
-        for i in range(rows):
-            wide[i + 2, PAD : PAD + cols, :] = p2_out[i]
-        for i in range(rows):
-            d = d2_out[i] - bend(wide, i + 2, cols)
-            p3_out[i], w3_out[i] = column_step(
-                p2_out[i] - sound * d,
-                w2_out[i] + BUOYANCY * theta_out[i],
-                sound,
-                inside,
-                inverse,
-            )
-        r = lax.broadcasted_iota(jnp.int32, (levels, levels), 0)
-        k = lax.broadcasted_iota(jnp.int32, (levels, levels), 1)
-        push = jnp.where(k == r, -BUOYANCY, 0.0)
-        drift_p, drift_w = (jnp.zeros_like(push), jnp.zeros_like(push))
-        for _ in range(SUB):
-            drift_p, drift_w = column_step(drift_p, drift_w + push, sound, inside, inverse)
-        drift_out[:, 0:levels] = drift_p
-        drift_out[:, levels:] = drift_w
-
-        even_x, even_y = (even(axes[0]), even(axes[1]))
-        for k, field in enumerate((p_ref, p1_out, p2_out)):
-            for n in range(2):
-                if k > 0:
-                    up, down = (field[rows - 2 + n], field[n])
-                    xa_out[2 * k + n] = jnp.where(even_x, up, down)
-                    xb_out[2 * k + n] = jnp.where(even_x, down, up)
-                up, down = (field[:, cols - 2 + n, :], field[:, n, :])
-                ya_out[2 * k + n] = jnp.where(even_y, up, down)
-                yb_out[2 * k + n] = jnp.where(even_y, down, up)
-        up, down = (p_ref[rows - 2] + 2.0 * u_ref[rows - 1], p_ref[1] - 2.0 * u_ref[0])
-        xa_out[0] = jnp.where(even_x, up, p_ref[0])
-        xa_out[1] = jnp.where(even_x, p_ref[rows - 1], down)
-        xb_out[0] = jnp.where(even_x, p_ref[0], up)
-        xb_out[1] = jnp.where(even_x, down, p_ref[rows - 1])
-        up, down = (v_ref[:, cols - 1, :], v_ref[:, 0, :])
-        ya_out[6] = jnp.where(even_y, up, down)
-        yb_out[6] = jnp.where(even_y, down, up)
-        for m, i in enumerate((0, rows - 1)):
-            up, down = (u_ref[i, cols - 2 : cols, :], u_ref[i, 0:2, :])
-            ya_out[7, 2 * m : 2 * m + 2, :] = jnp.where(even_y, up, down)
-            yb_out[7, 2 * m : 2 * m + 2, :] = jnp.where(even_y, down, up)
-        far_up, far_down = ([], [])
-        for side, c in ((far_up, cols - 4), (far_down, 2)):
-            for n in range(2):
-                line = lambda ref, i: ref[i, c + n : c + n + 1, :]
-                side += [line(p_ref, 0), line(p_ref, 1) - 2.0 * line(u_ref, 0)]
-            for n in range(2):
-                line = lambda ref, i: ref[i, c + n : c + n + 1, :]
-                side += [
-                    line(p_ref, rows - 2) + 2.0 * line(u_ref, rows - 1),
-                    line(p_ref, rows - 1),
-                ]
-        up, down = (jnp.concatenate(far_up, axis=0), jnp.concatenate(far_down, axis=0))
-        ya_out[8, 0:8, :] = jnp.where(even_y, up, down)
-        yb_out[8, 0:8, :] = jnp.where(even_y, down, up)
-        for out in (ya_out, yb_out):
-            out[7, 4:, :] = jnp.zeros((rows - 4, levels), jnp.float32)
-            out[9] = jnp.zeros((rows, levels), jnp.float32)
-            out[9, 0:2, :] = sums_out[...]
-        for m, i in enumerate((0, rows - 2)):
-            for n in range(2):
-                edge_out[4 * m + n : 4 * m + n + 1, :] = v_ref[i + n, 0:1, :]
-                edge_out[4 * m + 2 + n : 4 * m + 3 + n, :] = v_ref[i + n, cols - 1 : cols, :]
-        for m, i in enumerate((1, rows - 2)):
-            edge_out[8 + 4 * m : 10 + 4 * m, :] = p_ref[i, 0:2, :]
-            edge_out[10 + 4 * m : 12 + 4 * m, :] = p_ref[i, cols - 2 : cols, :]
-        for step in range(steps):
-            chunk_move(radius_out, radius_final, 2, step).wait()
-        for move in moves[8:]:
-            move.wait()
+    percent_sum = jnp.zeros((cols, levels), jnp.float32)
+    theta_sum = jnp.zeros((cols, levels), jnp.float32)
+    for i in range(rows):
+        change = MASS_FACTOR * total[:, i, :]
+        added = jnp.concatenate(
+            [
+                jnp.zeros((lowest, cols), jnp.float32),
+                change,
+                jnp.zeros((levels - lowest - layers, cols), jnp.float32),
+            ],
+            axis=0,
+        ).T
+        humid = humidity_ref[i] - added
+        warm = theta_ref[i] + LATENT_HEAT * added
+        humidity_out[i] = humid
+        heat_out[i] = warm
+        percent_sum += 100.0 * (humid * jnp.exp(-VAPOUR_SLOPE * warm) - 1.0)
+        theta_sum += warm
+    sums_out[0:1] = jnp.sum(percent_sum, axis=0, keepdims=True)
+    sums_out[1:2] = jnp.sum(theta_sum, axis=0, keepdims=True)
+
+    for move in moves[8:]:
+        move.start()
+    for move in moves[4:8]:
+        move.wait()
+    sound = sound_ref[...]
+    inside = interior(levels)
+    stack_weights(series[...], weights)
+    inverse = weights[...]
+    clear_rim(wide, rows, cols)
+    for i in range(rows):
+        wide[i + 2, PAD : PAD + cols, :] = p_ref[i]
+    j = lax.broadcasted_iota(jnp.int32, (cols, levels), 0)
+    for i in range(rows):
+        spread = jnp.zeros((cols, levels), jnp.float32)
+        if i + 1 < rows:
+            spread += u_ref[i + 1]
+        if i > 0:
+            spread -= u_ref[i - 1]
+        v = v_ref[i]
+        spread += jnp.where(j < cols - 1, pltpu.roll(v, cols - 1, 0), 0.0)
+        spread -= jnp.where(j > 0, pltpu.roll(v, 1, 0), 0.0)
+        d = 0.5 * spread - bend(wide, i + 2, cols)
+        p1, w1 = column_step(
+            p_ref[i] - sound * d,
+            w_ref[i] + BUOYANCY * heat_out[i],
+            sound,
+            inside,
+            inverse,
+        )
+        d2_out[i] = d
+        p1_out[i] = p1
+        w2_out[i] = w1
+    for i in range(rows):
+        wide[i + 2, PAD : PAD + cols, :] = p1_out[i]
+    for i in range(rows):
+        d = d2_out[i] - bend(wide, i + 2, cols)
+        p2, w2 = column_step(
+            p1_out[i] - sound * d,
+            w2_out[i] + BUOYANCY * heat_out[i],
+            sound,
+            inside,
+            inverse,
+        )
+        d2_out[i] = d
+        p2_out[i] = p2
+        w2_out[i] = w2
+
+    even_x, even_y = (even(axes[0]), even(axes[1]))
+    for k, field in enumerate((p_ref, p1_out, p2_out)):
+        for n in range(2):
+            if k > 0:
+                up, down = (field[rows - 2 + n], field[n])
+                xa_out[2 * k + n] = jnp.where(even_x, up, down)
+                xb_out[2 * k + n] = jnp.where(even_x, down, up)
+            up, down = (field[:, cols - 2 + n, :], field[:, n, :])
+            ya_out[2 * k + n] = jnp.where(even_y, up, down)
+            yb_out[2 * k + n] = jnp.where(even_y, down, up)
+    up, down = (p_ref[rows - 2] + 2.0 * u_ref[rows - 1], p_ref[1] - 2.0 * u_ref[0])
+    xa_out[0] = jnp.where(even_x, up, p_ref[0])
+    xa_out[1] = jnp.where(even_x, p_ref[rows - 1], down)
+    xb_out[0] = jnp.where(even_x, p_ref[0], up)
+    xb_out[1] = jnp.where(even_x, down, p_ref[rows - 1])
+    up, down = (v_ref[:, cols - 1, :], v_ref[:, 0, :])
+    ya_out[6] = jnp.where(even_y, up, down)
+    yb_out[6] = jnp.where(even_y, down, up)
+    for m, i in enumerate((0, rows - 1)):
+        up, down = (u_ref[i, cols - 2 : cols, :], u_ref[i, 0:2, :])
+        ya_out[7, 2 * m : 2 * m + 2, :] = jnp.where(even_y, up, down)
+        yb_out[7, 2 * m : 2 * m + 2, :] = jnp.where(even_y, down, up)
+    far_up, far_down = ([], [])
+    for side, c in ((far_up, cols - 4), (far_down, 2)):
+        for n in range(2):
+            line = lambda ref, i: ref[i, c + n : c + n + 1, :]
+            side += [line(p_ref, 0), line(p_ref, 1) - 2.0 * line(u_ref, 0)]
+        for n in range(2):
+            line = lambda ref, i: ref[i, c + n : c + n + 1, :]
+            side += [
+                line(p_ref, rows - 2) + 2.0 * line(u_ref, rows - 1),
+                line(p_ref, rows - 1),
+            ]
+    up, down = (jnp.concatenate(far_up, axis=0), jnp.concatenate(far_down, axis=0))
+    ya_out[8, 0:8, :] = jnp.where(even_y, up, down)
+    yb_out[8, 0:8, :] = jnp.where(even_y, down, up)
+    for out in (ya_out, yb_out):
+        out[7, 4:, :] = jnp.zeros((rows - 4, levels), jnp.float32)
+        out[9] = jnp.zeros((rows, levels), jnp.float32)
+        out[9, 0:2, :] = sums_out[...]
+    for m, i in enumerate((0, rows - 2)):
+        for n in range(2):
+            edge_out[4 * m + n : 4 * m + n + 1, :] = v_ref[i + n, 0:1, :]
+            edge_out[4 * m + 2 + n : 4 * m + 3 + n, :] = v_ref[i + n, cols - 1 : cols, :]
+    for m, i in enumerate((1, rows - 2)):
+        edge_out[8 + 4 * m : 10 + 4 * m, :] = p_ref[i, 0:2, :]
+        edge_out[10 + 4 * m : 12 + 4 * m, :] = p_ref[i, cols - 2 : cols, :]
+    for step in range(steps):
+        chunk_move(radius_out, radius_final, 2, step).wait()
+    for move in moves[8:]:
+        move.wait()
 
 
 def first(sound, theta, humidity, radius_sq, multiplicity, count, p, u, v, w):
@@ -336,9 +337,9 @@
     f32 = lambda *shape: jax.ShapeDtypeStruct(shape, jnp.float32)
     block = f32(*theta.shape)
     outs = (
-        [block, block, f32(*radius_sq.shape), f32(2, levels), f32(levels, levels)]
-        + [block] * 4
-        + [f32(levels, 2 * levels)]
+        [block, block, f32(*radius_sq.shape), f32(2, levels)]
+        + [jax.ShapeDtypeStruct((2 * levels, 2 * levels), jnp.bfloat16)]
+        + [block] * 5
         + [f32(6, cols, levels)] * 2
         + [f32(10, rows, levels)] * 2
         + [f32(16, levels)]
@@ -354,9 +355,8 @@
             layer_block,
             layer_block,
             pltpu.VMEM((levels, levels), jnp.float32),
+            pltpu.VMEM((levels, levels), jnp.float32),
             pltpu.VMEM((rows + 4, cols + 2 * PAD, levels), jnp.float32),
-            local_block,
-            local_block,
             pltpu.VMEM(sound.shape, jnp.float32),
             local_block,
             local_block,
@@ -364,7 +364,7 @@
             pltpu.VMEM(multiplicity.shape, multiplicity.dtype),
             pltpu.VMEM(count.shape, count.dtype),
         ]
-        + [local_block] * 6
+        + [local_block] * 5
         + [
             pltpu.VMEM(radius_sq.shape, jnp.float32),
             pltpu.SemaphoreType.DMA((10,)),
@@ -378,7 +378,47 @@
     )(sound, theta, humidity, radius_sq, multiplicity, count, p, u, v, w)
 
 
-def corner_kernel(axes, ya_ref, yb_ref, edge_ref, sums_ref, a_out, b_out, sums_out):
+def third_kernel(sound_ref, inverse_ref, heat_ref, p_ref, w_ref, d_ref, p_out, w_out, drift_out, wide):
+    rows, cols, levels = p_ref.shape
+    sound = sound_ref[...]
+    inside = interior(levels)
+    inverse = inverse_ref[...]
+    clear_rim(wide, rows, cols)
+    for i in range(rows):
+        wide[i + 2, PAD : PAD + cols, :] = p_ref[i]
+    for i in range(rows):
+        d = d_ref[i] - bend(wide, i + 2, cols)
+        p_out[i], w_out[i] = column_step(
+            p_ref[i] - sound * d, w_ref[i] + BUOYANCY * heat_ref[i], sound, inside, inverse
+        )
+    r = lax.broadcasted_iota(jnp.int32, (levels, levels), 0)
+    k = lax.broadcasted_iota(jnp.int32, (levels, levels), 1)
+    push = jnp.where(k == r, -BUOYANCY, 0.0)
+    drift_p, drift_w = (jnp.zeros_like(push), jnp.zeros_like(push))
+    for _ in range(SUB):
+        drift_p, drift_w = column_step(drift_p, drift_w + push, sound, inside, inverse)
+    drift_out[:, 0:levels] = drift_p
+    drift_out[:, levels:] = drift_w
+
+
+def third(sound, weights, heat, p, w, d):
+    rows, cols, levels = p.shape
+    block = jax.ShapeDtypeStruct(p.shape, jnp.float32)
+    return pl.pallas_call(
+        third_kernel,
+        in_specs=[VMEM] * 6,
+        out_specs=[VMEM] * 3,
+        out_shape=[block, block, jax.ShapeDtypeStruct((levels, 2 * levels), jnp.float32)],
+        scratch_shapes=[pltpu.VMEM((rows + 4, cols + 2 * PAD, levels), jnp.float32)],
+        compiler_params=pltpu.CompilerParams(vmem_limit_bytes=GRANT),
+        cost_estimate=pl.CostEstimate(
+            flops=2_000_000_000, bytes_accessed=4_000_000, transcendentals=0
+        ),
+        name="third_step",
+    )(sound, weights, heat, p, w, d)
+
+
+def corner_kernel(axes, ya_ref, yb_ref, edge_ref, sums_ref, a_out, b_out):
     even_x, even_y = (even(axes[0]), even(axes[1]))
     rows = ya_ref.shape[1]
     levels = ya_ref.shape[2]
@@ -402,9 +442,8 @@
         put(at + 16, side[8, 4:8], side[8, 0:4])
     put(2 * SIDE, edge_ref[4:8, :], edge_ref[0:4, :])
     put(2 * SIDE + 4, edge_ref[12:16, :], edge_ref[8:12, :])
-    both = sums_ref[...] + ya_ref[9, 0:2, :]
+    both = sums_ref[...]
     put(2 * SIDE + 8, both, both)
-    sums_out[...] = both
     rest = jnp.zeros((EXTRA - 2 * SIDE - 10, levels), jnp.float32)
     put(2 * SIDE + 10, rest, rest)
 
@@ -415,8 +454,8 @@
     return pl.pallas_call(
         functools.partial(corner_kernel, ("gx", "gy")),
         in_specs=[VMEM] * 4,
-        out_specs=[VMEM] * 3,
-        out_shape=[out, out, jax.ShapeDtypeStruct(sums.shape, jnp.float32)],
+        out_specs=[VMEM] * 2,
+        out_shape=[out, out],
         compiler_params=pltpu.CompilerParams(vmem_limit_bytes=GRANT),
         cost_estimate=pl.CostEstimate(flops=10_000_000, bytes_accessed=100_000, transcendentals=0),
         name="corner",
@@ -437,41 +476,8 @@
             mu[:, base + c, :] += 0.25 * field[:, base - 2 + c, :]
 
 
-def last_kernel(
-    axes,
-    columns,
-    sound_ref,
-    inverse_ref,
-    p0_ref,
-    u_ref,
-    v_ref,
-    p1_ref,
-    p2_ref,
-    p3_ref,
-    w3_ref,
-    xa,
-    xb,
-    ya,
-    yb,
-    ca,
-    cb,
-    drift_ref,
-    sums_ref,
-    u_out,
-    v_out,
-    w_out,
-    p_out,
-    profile_out,
-    f0,
-    f1,
-    f2,
-    mu,
-    yp,
-    yw,
-    yd,
-    urows,
-    vcols,
-):
+def response_one(axes, sound_ref, inverse_ref, p0_ref, u_ref, v_ref, p1_ref, p2_ref, *refs):
+    xa, xb, ya, yb, ca, cb, f0, f1, f2, yp, yw, yd, far_out, mu, urows, vcols = refs
     rows, cols, levels = p0_ref.shape
     ext = cols + 2 * PAD
     even_x, even_y = (even(axes[0]), even(axes[1]))
@@ -540,7 +546,7 @@
     mu[:, PAD, :] += 0.5 * vcols[0]
     mu[:, PAD + cols - 1, :] -= 0.5 * vcols[3]
     mu[:, PAD + cols, :] += 0.5 * vcols[2]
-    for c_rows, at, row in ((low_c, 0, 2), (high_c, rows + 2, rows)):
+    for c_rows, row in ((low_c, 2), (high_c, rows)):
         for s, c in enumerate((PAD - 4, PAD + cols + 2)):
             for n in range(2):
                 start = SIDE * s + 16 + 2 * n
@@ -550,8 +556,8 @@
         [c_rows[SIDE * s + 12 : SIDE * s + 16] for c_rows in (low_c, high_c) for s in range(2)],
         axis=0,
     )
-    far, _ = column_step(sound * far, jnp.zeros_like(far), sound, inside, inverse)
-    far = 0.25 * far
+    far, _ = column_step(sound * far, None, sound, inside, inverse)
+    far_out[...] = 0.25 * far
 
     for r in range(rows + 4):
         if 4 <= r < rows:
@@ -565,9 +571,18 @@
             d = -mu[r, span, :]
             q = -sound * d
             yp[r, span, :], yw[r, span, :] = column_step(
-                q, jnp.zeros_like(q), sound, inside, inverse
+                q, None, sound, inside, inverse
             )
             yd[r, span, :] = d
+
+
+def response_two(shape, sound_ref, inverse_ref, f0, f1, f2, yp, yw, yd, far_ref, *refs):
+    s_out, yp_out, yw_out, yd_out, mu = refs
+    rows, cols, levels = shape
+    ext = cols + 2 * PAD
+    sound = sound_ref[...]
+    inside = interior(levels)
+    inverse = inverse_ref[...]
     cross(mu, f1, rows, cols)
     for r in range(rows + 4):
         y = yp[r]
@@ -577,20 +592,30 @@
         if r < rows + 2:
             near += yp[r + 2]
         mu[r] += 0.25 * near - y
-        f0[r] += f1[r] + y
+        s_out[r] = f0[r] + f1[r] + y
     for m, at in enumerate((0, rows + 2)):
         for s, c in enumerate((PAD, PAD + cols - 2)):
             for n in range(2):
                 start = 8 * m + 4 * s + 2 * n
                 for e in range(2):
-                    mu[at + e, c + n : c + n + 1, :] += far[start + e : start + e + 1]
+                    mu[at + e, c + n : c + n + 1, :] += far_ref[start + e : start + e + 1, :]
     for r in range(rows + 4):
         d = yd[r] - mu[r]
         p, w = column_step(yp[r] - sound * d, yw[r], sound, inside, inverse)
-        yd[r] = d
-        yp[r] = p
-        yw[r] = w
-        f0[r] += f2[r] + p
+        yd_out[r] = d
+        yp_out[r] = p
+        yw_out[r] = w
+        s_out[r] += f2[r] + p
+
+
+def response_three(columns, sound_ref, inverse_ref, u_ref, v_ref, p3_ref, w3_ref, f2, *refs):
+    s_ref, yp, yw, yd, drift_ref, sums_ref = refs[:6]
+    u_out, v_out, w_out, p_out, profile_out, mu = refs[6:]
+    rows, cols, levels = u_ref.shape
+    sound = sound_ref[...]
+    inside = interior(levels)
+    inverse = inverse_ref[...]
+    body = slice(PAD, PAD + cols)
     cross(mu, f2, rows, cols)
     total = sums_ref[...] * (1.0 / columns)
     profile_out[...] = total[0:1]
@@ -605,31 +630,20 @@
         )
         p_out[i] = p3_ref[i] + p + drift_p
         w_out[i] = w3_ref[i] + w + drift_w
-        u_out[i] = u_ref[i] - 0.5 * (f0[r + 1, body, :] - f0[r - 1, body, :])
-        east = lambda n: f0[r, PAD + n : PAD + n + cols, :]
+        u_out[i] = u_ref[i] - 0.5 * (s_ref[r + 1, body, :] - s_ref[r - 1, body, :])
+        east = lambda n: s_ref[r, PAD + n : PAD + n + cols, :]
         v_out[i] = v_ref[i] - 0.5 * (east(1) - east(-1))
 
 
-def last(columns, *args):
-    rows, cols, levels = args[2].shape
-    f32 = lambda *shape: jax.ShapeDtypeStruct(shape, jnp.float32)
-    block = f32(rows, cols, levels)
-    wide = pltpu.VMEM((rows + 4, cols + 2 * PAD, levels), jnp.float32)
+def response(kernel, args, outs, scratch, flops):
     return pl.pallas_call(
-        functools.partial(last_kernel, ("gx", "gy"), columns),
+        kernel,
         in_specs=[VMEM] * len(args),
-        out_specs=[VMEM] * 5,
-        out_shape=[block] * 4 + [f32(1, levels)],
-        scratch_shapes=[wide] * 7
-        + [
-            pltpu.VMEM((4, cols + 2 * PAD, levels), jnp.float32),
-            pltpu.VMEM((4, rows + 4, levels), jnp.float32),
-        ],
+        out_specs=[VMEM] * len(outs),
+        out_shape=outs,
+        scratch_shapes=scratch,
         compiler_params=pltpu.CompilerParams(vmem_limit_bytes=GRANT),
-        cost_estimate=pl.CostEstimate(
-            flops=3_000_000_000, bytes_accessed=6_000_000, transcendentals=0
-        ),
-        name="response",
+        cost_estimate=pl.CostEstimate(flops=flops, bytes_accessed=6_000_000, transcendentals=0),
     )(*args)
 
 
@@ -641,20 +655,22 @@
 
 def exchange(a, b, axis):
     near, far = swaps(lax.axis_size(axis))
-    return lax.ppermute(a, axis, near), lax.ppermute(b, axis, far)
-
-
-def total_sum(value):
-    for axis in ("gx", "gy"):
-        count = lax.axis_size(axis)
-        distance = 2
-        while distance < count:
-            value = value + lax.ppermute(value, axis, [(i, i ^ distance) for i in range(count)])
-            distance *= 2
+    a = lax.ppermute(a, axis, near)
+    b = lax.ppermute(b, axis, far)
+    return a, b
+
+
+def total_sum(value, axis):
+    count = lax.axis_size(axis)
+    distance = 2
+    while distance < count:
+        moved = lax.ppermute(value, axis, [(i, i ^ distance) for i in range(count)])
+        value = value + moved
+        distance *= 2
     return value
 
 
-def local(
+def window(
     eastward,
     northward,
     vertical,
@@ -673,12 +689,12 @@
         humidity_out,
         radius_out,
         sums,
-        inverse,
+        weights,
         p1,
         p2,
-        p3,
-        w3,
-        drift,
+        w2,
+        d2,
+        heat,
         xa,
         xb,
         ya,
@@ -701,31 +717,41 @@
             )
         )
     )
+    rows, cols, levels = theta.shape
+    f32 = lambda *shape: jax.ShapeDtypeStruct(shape, jnp.float32)
+    wide = (rows + 4, cols + 2 * PAD, levels)
     xa, xb = exchange(xa, xb, "gx")
     ya, yb = exchange(ya, yb, "gy")
-    ca, cb, sums = corner(ya, yb, edge, sums)
+    sums = total_sum(sums + ya[9, 0:2], "gy")
+    ca, cb = corner(ya, yb, edge, sums)
     ca, cb = exchange(ca, cb, "gx")
     at = 2 * SIDE + 8
-    sums = total_sum(sums + ca[at : at + 2])
-    u, v, w, p, profile = last(
-        columns,
-        sound,
-        inverse,
-        pressure,
-        eastward,
-        northward,
-        p1,
-        p2,
-        p3,
-        w3,
-        xa,
-        xb,
-        ya,
-        yb,
-        ca,
-        cb,
-        drift,
-        sums,
+    sums = total_sum(sums + ca[at : at + 2], "gx")
+    p3, w3, drift = third(sound, weights, heat, p2, w2, d2)
+    f0, f1, f2, yp, yw, yd, far = response(
+        functools.partial(response_one, ("gx", "gy")),
+        (sound, weights, pressure, eastward, northward, p1, p2, xa, xb, ya, yb, ca, cb),
+        [f32(*wide)] * 6 + [f32(16, levels)],
+        [
+            pltpu.VMEM(wide, jnp.float32),
+            pltpu.VMEM((4, cols + 2 * PAD, levels), jnp.float32),
+            pltpu.VMEM((4, rows + 4, levels), jnp.float32),
+        ],
+        4_000_000_000,
+    )
+    moved, yp, yw, yd = response(
+        functools.partial(response_two, theta.shape),
+        (sound, weights, f0, f1, f2, yp, yw, yd, far),
+        [f32(*wide)] * 4,
+        [pltpu.VMEM(wide, jnp.float32)],
+        4_000_000_000,
+    )
+    u, v, w, p, profile = response(
+        functools.partial(response_three, columns),
+        (sound, weights, eastward, northward, p3, w3, f2, moved, yp, yw, yd, drift, sums),
+        [f32(*theta.shape)] * 4 + [f32(1, levels)],
+        [pltpu.VMEM(wide, jnp.float32)],
+        2_000_000_000,
     )
     return (u, v, w, p, theta_out, humidity_out, radius_out, profile[0])
 
@@ -734,7 +760,7 @@
     grid = P("gx", "gy", None)
     drops = P(None, None, "gx", "gy")
     return jax.shard_map(
-        local,
+        window,
         mesh=mesh,
         in_specs=(grid,) * 6 + (P(), drops, drops, P(None, "gx", "gy")),
         out_specs=(grid,) * 6 + (drops, P()),

time: 38.5 us -> 38.2 us (level)
  waiting for transfers between devices: 13.3 us -> 9.08 us
  starting transfers between devices: 11.1 us -> 15.2 us
    ppermute x9, waiting for transfers between devices: 13.3 us -> 9.08 us  [the longest x3 9.06 us: total_sum(): moved = lax.ppermute(value, axis, [(i, i ^ distance) for i in range(count)])]
    ppermute x9, starting transfers between devices: 11.1 us -> 15.2 us  [the longest x3 6.34 us: exchange(): b = lax.ppermute(b, axis, far)]
    pallas_call x1, Pallas kernels: 8.42 us -> 7.46 us  [first(): pl.pallas_call(functools.partial(first_kernel, ('gx', 'gy')), in_specs=[h...]
    pallas_call x1 -> x4, Pallas kernels: 4.74 us -> 5.55 us  [the longest x3 4.45 us: response(): pl.pallas_call(kernel, in_specs=[VMEM] * len(args), out_specs=[VMEM] * le...]
  transfers between devices with their start and end apart: 9 -> 9, of which waited for: 5 -> 3; matrix products, arithmetic and copies ran while one was open for 0% -> 0% of each run, Pallas kernels for 0% -> 3%
where the time goes in v3:
time: 38.2 us; the launch traced here: 38.1 us
  starting transfers between devices  15.2 us (40%)
  Pallas kernels  13 us (34%)
  waiting for transfers between devices  9.08 us (24%)
  between operations  0.74 us (2%)
    ppermute x3, waiting for transfers between devices, total_sum(): moved = lax.ppermute(value, axis, [(i, i ^ distance) for i in range(count)])  9.06 us
    pallas_call x1, Pallas kernels, first(): pl.pallas_call(functools.partial(first_kernel, ('gx', 'gy')), in_specs=[h...  7.46 us
    ppermute x3, starting transfers between devices, exchange(): b = lax.ppermute(b, axis, far)  6.34 us
    ppermute x3, starting transfers between devices, total_sum(): moved = lax.ppermute(value, axis, [(i, i ^ distance) for i in range(count)])  5.17 us
    pallas_call x3, Pallas kernels, response(): pl.pallas_call(kernel, in_specs=[VMEM] * len(args), out_specs=[VMEM] * le...  4.45 us
    ppermute x3, starting transfers between devices, exchange(): a = lax.ppermute(a, axis, near)  3.68 us
    pallas_call x1, Pallas kernels, third(): pl.pallas_call(third_kernel, in_specs=[VMEM] * 6, out_specs=[VMEM] * 3, o...  1.11 us
  transfers between devices with their start and end apart: 9, of which 3 were waited for; matrix products, arithmetic and copies ran while one was open for 0% of the time, Pallas kernels for 3%

profile of v3, /device:TPU:0, one launch (start us, length us, event | category | flops | bytes accessed | tf_op | source)
XLA Modules:
  0.0 38.1 jit_solution(5363109144056929830)
XLA Ops:
  0.6 0.0 copy-start.3
  0.6 7.5 %condense_and_evolve.1 = (f32[8,128,128]{2,1,0:T(8,128)}, f32[8,128,128]{2,1,0:T(8,128)}, f32[64,8,8,128]{3,2,1,0:T(8,128)}, f32[2,128]{1,0:T(2,128)S(1)}, bf16[...) custom-call(f32[1,128]{1,0:T(1,128)} %bitcast.6, ...), custom_call_target="tpu_custom_call" | custom-call | flops 8000000000 | bytes 12000000 | tf_op jit(solution)/shard_map/condense_and_evolve/pallas_call | solution.py:349
  8.1 3.1 %collective-permute-start.2 = (f32[10,8,128]{2,1,0:T(8,128)S(1)}, f32[10,8,128]{2,1,0:T(8,128)S(1)}, u32[]{:S(2)}, u32[]{:S(2)}) collective-permute-start(f32[10,8,128]{2,1,0:T(8,128)S(1)} %get-tuple-element.54), channel_id=1, source_target_pairs={{0,1},{1,0},{2,3},{3,2},{4,5},{5,4},{6,7},{7,6},{8,9},{9,8},{10,11... | collective-permute-start | bytes 122888 | tf_op jit(solution)/shard_map/ppermute | solution.py:658
  11.2 2.5 %collective-permute-start.3 = (f32[10,8,128]{2,1,0:T(8,128)S(1)}, f32[10,8,128]{2,1,0:T(8,128)S(1)}, u32[]{:S(2)}, u32[]{:S(2)}) collective-permute-start(f32[10,8,128]{2,1,0:T(8,128)S(1)} %get-tuple-element.55), channel_id=1, source_target_pairs={{0,3},{1,2},{2,1},{3,0},{4,7},{5,6},{6,5},{7,4},{8,11},{9,10},{10,... | collective-permute-start | bytes 122888 | tf_op jit(solution)/shard_map/ppermute | solution.py:659
  13.7 0.0 collective-permute-done.2.ya_ref.refs_2_
  13.7 2.9 %collective-permute-start.4 = (f32[2,128]{1,0:T(2,128)S(1)}, f32[2,128]{1,0:T(2,128)S(1)}, u32[]{:S(2)}, u32[]{:S(2)}) collective-permute-start(f32[2,128]{1,0:T(2,128)S(1)} %fusion), channel_id=1, source_target_pairs={{0,2},{1,3},{2,0},{3,1},{4,6},{5,7},{6,4},{7,5},{8,10},{9,11},{10,... | collective-permute-start | bytes 3080 | tf_op jit(solution)/shard_map/ppermute | solution.py:667
  16.6 1.6 %collective-permute-done.4 = f32[2,128]{1,0:T(2,128)S(1)} collective-permute-done((f32[2,128]{1,0:T(2,128)S(1)}, f32[2,128]{1,0:T(2,128)S(1)}, u32[]{:S(2)}, u32[]{:S(2)}) %collective-permute-start.4) | collective-permute-done | bytes 1056 | tf_op jit(solution)/shard_map/ppermute | solution.py:667
  18.2 0.0 collective-permute-done.3.yb_ref.refs_3_
  18.2 0.1 collective-permute-start.5
  18.3 0.5 %collective-permute-start = (f32[6,128,128]{2,1,0:T(8,128)S(1)}, f32[6,128,128]{2,1,0:T(8,128)S(1)}, u32[]{:S(2)}, u32[]{:S(2)}) collective-permute-start(f32[6,128,128]{2,1,0:T(8,128)S(1)} %get-tuple-element.52), channel_id=1, source_target_pairs={{0,4},{4,0},{8,12},{12,8},{16,20},{20,16},{24,28},{28,24},{1,5},{5... | collective-permute-start | bytes 1179656 | tf_op jit(solution)/shard_map/ppermute | solution.py:658
  18.8 2.1 %collective-permute-start.1 = (f32[6,128,128]{2,1,0:T(8,128)S(1)}, f32[6,128,128]{2,1,0:T(8,128)S(1)}, u32[]{:S(2)}, u32[]{:S(2)}) collective-permute-start(f32[6,128,128]{2,1,0:T(8,128)S(1)} %get-tuple-element.53), channel_id=1, source_target_pairs={{0,28},{4,8},{8,4},{12,16},{16,12},{20,24},{24,20},{28,0},{1,29},{... | collective-permute-start | bytes 1179656 | tf_op jit(solution)/shard_map/ppermute | solution.py:659
  20.9 0.0 collective-permute-done.5.refs_4_
  20.9 0.0 collective-permute-start.7
  21.0 1.7 %collective-permute-start.6 = (f32[56,128]{1,0:T(8,128)S(1)}, f32[56,128]{1,0:T(8,128)S(1)}, u32[]{:S(2)}, u32[]{:S(2)}) collective-permute-start(f32[56,128]{1,0:T(8,128)S(1)} %get-tuple-element.59), channel_id=1, source_target_pairs={{0,28},{4,8},{8,4},{12,16},{16,12},{20,24},{24,20},{28,0},{1,29},{... | collective-permute-start | bytes 86024 | tf_op jit(solution)/shard_map/ppermute | solution.py:659
  22.7 7.1 %collective-permute-done.7 = f32[2,128]{1,0:T(2,128)S(1)} collective-permute-done((f32[2,128]{1,0:T(2,128)S(1)}, f32[2,128]{1,0:T(2,128)S(1)}, u32[]{:S(2)}, u32[]{:S(2)}) %collective-permute-start.7) | collective-permute-done | bytes 1056 | tf_op jit(solution)/shard_map/ppermute | solution.py:667
  29.8 2.2 %collective-permute-start.8 = (f32[2,128]{1,0:T(2,128)S(1)}, f32[2,128]{1,0:T(2,128)S(1)}, u32[]{:S(2)}, u32[]{:S(2)}) collective-permute-start(f32[2,128]{1,0:T(2,128)S(1)} %add.18), channel_id=1, source_target_pairs={{0,16},{4,20},{8,24},{12,28},{16,0},{20,4},{24,8},{28,12},{1,17},{... | collective-permute-start | bytes 3080 | tf_op jit(solution)/shard_map/ppermute | solution.py:667
  32.0 0.0 copy-done.3
  32.0 0.0 copy-start
  32.0 0.0 copy-start.1
  32.0 0.0 copy-start.2
  32.0 1.1 %third_step.1 = (f32[8,128,128]{2,1,0:T(8,128)S(1)}, f32[8,128,128]{2,1,0:T(8,128)S(1)}, f32[128,256]{1,0:T(8,128)S(1)}) custom-call(f32[1,128]{1,0:T(1,128)S(1)} %bitcast.7, bf16[256,256]{1,0:T(8,128)(2,1)S(1)} %get-tuple-element.44.inverse_ref, f32[8,128,128]{2,1,0:T(8,128)S(1)} %get-tuple-element.45.heat_ref, ...), custom_call_target="tpu_custom_call" | custom-call | flops 2000000000 | bytes 4000000 | tf_op jit(solution)/shard_map/third_step/pallas_call | solution.py:407
  33.1 0.4 %collective-permute-done.8 = f32[2,128]{1,0:T(2,128)S(1)} collective-permute-done((f32[2,128]{1,0:T(2,128)S(1)}, f32[2,128]{1,0:T(2,128)S(1)}, u32[]{:S(2)}, u32[]{:S(2)}) %collective-permute-start.8) | collective-permute-done | bytes 1056 | tf_op jit(solution)/shard_map/ppermute | solution.py:667
  33.6 0.0 collective-permute-done.6.refs_5_
  33.6 0.0 collective-permute-done.refs_0_
  33.6 0.0 collective-permute-done.1.refs_1_
  33.6 0.0 copy-done
  33.6 0.0 copy-done.1
  33.6 0.0 copy-done.2
  33.6 1.0 %shard_map.161 = (f32[12,144,128]{2,1,0:T(8,128)S(1)}, f32[12,144,128]{2,1,0:T(8,128)S(1)}, f32[12,144,128]{2,1,0:T(8,128)S(1)}, f32[12,144,128]{2,1,0:T(8,128)S...) custom-call(f32[1,128]{1,0:T(1,128)S(1)} %bitcast.8, ...), custom_call_target="tpu_custom_call" | custom-call | flops 4000000000 | bytes 6000000 | tf_op jit(solution)/shard_map/pallas_call | solution.py:639
  34.6 1.3 %shard_map.162 = (f32[12,144,128]{2,1,0:T(8,128)S(1)}, f32[12,144,128]{2,1,0:T(8,128)S(1)}, f32[12,144,128]{2,1,0:T(8,128)S(1)}, f32[12,144,128]{2,1,0:T(8,128)S(1)}) custom-call(f32[1,128]{1,0:T(1,128)S(1)} %bitcast.9, bf16[256,256]{1,0:T(8,128)(2,1)S(1)} %get-tuple-element.44.inverse_ref, f32[12,144,128]{2,1,0:T(8,128)S(1)} %get-tuple-element.61.f0, ...), custom_call_target="tpu_custom_call" | custom-call | flops 4000000000 | bytes 6000000 | tf_op jit(solution)/shard_map/pallas_call | solution.py:639
  35.9 2.1 %shard_map.163 = (f32[8,128,128]{2,1,0:T(8,128)}, f32[8,128,128]{2,1,0:T(8,128)}, f32[8,128,128]{2,1,0:T(8,128)}, f32[8,128,128]{2,1,0:T(8,128)}, f32[1,128]{1,0:T(1,128)}) custom-call(f32[1,128]{1,0:T(1,128)S(1)} %bitcast.10, bf16[256,256]{1,0:T(8,128)(2,1)S(1)} %get-tuple-element.44.inverse_ref, f32[8,128,128]{2,1,0:T(8,128)S(1)} %copy-done.1, ...), custom_call_target="tpu_custom_call" | custom-call | flops 2000000000 | bytes 6000000 | tf_op jit(solution)/shard_map/pallas_call | solution.py:639
  (6 shorter events, 0.0 us)
Async XLA Ops:
  0.6 31.4 %copy-start.3 = (f32[128]{0:T(128)S(1)}, f32[128]{0:T(128)}, u32[]{:S(2)}) copy-start(f32[128]{0:T(128)} %param.16) | copy-start | bytes 1540
  8.1 5.6 %collective-permute-start.2 = (f32[10,8,128]{2,1,0:T(8,128)S(1)}, f32[10,8,128]{2,1,0:T(8,128)S(1)}, u32[]{:S(2)}, u32[]{:S(2)}) collective-permute-start(f32[10,8,128]{2,1,0:T(8,128)S(1)} %get-tuple-element.54), channel_id=1, source_target_pairs={{0,1},{1,0},{2,3},{3,2},{4,5},{5,4},{6,7},{7,6},{8,9},{9,8},{10,11... | collective-permute-start | bytes 122888 | tf_op jit(solution)/shard_map/ppermute | solution.py:658
  11.2 7.0 %collective-permute-start.3 = (f32[10,8,128]{2,1,0:T(8,128)S(1)}, f32[10,8,128]{2,1,0:T(8,128)S(1)}, u32[]{:S(2)}, u32[]{:S(2)}) collective-permute-start(f32[10,8,128]{2,1,0:T(8,128)S(1)} %get-tuple-element.55), channel_id=1, source_target_pairs={{0,3},{1,2},{2,1},{3,0},{4,7},{5,6},{6,5},{7,4},{8,11},{9,10},{10,... | collective-permute-start | bytes 122888 | tf_op jit(solution)/shard_map/ppermute | solution.py:659
  13.7 4.5 %collective-permute-start.4 = (f32[2,128]{1,0:T(2,128)S(1)}, f32[2,128]{1,0:T(2,128)S(1)}, u32[]{:S(2)}, u32[]{:S(2)}) collective-permute-start(f32[2,128]{1,0:T(2,128)S(1)} %fusion), channel_id=1, source_target_pairs={{0,2},{1,3},{2,0},{3,1},{4,6},{5,7},{6,4},{7,5},{8,10},{9,11},{10,... | collective-permute-start | bytes 3080 | tf_op jit(solution)/shard_map/ppermute | solution.py:667
  18.2 2.7 %collective-permute-start.5 = (f32[56,128]{1,0:T(8,128)S(1)}, f32[56,128]{1,0:T(8,128)S(1)}, u32[]{:S(2)}, u32[]{:S(2)}) collective-permute-start(f32[56,128]{1,0:T(8,128)S(1)} %get-tuple-element.58), channel_id=1, source_target_pairs={{0,4},{4,0},{8,12},{12,8},{16,20},{20,16},{24,28},{28,24},{1,5},{5... | collective-permute-start | bytes 86024 | tf_op jit(solution)/shard_map/ppermute | solution.py:658
  18.3 15.3 %collective-permute-start = (f32[6,128,128]{2,1,0:T(8,128)S(1)}, f32[6,128,128]{2,1,0:T(8,128)S(1)}, u32[]{:S(2)}, u32[]{:S(2)}) collective-permute-start(f32[6,128,128]{2,1,0:T(8,128)S(1)} %get-tuple-element.52), channel_id=1, source_target_pairs={{0,4},{4,0},{8,12},{12,8},{16,20},{20,16},{24,28},{28,24},{1,5},{5... | collective-permute-start | bytes 1179656 | tf_op jit(solution)/shard_map/ppermute | solution.py:658
  18.8 14.8 %collective-permute-start.1 = (f32[6,128,128]{2,1,0:T(8,128)S(1)}, f32[6,128,128]{2,1,0:T(8,128)S(1)}, u32[]{:S(2)}, u32[]{:S(2)}) collective-permute-start(f32[6,128,128]{2,1,0:T(8,128)S(1)} %get-tuple-element.53), channel_id=1, source_target_pairs={{0,28},{4,8},{8,4},{12,16},{16,12},{20,24},{24,20},{28,0},{1,29},{... | collective-permute-start | bytes 1179656 | tf_op jit(solution)/shard_map/ppermute | solution.py:659
  20.9 8.9 %collective-permute-start.7 = (f32[2,128]{1,0:T(2,128)S(1)}, f32[2,128]{1,0:T(2,128)S(1)}, u32[]{:S(2)}, u32[]{:S(2)}) collective-permute-start(f32[2,128]{1,0:T(2,128)S(1)} %slice_add_fusion), channel_id=1, source_target_pairs={{0,8},{4,12},{8,0},{12,4},{16,24},{20,28},{24,16},{28,20},{1,9},{5... | collective-permute-start | bytes 3080 | tf_op jit(solution)/shard_map/ppermute | solution.py:667
  21.0 12.6 %collective-permute-start.6 = (f32[56,128]{1,0:T(8,128)S(1)}, f32[56,128]{1,0:T(8,128)S(1)}, u32[]{:S(2)}, u32[]{:S(2)}) collective-permute-start(f32[56,128]{1,0:T(8,128)S(1)} %get-tuple-element.59), channel_id=1, source_target_pairs={{0,28},{4,8},{8,4},{12,16},{16,12},{20,24},{24,20},{28,0},{1,29},{... | collective-permute-start | bytes 86024 | tf_op jit(solution)/shard_map/ppermute | solution.py:659
  29.8 3.8 %collective-permute-start.8 = (f32[2,128]{1,0:T(2,128)S(1)}, f32[2,128]{1,0:T(2,128)S(1)}, u32[]{:S(2)}, u32[]{:S(2)}) collective-permute-start(f32[2,128]{1,0:T(2,128)S(1)} %add.18), channel_id=1, source_target_pairs={{0,16},{4,20},{8,24},{12,28},{16,0},{20,4},{24,8},{28,12},{1,17},{... | collective-permute-start | bytes 3080 | tf_op jit(solution)/shard_map/ppermute | solution.py:667
  32.0 1.6 %copy-start = (f32[8,128,128]{2,1,0:T(8,128)S(1)}, f32[8,128,128]{2,1,0:T(8,128)}, u32[]{:S(2)}) copy-start(f32[8,128,128]{2,1,0:T(8,128)} %p0_ref.1) | copy-start | bytes 1572868
  32.0 1.6 %copy-start.1 = (f32[8,128,128]{2,1,0:T(8,128)S(1)}, f32[8,128,128]{2,1,0:T(8,128)}, u32[]{:S(2)}) copy-start(f32[8,128,128]{2,1,0:T(8,128)} %u_ref.3) | copy-start | bytes 1572868
  32.0 1.6 %copy-start.2 = (f32[8,128,128]{2,1,0:T(8,128)S(1)}, f32[8,128,128]{2,1,0:T(8,128)}, u32[]{:S(2)}) copy-start(f32[8,128,128]{2,1,0:T(8,128)} %v_ref.3) | copy-start | bytes 1572868

commit v4 on v3

--- a/solution.py
+++ b/solution.py
@@ -88,27 +88,18 @@
     return 0.25 * ((up + down) + (east(2) + east(-2))) - east(0)
 
 
-def inverse_series(step, sound_ref, series, power):
+def inverse_start(sound, series, power):
     levels = series.shape[0]
-
-    @pl.when(step == 0)
-    def _():
-        r = lax.broadcasted_iota(jnp.int32, (levels, levels), 0)
-        k = lax.broadcasted_iota(jnp.int32, (levels, levels), 1)
-        sound = jnp.broadcast_to(sound_ref[...], (levels, levels))
-        upper = jnp.where((k == r + 1) & (k < levels - 1), -sound, 0.0)
-        above = pltpu.roll(sound, levels - 1, 1)
-        diagonal = jnp.where(k == r, jnp.where(k < levels - 1, 1.0 + sound + above, 1.0), 0.0)
-        eye = jnp.where(k == r, 1.0, 0.0)
-        residual = eye - (diagonal + upper + upper.T) * (1.0 / 3.0)
-        series[...] = (eye + residual) * (1.0 / 3.0)
-        power[...] = exact_dot(residual, residual)
-
-    @pl.when((step > 0) & (step < TERMS))
-    def _():
-        old = series[...]
-        series[...] = old + exact_dot(old, power[...])
-        power[...] = exact_dot(power[...], power[...])
+    r = lax.broadcasted_iota(jnp.int32, (levels, levels), 0)
+    k = lax.broadcasted_iota(jnp.int32, (levels, levels), 1)
+    sound = jnp.broadcast_to(sound, (levels, levels))
+    upper = jnp.where((k == r + 1) & (k < levels - 1), -sound, 0.0)
+    above = pltpu.roll(sound, levels - 1, 1)
+    diagonal = jnp.where(k == r, jnp.where(k < levels - 1, 1.0 + sound + above, 1.0), 0.0)
+    eye = jnp.where(k == r, 1.0, 0.0)
+    residual = eye - (diagonal + upper + upper.T) * (1.0 / 3.0)
+    series[...] = eye * (1.0 / 3.0)
+    power[...] = residual
 
 
 def first_kernel(
@@ -193,12 +184,16 @@
         sat = humidity_ref[i] * jnp.exp(-VAPOUR_SLOPE * theta_ref[i]) - 1.0
         cloud[:, i, :] = GROWTH_RATE * sat.T[lowest : lowest + layers]
     total[...] = jnp.zeros_like(total)
+    inverse_start(sound_ref[...], series, power)
+    assert steps >= TERMS
 
     @pl.loop(0, steps)
     def _(step):
         chunk_move(radius_hbm, radius_all, 0, step).wait()
         chunk_move(mult_hbm, mult_all, 1, step).wait()
-        inverse_series(step, sound_ref, series, power)
+        scale = power[...]
+        series[...] += exact_dot(series[...], scale)
+        power[...] = exact_dot(scale, scale)
         for n in range(CHUNK):
             s = step * CHUNK + n
             live = s < count_ref[...]
@@ -608,31 +603,36 @@
         s_out[r] += f2[r] + p
 
 
-def response_three(columns, sound_ref, inverse_ref, u_ref, v_ref, p3_ref, w3_ref, f2, *refs):
-    s_ref, yp, yw, yd, drift_ref, sums_ref = refs[:6]
-    u_out, v_out, w_out, p_out, profile_out, mu = refs[6:]
+def response_three(sound_ref, inverse_ref, u_ref, v_ref, p3_ref, w3_ref, f2, *refs):
+    s_ref, yp, yw, yd, u_out, v_out, w_out, p_out, mu = refs
     rows, cols, levels = u_ref.shape
     sound = sound_ref[...]
     inside = interior(levels)
     inverse = inverse_ref[...]
     body = slice(PAD, PAD + cols)
     cross(mu, f2, rows, cols)
-    total = sums_ref[...] * (1.0 / columns)
-    profile_out[...] = total[0:1]
-    mean = jnp.broadcast_to(total[1:2], (8, levels))
-    drift = exact_dot(mean, drift_ref[...])
-    drift_p, drift_w = (drift[0:1, 0:levels], drift[0:1, levels:])
     for i in range(rows):
         r = i + 2
         d = yd[r, body, :] - mu[r, body, :] - bend(yp, r, cols)
         p, w = column_step(
             yp[r, body, :] - sound * d, yw[r, body, :], sound, inside, inverse
         )
-        p_out[i] = p3_ref[i] + p + drift_p
-        w_out[i] = w3_ref[i] + w + drift_w
+        p_out[i] = p3_ref[i] + p
+        w_out[i] = w3_ref[i] + w
         u_out[i] = u_ref[i] - 0.5 * (s_ref[r + 1, body, :] - s_ref[r - 1, body, :])
         east = lambda n: s_ref[r, PAD + n : PAD + n + cols, :]
         v_out[i] = v_ref[i] - 0.5 * (east(1) - east(-1))
+
+
+def settle_kernel(columns, p_ref, w_ref, drift_ref, sums_ref, w_out, p_out, profile_out):
+    rows, _, levels = p_ref.shape
+    total = sums_ref[...] * (1.0 / columns)
+    profile_out[...] = total[0:1]
+    mean = jnp.broadcast_to(total[1:2], (8, levels))
+    drift = exact_dot(mean, drift_ref[...])
+    for i in range(rows):
+        p_out[i] = p_ref[i] + drift[0:1, 0:levels]
+        w_out[i] = w_ref[i] + drift[0:1, levels:]
 
 
 def response(kernel, args, outs, scratch, flops):
@@ -746,12 +746,19 @@
         [pltpu.VMEM(wide, jnp.float32)],
         4_000_000_000,
     )
-    u, v, w, p, profile = response(
-        functools.partial(response_three, columns),
-        (sound, weights, eastward, northward, p3, w3, f2, moved, yp, yw, yd, drift, sums),
-        [f32(*theta.shape)] * 4 + [f32(1, levels)],
+    u, v, w, p = response(
+        response_three,
+        (sound, weights, eastward, northward, p3, w3, f2, moved, yp, yw, yd),
+        [f32(*theta.shape)] * 4,
         [pltpu.VMEM(wide, jnp.float32)],
-        2_000_000_000,
+        4_000_000_000,
+    )
+    w, p, profile = response(
+        functools.partial(settle_kernel, columns),
+        (p, w, drift, sums),
+        [f32(*theta.shape)] * 2 + [f32(1, levels)],
+        [],
+        100_000_000,
     )
     return (u, v, w, p, theta_out, humidity_out, radius_out, profile[0])
 

time: 38.2 us -> 38.8 us (1.016)
  Pallas kernels: 13 us -> 13.6 us
    pallas_call x3 -> x4, Pallas kernels: 4.45 us -> 5.22 us  [response(): pl.pallas_call(kernel, in_specs=[VMEM] * len(args), out_specs=[VMEM] * le...]
where the time goes in v4:
time: 38.8 us; the launch traced here: 38.6 us
  starting transfers between devices  15.2 us (39%)
  Pallas kernels  13.6 us (35%)
  waiting for transfers between devices  9.07 us (23%)
  between operations  0.74 us (2%)
    ppermute x3, waiting for transfers between devices, total_sum(): moved = lax.ppermute(value, axis, [(i, i ^ distance) for i in range(count)])  9.05 us
    pallas_call x1, Pallas kernels, first(): pl.pallas_call(functools.partial(first_kernel, ('gx', 'gy')), in_specs=[h...  7.25 us
    ppermute x3, starting transfers between devices, exchange(): b = lax.ppermute(b, axis, far)  6.34 us
    pallas_call x4, Pallas kernels, response(): pl.pallas_call(kernel, in_specs=[VMEM] * len(args), out_specs=[VMEM] * le...  5.22 us
    ppermute x3, starting transfers between devices, total_sum(): moved = lax.ppermute(value, axis, [(i, i ^ distance) for i in range(count)])  5.17 us
    ppermute x3, starting transfers between devices, exchange(): a = lax.ppermute(a, axis, near)  3.69 us
    pallas_call x1, Pallas kernels, third(): pl.pallas_call(third_kernel, in_specs=[VMEM] * 6, out_specs=[VMEM] * 3, o...  1.1 us
  transfers between devices with their start and end apart: 9, of which 3 were waited for; matrix products, arithmetic and copies ran while one was open for 0% of the time, Pallas kernels for 3%

profile of v4, /device:TPU:0, one launch (start us, length us, event | category | flops | bytes accessed | tf_op | source)
XLA Modules:
  0.0 38.6 jit_solution(14127887212706054533)
XLA Ops:
  0.6 0.0 copy-start.3
  0.6 7.3 %condense_and_evolve.1 = (f32[8,128,128]{2,1,0:T(8,128)}, f32[8,128,128]{2,1,0:T(8,128)}, f32[64,8,8,128]{3,2,1,0:T(8,128)}, f32[2,128]{1,0:T(2,128)S(1)}, bf16[...) custom-call(f32[1,128]{1,0:T(1,128)} %bitcast.6, ...), custom_call_target="tpu_custom_call" | custom-call | flops 8000000000 | bytes 12000000 | tf_op jit(solution)/shard_map/condense_and_evolve/pallas_call | solution.py:344
  7.9 3.1 %collective-permute-start.2 = (f32[10,8,128]{2,1,0:T(8,128)S(1)}, f32[10,8,128]{2,1,0:T(8,128)S(1)}, u32[]{:S(2)}, u32[]{:S(2)}) collective-permute-start(f32[10,8,128]{2,1,0:T(8,128)S(1)} %get-tuple-element.56), channel_id=1, source_target_pairs={{0,1},{1,0},{2,3},{3,2},{4,5},{5,4},{6,7},{7,6},{8,9},{9,8},{10,11... | collective-permute-start | bytes 122888 | tf_op jit(solution)/shard_map/ppermute | solution.py:658
  11.0 2.5 %collective-permute-start.3 = (f32[10,8,128]{2,1,0:T(8,128)S(1)}, f32[10,8,128]{2,1,0:T(8,128)S(1)}, u32[]{:S(2)}, u32[]{:S(2)}) collective-permute-start(f32[10,8,128]{2,1,0:T(8,128)S(1)} %get-tuple-element.57), channel_id=1, source_target_pairs={{0,3},{1,2},{2,1},{3,0},{4,7},{5,6},{6,5},{7,4},{8,11},{9,10},{10,... | collective-permute-start | bytes 122888 | tf_op jit(solution)/shard_map/ppermute | solution.py:659
  13.5 0.0 collective-permute-done.2.ya_ref.refs_2_
  13.5 2.9 %collective-permute-start.4 = (f32[2,128]{1,0:T(2,128)S(1)}, f32[2,128]{1,0:T(2,128)S(1)}, u32[]{:S(2)}, u32[]{:S(2)}) collective-permute-start(f32[2,128]{1,0:T(2,128)S(1)} %fusion), channel_id=1, source_target_pairs={{0,2},{1,3},{2,0},{3,1},{4,6},{5,7},{6,4},{7,5},{8,10},{9,11},{10,... | collective-permute-start | bytes 3080 | tf_op jit(solution)/shard_map/ppermute | solution.py:667
  16.4 1.6 %collective-permute-done.4 = f32[2,128]{1,0:T(2,128)S(1)} collective-permute-done((f32[2,128]{1,0:T(2,128)S(1)}, f32[2,128]{1,0:T(2,128)S(1)}, u32[]{:S(2)}, u32[]{:S(2)}) %collective-permute-start.4) | collective-permute-done | bytes 1056 | tf_op jit(solution)/shard_map/ppermute | solution.py:667
  18.0 0.0 collective-permute-done.3.yb_ref.refs_3_
  18.0 0.1 collective-permute-start.5
  18.1 0.5 %collective-permute-start = (f32[6,128,128]{2,1,0:T(8,128)S(1)}, f32[6,128,128]{2,1,0:T(8,128)S(1)}, u32[]{:S(2)}, u32[]{:S(2)}) collective-permute-start(f32[6,128,128]{2,1,0:T(8,128)S(1)} %get-tuple-element.54), channel_id=1, source_target_pairs={{0,4},{4,0},{8,12},{12,8},{16,20},{20,16},{24,28},{28,24},{1,5},{5... | collective-permute-start | bytes 1179656 | tf_op jit(solution)/shard_map/ppermute | solution.py:658
  18.6 2.1 %collective-permute-start.1 = (f32[6,128,128]{2,1,0:T(8,128)S(1)}, f32[6,128,128]{2,1,0:T(8,128)S(1)}, u32[]{:S(2)}, u32[]{:S(2)}) collective-permute-start(f32[6,128,128]{2,1,0:T(8,128)S(1)} %get-tuple-element.55), channel_id=1, source_target_pairs={{0,28},{4,8},{8,4},{12,16},{16,12},{20,24},{24,20},{28,0},{1,29},{... | collective-permute-start | bytes 1179656 | tf_op jit(solution)/shard_map/ppermute | solution.py:659
  20.7 0.0 collective-permute-done.5.refs_4_
  20.7 0.0 collective-permute-start.7
  20.8 1.7 %collective-permute-start.6 = (f32[56,128]{1,0:T(8,128)S(1)}, f32[56,128]{1,0:T(8,128)S(1)}, u32[]{:S(2)}, u32[]{:S(2)}) collective-permute-start(f32[56,128]{1,0:T(8,128)S(1)} %get-tuple-element.61), channel_id=1, source_target_pairs={{0,28},{4,8},{8,4},{12,16},{16,12},{20,24},{24,20},{28,0},{1,29},{... | collective-permute-start | bytes 86024 | tf_op jit(solution)/shard_map/ppermute | solution.py:659
  22.5 7.1 %collective-permute-done.7 = f32[2,128]{1,0:T(2,128)S(1)} collective-permute-done((f32[2,128]{1,0:T(2,128)S(1)}, f32[2,128]{1,0:T(2,128)S(1)}, u32[]{:S(2)}, u32[]{:S(2)}) %collective-permute-start.7) | collective-permute-done | bytes 1056 | tf_op jit(solution)/shard_map/ppermute | solution.py:667
  29.6 2.2 %collective-permute-start.8 = (f32[2,128]{1,0:T(2,128)S(1)}, f32[2,128]{1,0:T(2,128)S(1)}, u32[]{:S(2)}, u32[]{:S(2)}) collective-permute-start(f32[2,128]{1,0:T(2,128)S(1)} %add.18), channel_id=1, source_target_pairs={{0,16},{4,20},{8,24},{12,28},{16,0},{20,4},{24,8},{28,12},{1,17},{... | collective-permute-start | bytes 3080 | tf_op jit(solution)/shard_map/ppermute | solution.py:667
  31.8 0.0 copy-done.3
  31.8 0.0 copy-start
  31.8 0.0 copy-start.1
  31.8 0.0 copy-start.2
  31.8 1.1 %third_step.1 = (f32[8,128,128]{2,1,0:T(8,128)S(1)}, f32[8,128,128]{2,1,0:T(8,128)S(1)}, f32[128,256]{1,0:T(8,128)S(1)}) custom-call(f32[1,128]{1,0:T(1,128)S(1)} %bitcast.7, bf16[256,256]{1,0:T(8,128)(2,1)S(1)} %get-tuple-element.46.inverse_ref, f32[8,128,128]{2,1,0:T(8,128)S(1)} %get-tuple-element.47.heat_ref, ...), custom_call_target="tpu_custom_call" | custom-call | flops 2000000000 | bytes 4000000 | tf_op jit(solution)/shard_map/third_step/pallas_call | solution.py:402
  32.9 0.4 %collective-permute-done.8 = f32[2,128]{1,0:T(2,128)S(1)} collective-permute-done((f32[2,128]{1,0:T(2,128)S(1)}, f32[2,128]{1,0:T(2,128)S(1)}, u32[]{:S(2)}, u32[]{:S(2)}) %collective-permute-start.8) | collective-permute-done | bytes 1056 | tf_op jit(solution)/shard_map/ppermute | solution.py:667
  33.4 0.0 collective-permute-done.6.refs_5_
  33.4 0.0 collective-permute-done.refs_0_
  33.4 0.0 collective-permute-done.1.refs_1_
  33.4 0.0 copy-done
  33.4 0.0 copy-done.1
  33.4 0.0 copy-done.2
  33.4 1.0 %shard_map.161 = (f32[12,144,128]{2,1,0:T(8,128)S(1)}, f32[12,144,128]{2,1,0:T(8,128)S(1)}, f32[12,144,128]{2,1,0:T(8,128)S(1)}, f32[12,144,128]{2,1,0:T(8,128)S...) custom-call(f32[1,128]{1,0:T(1,128)S(1)} %bitcast.8, ...), custom_call_target="tpu_custom_call" | custom-call | flops 4000000000 | bytes 6000000 | tf_op jit(solution)/shard_map/pallas_call | solution.py:639
  34.4 1.3 %shard_map.162 = (f32[12,144,128]{2,1,0:T(8,128)S(1)}, f32[12,144,128]{2,1,0:T(8,128)S(1)}, f32[12,144,128]{2,1,0:T(8,128)S(1)}, f32[12,144,128]{2,1,0:T(8,128)S(1)}) custom-call(f32[1,128]{1,0:T(1,128)S(1)} %bitcast.9, bf16[256,256]{1,0:T(8,128)(2,1)S(1)} %get-tuple-element.46.inverse_ref, f32[12,144,128]{2,1,0:T(8,128)S(1)} %get-tuple-element.63.f0, ...), custom_call_target="tpu_custom_call" | custom-call | flops 4000000000 | bytes 6000000 | tf_op jit(solution)/shard_map/pallas_call | solution.py:639
  35.7 1.7 %shard_map.163 = (f32[8,128,128]{2,1,0:T(8,128)}, f32[8,128,128]{2,1,0:T(8,128)}, f32[8,128,128]{2,1,0:T(8,128)S(1)}, f32[8,128,128]{2,1,0:T(8,128)S(1)}) custom-call(f32[1,128]{1,0:T(1,128)S(1)} %bitcast.10, bf16[256,256]{1,0:T(8,128)(2,1)S(1)} %get-tuple-element.46.inverse_ref, f32[8,128,128]{2,1,0:T(8,128)S(1)} %copy-done.1, ...), custom_call_target="tpu_custom_call" | custom-call | flops 4000000000 | bytes 6000000 | tf_op jit(solution)/shard_map/pallas_call | solution.py:639
  37.5 1.2 %shard_map.164 = (f32[8,128,128]{2,1,0:T(8,128)}, f32[8,128,128]{2,1,0:T(8,128)}, f32[1,128]{1,0:T(1,128)}) custom-call(f32[8,128,128]{2,1,0:T(8,128)S(1)} %get-tuple-element.75.p_ref, f32[8,128,128]{2,1,0:T(8,128)S(1)} %get-tuple-element.76.w_ref, f32[128,256]{1,0:T(8,128)S(1)} %get-tuple-element.77.drift_ref, f32[2,128]{1,0:T(2,128)S(1)} %add.19.sums_ref), custom_call_target="tpu_custom_call" | custom-call | flops 100000000 | bytes 6000000 | tf_op jit(solution)/shard_map/pallas_call | solution.py:639
  (6 shorter events, 0.0 us)
Async XLA Ops:
  0.6 31.2 %copy-start.3 = (f32[128]{0:T(128)S(1)}, f32[128]{0:T(128)}, u32[]{:S(2)}) copy-start(f32[128]{0:T(128)} %param.16) | copy-start | bytes 1540
  7.9 5.6 %collective-permute-start.2 = (f32[10,8,128]{2,1,0:T(8,128)S(1)}, f32[10,8,128]{2,1,0:T(8,128)S(1)}, u32[]{:S(2)}, u32[]{:S(2)}) collective-permute-start(f32[10,8,128]{2,1,0:T(8,128)S(1)} %get-tuple-element.56), channel_id=1, source_target_pairs={{0,1},{1,0},{2,3},{3,2},{4,5},{5,4},{6,7},{7,6},{8,9},{9,8},{10,11... | collective-permute-start | bytes 122888 | tf_op jit(solution)/shard_map/ppermute | solution.py:658
  11.0 7.0 %collective-permute-start.3 = (f32[10,8,128]{2,1,0:T(8,128)S(1)}, f32[10,8,128]{2,1,0:T(8,128)S(1)}, u32[]{:S(2)}, u32[]{:S(2)}) collective-permute-start(f32[10,8,128]{2,1,0:T(8,128)S(1)} %get-tuple-element.57), channel_id=1, source_target_pairs={{0,3},{1,2},{2,1},{3,0},{4,7},{5,6},{6,5},{7,4},{8,11},{9,10},{10,... | collective-permute-start | bytes 122888 | tf_op jit(solution)/shard_map/ppermute | solution.py:659
  13.5 4.5 %collective-permute-start.4 = (f32[2,128]{1,0:T(2,128)S(1)}, f32[2,128]{1,0:T(2,128)S(1)}, u32[]{:S(2)}, u32[]{:S(2)}) collective-permute-start(f32[2,128]{1,0:T(2,128)S(1)} %fusion), channel_id=1, source_target_pairs={{0,2},{1,3},{2,0},{3,1},{4,6},{5,7},{6,4},{7,5},{8,10},{9,11},{10,... | collective-permute-start | bytes 3080 | tf_op jit(solution)/shard_map/ppermute | solution.py:667
  18.0 2.7 %collective-permute-start.5 = (f32[56,128]{1,0:T(8,128)S(1)}, f32[56,128]{1,0:T(8,128)S(1)}, u32[]{:S(2)}, u32[]{:S(2)}) collective-permute-start(f32[56,128]{1,0:T(8,128)S(1)} %get-tuple-element.60), channel_id=1, source_target_pairs={{0,4},{4,0},{8,12},{12,8},{16,20},{20,16},{24,28},{28,24},{1,5},{5... | collective-permute-start | bytes 86024 | tf_op jit(solution)/shard_map/ppermute | solution.py:658
  18.1 15.3 %collective-permute-start = (f32[6,128,128]{2,1,0:T(8,128)S(1)}, f32[6,128,128]{2,1,0:T(8,128)S(1)}, u32[]{:S(2)}, u32[]{:S(2)}) collective-permute-start(f32[6,128,128]{2,1,0:T(8,128)S(1)} %get-tuple-element.54), channel_id=1, source_target_pairs={{0,4},{4,0},{8,12},{12,8},{16,20},{20,16},{24,28},{28,24},{1,5},{5... | collective-permute-start | bytes 1179656 | tf_op jit(solution)/shard_map/ppermute | solution.py:658
  18.6 14.8 %collective-permute-start.1 = (f32[6,128,128]{2,1,0:T(8,128)S(1)}, f32[6,128,128]{2,1,0:T(8,128)S(1)}, u32[]{:S(2)}, u32[]{:S(2)}) collective-permute-start(f32[6,128,128]{2,1,0:T(8,128)S(1)} %get-tuple-element.55), channel_id=1, source_target_pairs={{0,28},{4,8},{8,4},{12,16},{16,12},{20,24},{24,20},{28,0},{1,29},{... | collective-permute-start | bytes 1179656 | tf_op jit(solution)/shard_map/ppermute | solution.py:659
  20.7 8.9 %collective-permute-start.7 = (f32[2,128]{1,0:T(2,128)S(1)}, f32[2,128]{1,0:T(2,128)S(1)}, u32[]{:S(2)}, u32[]{:S(2)}) collective-permute-start(f32[2,128]{1,0:T(2,128)S(1)} %slice_add_fusion), channel_id=1, source_target_pairs={{0,8},{4,12},{8,0},{12,4},{16,24},{20,28},{24,16},{28,20},{1,9},{5... | collective-permute-start | bytes 3080 | tf_op jit(solution)/shard_map/ppermute | solution.py:667
  20.8 12.6 %collective-permute-start.6 = (f32[56,128]{1,0:T(8,128)S(1)}, f32[56,128]{1,0:T(8,128)S(1)}, u32[]{:S(2)}, u32[]{:S(2)}) collective-permute-start(f32[56,128]{1,0:T(8,128)S(1)} %get-tuple-element.61), channel_id=1, source_target_pairs={{0,28},{4,8},{8,4},{12,16},{16,12},{20,24},{24,20},{28,0},{1,29},{... | collective-permute-start | bytes 86024 | tf_op jit(solution)/shard_map/ppermute | solution.py:659
  29.6 3.8 %collective-permute-start.8 = (f32[2,128]{1,0:T(2,128)S(1)}, f32[2,128]{1,0:T(2,128)S(1)}, u32[]{:S(2)}, u32[]{:S(2)}) collective-permute-start(f32[2,128]{1,0:T(2,128)S(1)} %add.18), channel_id=1, source_target_pairs={{0,16},{4,20},{8,24},{12,28},{16,0},{20,4},{24,8},{28,12},{1,17},{... | collective-permute-start | bytes 3080 | tf_op jit(solution)/shard_map/ppermute | solution.py:667
  31.8 1.6 %copy-start = (f32[8,128,128]{2,1,0:T(8,128)S(1)}, f32[8,128,128]{2,1,0:T(8,128)}, u32[]{:S(2)}) copy-start(f32[8,128,128]{2,1,0:T(8,128)} %p0_ref.1) | copy-start | bytes 1572868
  31.8 1.6 %copy-start.1 = (f32[8,128,128]{2,1,0:T(8,128)S(1)}, f32[8,128,128]{2,1,0:T(8,128)}, u32[]{:S(2)}) copy-start(f32[8,128,128]{2,1,0:T(8,128)} %u_ref.3) | copy-start | bytes 1572868
  31.8 1.6 %copy-start.2 = (f32[8,128,128]{2,1,0:T(8,128)S(1)}, f32[8,128,128]{2,1,0:T(8,128)}, u32[]{:S(2)}) copy-start(f32[8,128,128]{2,1,0:T(8,128)} %v_ref.3) | copy-start | bytes 1572868

commit v5 on v4

--- a/solution.py
+++ b/solution.py
@@ -173,13 +173,15 @@
 
     for move in moves[:4]:
         move.start()
-    for step in range(steps):
+    chunk_move(radius_hbm, radius_all, 0, 0).start()
+    chunk_move(mult_hbm, mult_all, 1, 0).start()
+    for move in moves[:4]:
+        move.wait()
+    for step in range(1, steps):
         chunk_move(radius_hbm, radius_all, 0, step).start()
         chunk_move(mult_hbm, mult_all, 1, step).start()
     for move in moves[4:8]:
         move.start()
-    for move in moves[:4]:
-        move.wait()
     for i in range(rows):
         sat = humidity_ref[i] * jnp.exp(-VAPOUR_SLOPE * theta_ref[i]) - 1.0
         cloud[:, i, :] = GROWTH_RATE * sat.T[lowest : lowest + layers]
@@ -604,12 +606,23 @@
 
 
 def response_three(sound_ref, inverse_ref, u_ref, v_ref, p3_ref, w3_ref, f2, *refs):
-    s_ref, yp, yw, yd, u_out, v_out, w_out, p_out, mu = refs
+    s_ref, yp, yw, yd, u_final, v_final, w_out, p_out, mu, u_out, v_out, sems = refs
+    moves = [
+        pltpu.make_async_copy(u_out, u_final, sems.at[0]),
+        pltpu.make_async_copy(v_out, v_final, sems.at[1]),
+    ]
     rows, cols, levels = u_ref.shape
     sound = sound_ref[...]
     inside = interior(levels)
     inverse = inverse_ref[...]
     body = slice(PAD, PAD + cols)
+    for i in range(rows):
+        r = i + 2
+        u_out[i] = u_ref[i] - 0.5 * (s_ref[r + 1, body, :] - s_ref[r - 1, body, :])
+        east = lambda n: s_ref[r, PAD + n : PAD + n + cols, :]
+        v_out[i] = v_ref[i] - 0.5 * (east(1) - east(-1))
+    for move in moves:
+        move.start()
     cross(mu, f2, rows, cols)
     for i in range(rows):
         r = i + 2
@@ -619,9 +632,8 @@
         )
         p_out[i] = p3_ref[i] + p
         w_out[i] = w3_ref[i] + w
-        u_out[i] = u_ref[i] - 0.5 * (s_ref[r + 1, body, :] - s_ref[r - 1, body, :])
-        east = lambda n: s_ref[r, PAD + n : PAD + n + cols, :]
-        v_out[i] = v_ref[i] - 0.5 * (east(1) - east(-1))
+    for move in moves:
+        move.wait()
 
 
 def settle_kernel(columns, p_ref, w_ref, drift_ref, sums_ref, w_out, p_out, profile_out):
@@ -635,11 +647,11 @@
         w_out[i] = w_ref[i] + drift[0:1, levels:]
 
 
-def response(kernel, args, outs, scratch, flops):
+def response(kernel, args, outs, scratch, flops, direct=0):
     return pl.pallas_call(
         kernel,
         in_specs=[VMEM] * len(args),
-        out_specs=[VMEM] * len(outs),
+        out_specs=[pl.BlockSpec(memory_space=pltpu.HBM)] * direct + [VMEM] * (len(outs) - direct),
         out_shape=outs,
         scratch_shapes=scratch,
         compiler_params=pltpu.CompilerParams(vmem_limit_bytes=GRANT),
@@ -750,8 +762,11 @@
         response_three,
         (sound, weights, eastward, northward, p3, w3, f2, moved, yp, yw, yd),
         [f32(*theta.shape)] * 4,
-        [pltpu.VMEM(wide, jnp.float32)],
+        [pltpu.VMEM(wide, jnp.float32)]
+        + [pltpu.VMEM(theta.shape, jnp.float32)] * 2
+        + [pltpu.SemaphoreType.DMA((2,))],
         4_000_000_000,
+        direct=2,
     )
     w, p, profile = response(
         functools.partial(settle_kernel, columns),

time: 38.8 us -> 38 us (0.979)
  Pallas kernels: 13.6 us -> 12.8 us
    pallas_call x1, Pallas kernels: 7.25 us -> 6.47 us  [first(): pl.pallas_call(functools.partial(first_kernel, ('gx', 'gy')), in_specs=[h...]
where the time goes in v5:
time: 38 us; the launch traced here: 37.9 us
  starting transfers between devices  15.2 us (40%)
  Pallas kernels  12.8 us (34%)
  waiting for transfers between devices  9.08 us (24%)
  between operations  0.74 us (2%)
    ppermute x3, waiting for transfers between devices, total_sum(): moved = lax.ppermute(value, axis, [(i, i ^ distance) for i in range(count)])  9.06 us
    pallas_call x1, Pallas kernels, first(): pl.pallas_call(functools.partial(first_kernel, ('gx', 'gy')), in_specs=[h...  6.47 us
    ppermute x3, starting transfers between devices, exchange(): b = lax.ppermute(b, axis, far)  6.34 us
    pallas_call x4, Pallas kernels, response(): pl.pallas_call(kernel, in_specs=[VMEM] * len(args), out_specs=[pl.BlockSp...  5.24 us
    ppermute x3, starting transfers between devices, total_sum(): moved = lax.ppermute(value, axis, [(i, i ^ distance) for i in range(count)])  5.17 us
    ppermute x3, starting transfers between devices, exchange(): a = lax.ppermute(a, axis, near)  3.69 us
    pallas_call x1, Pallas kernels, third(): pl.pallas_call(third_kernel, in_specs=[VMEM] * 6, out_specs=[VMEM] * 3, o...  1.1 us
  transfers between devices with their start and end apart: 9, of which 3 were waited for; matrix products, arithmetic and copies ran while one was open for 0% of the time, Pallas kernels for 3%

profile of v5, /device:TPU:0, one launch (start us, length us, event | category | flops | bytes accessed | tf_op | source)
XLA Modules:
  0.0 37.9 jit_solution(1262183921949079423)
XLA Ops:
  0.6 0.0 copy-start.3
  0.6 6.5 %condense_and_evolve.1 = (f32[8,128,128]{2,1,0:T(8,128)}, f32[8,128,128]{2,1,0:T(8,128)}, f32[64,8,8,128]{3,2,1,0:T(8,128)}, f32[2,128]{1,0:T(2,128)S(1)}, bf16[...) custom-call(f32[1,128]{1,0:T(1,128)} %bitcast.6, ...), custom_call_target="tpu_custom_call" | custom-call | flops 8000000000 | bytes 12000000 | tf_op jit(solution)/shard_map/condense_and_evolve/pallas_call | solution.py:346
  7.1 3.1 %collective-permute-start.2 = (f32[10,8,128]{2,1,0:T(8,128)S(1)}, f32[10,8,128]{2,1,0:T(8,128)S(1)}, u32[]{:S(2)}, u32[]{:S(2)}) collective-permute-start(f32[10,8,128]{2,1,0:T(8,128)S(1)} %get-tuple-element.56), channel_id=1, source_target_pairs={{0,1},{1,0},{2,3},{3,2},{4,5},{5,4},{6,7},{7,6},{8,9},{9,8},{10,11... | collective-permute-start | bytes 122888 | tf_op jit(solution)/shard_map/ppermute | solution.py:670
  10.2 2.5 %collective-permute-start.3 = (f32[10,8,128]{2,1,0:T(8,128)S(1)}, f32[10,8,128]{2,1,0:T(8,128)S(1)}, u32[]{:S(2)}, u32[]{:S(2)}) collective-permute-start(f32[10,8,128]{2,1,0:T(8,128)S(1)} %get-tuple-element.57), channel_id=1, source_target_pairs={{0,3},{1,2},{2,1},{3,0},{4,7},{5,6},{6,5},{7,4},{8,11},{9,10},{10,... | collective-permute-start | bytes 122888 | tf_op jit(solution)/shard_map/ppermute | solution.py:671
  12.7 0.0 collective-permute-done.2.ya_ref.refs_2_
  12.7 2.9 %collective-permute-start.4 = (f32[2,128]{1,0:T(2,128)S(1)}, f32[2,128]{1,0:T(2,128)S(1)}, u32[]{:S(2)}, u32[]{:S(2)}) collective-permute-start(f32[2,128]{1,0:T(2,128)S(1)} %fusion), channel_id=1, source_target_pairs={{0,2},{1,3},{2,0},{3,1},{4,6},{5,7},{6,4},{7,5},{8,10},{9,11},{10,... | collective-permute-start | bytes 3080 | tf_op jit(solution)/shard_map/ppermute | solution.py:679
  15.6 1.6 %collective-permute-done.4 = f32[2,128]{1,0:T(2,128)S(1)} collective-permute-done((f32[2,128]{1,0:T(2,128)S(1)}, f32[2,128]{1,0:T(2,128)S(1)}, u32[]{:S(2)}, u32[]{:S(2)}) %collective-permute-start.4) | collective-permute-done | bytes 1056 | tf_op jit(solution)/shard_map/ppermute | solution.py:679
  17.2 0.0 collective-permute-done.3.yb_ref.refs_3_
  17.2 0.1 collective-permute-start.5
  17.3 0.5 %collective-permute-start = (f32[6,128,128]{2,1,0:T(8,128)S(1)}, f32[6,128,128]{2,1,0:T(8,128)S(1)}, u32[]{:S(2)}, u32[]{:S(2)}) collective-permute-start(f32[6,128,128]{2,1,0:T(8,128)S(1)} %get-tuple-element.54), channel_id=1, source_target_pairs={{0,4},{4,0},{8,12},{12,8},{16,20},{20,16},{24,28},{28,24},{1,5},{5... | collective-permute-start | bytes 1179656 | tf_op jit(solution)/shard_map/ppermute | solution.py:670
  17.8 2.1 %collective-permute-start.1 = (f32[6,128,128]{2,1,0:T(8,128)S(1)}, f32[6,128,128]{2,1,0:T(8,128)S(1)}, u32[]{:S(2)}, u32[]{:S(2)}) collective-permute-start(f32[6,128,128]{2,1,0:T(8,128)S(1)} %get-tuple-element.55), channel_id=1, source_target_pairs={{0,28},{4,8},{8,4},{12,16},{16,12},{20,24},{24,20},{28,0},{1,29},{... | collective-permute-start | bytes 1179656 | tf_op jit(solution)/shard_map/ppermute | solution.py:671
  19.9 0.0 collective-permute-done.5.refs_4_
  19.9 0.0 collective-permute-start.7
  20.0 1.7 %collective-permute-start.6 = (f32[56,128]{1,0:T(8,128)S(1)}, f32[56,128]{1,0:T(8,128)S(1)}, u32[]{:S(2)}, u32[]{:S(2)}) collective-permute-start(f32[56,128]{1,0:T(8,128)S(1)} %get-tuple-element.61), channel_id=1, source_target_pairs={{0,28},{4,8},{8,4},{12,16},{16,12},{20,24},{24,20},{28,0},{1,29},{... | collective-permute-start | bytes 86024 | tf_op jit(solution)/shard_map/ppermute | solution.py:671
  21.7 7.1 %collective-permute-done.7 = f32[2,128]{1,0:T(2,128)S(1)} collective-permute-done((f32[2,128]{1,0:T(2,128)S(1)}, f32[2,128]{1,0:T(2,128)S(1)}, u32[]{:S(2)}, u32[]{:S(2)}) %collective-permute-start.7) | collective-permute-done | bytes 1056 | tf_op jit(solution)/shard_map/ppermute | solution.py:679
  28.8 2.2 %collective-permute-start.8 = (f32[2,128]{1,0:T(2,128)S(1)}, f32[2,128]{1,0:T(2,128)S(1)}, u32[]{:S(2)}, u32[]{:S(2)}) collective-permute-start(f32[2,128]{1,0:T(2,128)S(1)} %add.18), channel_id=1, source_target_pairs={{0,16},{4,20},{8,24},{12,28},{16,0},{20,4},{24,8},{28,12},{1,17},{... | collective-permute-start | bytes 3080 | tf_op jit(solution)/shard_map/ppermute | solution.py:679
  31.0 0.0 copy-done.3
  31.0 0.0 copy-start
  31.0 0.0 copy-start.1
  31.0 0.0 copy-start.2
  31.0 1.1 %third_step.1 = (f32[8,128,128]{2,1,0:T(8,128)S(1)}, f32[8,128,128]{2,1,0:T(8,128)S(1)}, f32[128,256]{1,0:T(8,128)S(1)}) custom-call(f32[1,128]{1,0:T(1,128)S(1)} %bitcast.7, bf16[256,256]{1,0:T(8,128)(2,1)S(1)} %get-tuple-element.46.inverse_ref, f32[8,128,128]{2,1,0:T(8,128)S(1)} %get-tuple-element.47.heat_ref, ...), custom_call_target="tpu_custom_call" | custom-call | flops 2000000000 | bytes 4000000 | tf_op jit(solution)/shard_map/third_step/pallas_call | solution.py:404
  32.1 0.4 %collective-permute-done.8 = f32[2,128]{1,0:T(2,128)S(1)} collective-permute-done((f32[2,128]{1,0:T(2,128)S(1)}, f32[2,128]{1,0:T(2,128)S(1)}, u32[]{:S(2)}, u32[]{:S(2)}) %collective-permute-start.8) | collective-permute-done | bytes 1056 | tf_op jit(solution)/shard_map/ppermute | solution.py:679
  32.6 0.0 collective-permute-done.6.refs_5_
  32.6 0.0 collective-permute-done.refs_0_
  32.6 0.0 collective-permute-done.1.refs_1_
  32.6 0.0 copy-done
  32.6 0.0 copy-done.1
  32.6 0.0 copy-done.2
  32.6 1.0 %shard_map.161 = (f32[12,144,128]{2,1,0:T(8,128)S(1)}, f32[12,144,128]{2,1,0:T(8,128)S(1)}, f32[12,144,128]{2,1,0:T(8,128)S(1)}, f32[12,144,128]{2,1,0:T(8,128)S...) custom-call(f32[1,128]{1,0:T(1,128)S(1)} %bitcast.8, ...), custom_call_target="tpu_custom_call" | custom-call | flops 4000000000 | bytes 6000000 | tf_op jit(solution)/shard_map/pallas_call | solution.py:651
  33.6 1.3 %shard_map.162 = (f32[12,144,128]{2,1,0:T(8,128)S(1)}, f32[12,144,128]{2,1,0:T(8,128)S(1)}, f32[12,144,128]{2,1,0:T(8,128)S(1)}, f32[12,144,128]{2,1,0:T(8,128)S(1)}) custom-call(f32[1,128]{1,0:T(1,128)S(1)} %bitcast.9, bf16[256,256]{1,0:T(8,128)(2,1)S(1)} %get-tuple-element.46.inverse_ref, f32[12,144,128]{2,1,0:T(8,128)S(1)} %get-tuple-element.63.f0, ...), custom_call_target="tpu_custom_call" | custom-call | flops 4000000000 | bytes 6000000 | tf_op jit(solution)/shard_map/pallas_call | solution.py:651
  35.0 1.7 %shard_map.163 = (f32[8,128,128]{2,1,0:T(8,128)}, f32[8,128,128]{2,1,0:T(8,128)}, f32[8,128,128]{2,1,0:T(8,128)S(1)}, f32[8,128,128]{2,1,0:T(8,128)S(1)}) custom-call(f32[1,128]{1,0:T(1,128)S(1)} %bitcast.10, bf16[256,256]{1,0:T(8,128)(2,1)S(1)} %get-tuple-element.46.inverse_ref, f32[8,128,128]{2,1,0:T(8,128)S(1)} %copy-done.1, ...), custom_call_target="tpu_custom_call" | custom-call | flops 4000000000 | bytes 6000000 | tf_op jit(solution)/shard_map/pallas_call | solution.py:651
  36.7 1.2 %shard_map.164 = (f32[8,128,128]{2,1,0:T(8,128)}, f32[8,128,128]{2,1,0:T(8,128)}, f32[1,128]{1,0:T(1,128)}) custom-call(f32[8,128,128]{2,1,0:T(8,128)S(1)} %get-tuple-element.75.p_ref, f32[8,128,128]{2,1,0:T(8,128)S(1)} %get-tuple-element.76.w_ref, f32[128,256]{1,0:T(8,128)S(1)} %get-tuple-element.77.drift_ref, f32[2,128]{1,0:T(2,128)S(1)} %add.19.sums_ref), custom_call_target="tpu_custom_call" | custom-call | flops 100000000 | bytes 6000000 | tf_op jit(solution)/shard_map/pallas_call | solution.py:651
  (6 shorter events, 0.0 us)
Async XLA Ops:
  0.6 30.4 %copy-start.3 = (f32[128]{0:T(128)S(1)}, f32[128]{0:T(128)}, u32[]{:S(2)}) copy-start(f32[128]{0:T(128)} %param.16) | copy-start | bytes 1540
  7.1 5.6 %collective-permute-start.2 = (f32[10,8,128]{2,1,0:T(8,128)S(1)}, f32[10,8,128]{2,1,0:T(8,128)S(1)}, u32[]{:S(2)}, u32[]{:S(2)}) collective-permute-start(f32[10,8,128]{2,1,0:T(8,128)S(1)} %get-tuple-element.56), channel_id=1, source_target_pairs={{0,1},{1,0},{2,3},{3,2},{4,5},{5,4},{6,7},{7,6},{8,9},{9,8},{10,11... | collective-permute-start | bytes 122888 | tf_op jit(solution)/shard_map/ppermute | solution.py:670
  10.2 7.0 %collective-permute-start.3 = (f32[10,8,128]{2,1,0:T(8,128)S(1)}, f32[10,8,128]{2,1,0:T(8,128)S(1)}, u32[]{:S(2)}, u32[]{:S(2)}) collective-permute-start(f32[10,8,128]{2,1,0:T(8,128)S(1)} %get-tuple-element.57), channel_id=1, source_target_pairs={{0,3},{1,2},{2,1},{3,0},{4,7},{5,6},{6,5},{7,4},{8,11},{9,10},{10,... | collective-permute-start | bytes 122888 | tf_op jit(solution)/shard_map/ppermute | solution.py:671
  12.7 4.5 %collective-permute-start.4 = (f32[2,128]{1,0:T(2,128)S(1)}, f32[2,128]{1,0:T(2,128)S(1)}, u32[]{:S(2)}, u32[]{:S(2)}) collective-permute-start(f32[2,128]{1,0:T(2,128)S(1)} %fusion), channel_id=1, source_target_pairs={{0,2},{1,3},{2,0},{3,1},{4,6},{5,7},{6,4},{7,5},{8,10},{9,11},{10,... | collective-permute-start | bytes 3080 | tf_op jit(solution)/shard_map/ppermute | solution.py:679
  17.2 2.7 %collective-permute-start.5 = (f32[56,128]{1,0:T(8,128)S(1)}, f32[56,128]{1,0:T(8,128)S(1)}, u32[]{:S(2)}, u32[]{:S(2)}) collective-permute-start(f32[56,128]{1,0:T(8,128)S(1)} %get-tuple-element.60), channel_id=1, source_target_pairs={{0,4},{4,0},{8,12},{12,8},{16,20},{20,16},{24,28},{28,24},{1,5},{5... | collective-permute-start | bytes 86024 | tf_op jit(solution)/shard_map/ppermute | solution.py:670
  17.3 15.3 %collective-permute-start = (f32[6,128,128]{2,1,0:T(8,128)S(1)}, f32[6,128,128]{2,1,0:T(8,128)S(1)}, u32[]{:S(2)}, u32[]{:S(2)}) collective-permute-start(f32[6,128,128]{2,1,0:T(8,128)S(1)} %get-tuple-element.54), channel_id=1, source_target_pairs={{0,4},{4,0},{8,12},{12,8},{16,20},{20,16},{24,28},{28,24},{1,5},{5... | collective-permute-start | bytes 1179656 | tf_op jit(solution)/shard_map/ppermute | solution.py:670
  17.8 14.8 %collective-permute-start.1 = (f32[6,128,128]{2,1,0:T(8,128)S(1)}, f32[6,128,128]{2,1,0:T(8,128)S(1)}, u32[]{:S(2)}, u32[]{:S(2)}) collective-permute-start(f32[6,128,128]{2,1,0:T(8,128)S(1)} %get-tuple-element.55), channel_id=1, source_target_pairs={{0,28},{4,8},{8,4},{12,16},{16,12},{20,24},{24,20},{28,0},{1,29},{... | collective-permute-start | bytes 1179656 | tf_op jit(solution)/shard_map/ppermute | solution.py:671
  19.9 8.9 %collective-permute-start.7 = (f32[2,128]{1,0:T(2,128)S(1)}, f32[2,128]{1,0:T(2,128)S(1)}, u32[]{:S(2)}, u32[]{:S(2)}) collective-permute-start(f32[2,128]{1,0:T(2,128)S(1)} %slice_add_fusion), channel_id=1, source_target_pairs={{0,8},{4,12},{8,0},{12,4},{16,24},{20,28},{24,16},{28,20},{1,9},{5... | collective-permute-start | bytes 3080 | tf_op jit(solution)/shard_map/ppermute | solution.py:679
  20.0 12.6 %collective-permute-start.6 = (f32[56,128]{1,0:T(8,128)S(1)}, f32[56,128]{1,0:T(8,128)S(1)}, u32[]{:S(2)}, u32[]{:S(2)}) collective-permute-start(f32[56,128]{1,0:T(8,128)S(1)} %get-tuple-element.61), channel_id=1, source_target_pairs={{0,28},{4,8},{8,4},{12,16},{16,12},{20,24},{24,20},{28,0},{1,29},{... | collective-permute-start | bytes 86024 | tf_op jit(solution)/shard_map/ppermute | solution.py:671
  28.8 3.8 %collective-permute-start.8 = (f32[2,128]{1,0:T(2,128)S(1)}, f32[2,128]{1,0:T(2,128)S(1)}, u32[]{:S(2)}, u32[]{:S(2)}) collective-permute-start(f32[2,128]{1,0:T(2,128)S(1)} %add.18), channel_id=1, source_target_pairs={{0,16},{4,20},{8,24},{12,28},{16,0},{20,4},{24,8},{28,12},{1,17},{... | collective-permute-start | bytes 3080 | tf_op jit(solution)/shard_map/ppermute | solution.py:679
  31.0 1.6 %copy-start = (f32[8,128,128]{2,1,0:T(8,128)S(1)}, f32[8,128,128]{2,1,0:T(8,128)}, u32[]{:S(2)}) copy-start(f32[8,128,128]{2,1,0:T(8,128)} %p0_ref.1) | copy-start | bytes 1572868
  31.0 1.6 %copy-start.1 = (f32[8,128,128]{2,1,0:T(8,128)S(1)}, f32[8,128,128]{2,1,0:T(8,128)}, u32[]{:S(2)}) copy-start(f32[8,128,128]{2,1,0:T(8,128)} %u_ref.3) | copy-start | bytes 1572868
  31.0 1.6 %copy-start.2 = (f32[8,128,128]{2,1,0:T(8,128)S(1)}, f32[8,128,128]{2,1,0:T(8,128)}, u32[]{:S(2)}) copy-start(f32[8,128,128]{2,1,0:T(8,128)} %v_ref.3) | copy-start | bytes 1572868
